TPU v7x, 32 devices: a whole 2x2x4 slice. The times are simulated.
32 devices in a mesh: slab: 8 (over z, x), cross: 4 (over y, core).
Axes of the slice: x: 2, y: 2, z: 4, core: 2. Of those that a mesh axis runs over, the one named last changes fastest.
Arguments:
- gas_state: float32 [16, 64, 8192], P(None, 'slab', 'cross'), may hold values from -4 to 4, as said below
- parcel_record: float32 [5, 131072], P(None, ('slab', 'cross')), may hold values from -4 to 4, as said below
- condensed_shares: float32 [12, 131072], P(None, ('slab', 'cross')), may hold values from 0.02 to 0.2
- surface_steam_factor: float32 [12], replicated, may hold values from 0.2 to 2
- fine_cell: int32 [131072], P(('slab', 'cross')), may hold values from 0 to 20479, as said below
- block_counts: int32 [1024], P(('slab', 'cross')), may hold values from 16 to 128, as said below
Outputs:
- parcel_next: float32 [5, 131072], P(None, ('slab', 'cross'))
- fine_source: float32 [16, 64, 8192], P(None, 'slab', 'cross')
- correction: float32 [64, 4096], replicated
Inputs may be any that keep to these rules, and one draw needn't show every extreme that they name: fine_cell is plane * 2048 + k, with plane 0 and 9 the neighbouring slabs' last and first planes; it never points outside the gas mesh, and is non-decreasing over each device's 4096 slots. The live parcels of each aligned block of 128 slots are its first block_counts slots; the last block of each device's 4096 slots is full. `gas_state`: rows 0 to 2 velocity, row 3 temperature from 1 to 2, rows 4 on vapour fractions from 0 to 0.1. `parcel_record`: rows 0 to 2 velocity, row 3 temperature from 0.6 to 0.9, row 4 mass from 0.5 to 3.
All inputs are finite; a program needn't handle non-finite values.
Results may differ from a plain program's by a relative error of at most 0.00002.
Values sent between devices are 32-bit elements; how exact they have to be, the bound alone decides.
No kernel may reach another device: no remote copies, remote signals or barrier semaphores. Data moves between devices by JAX's collectives and lax.ppermute only.
A program may use at most 64 MiB of HBM per device.

v0:
```python
import jax
import jax.numpy as jnp
from jax import lax
from jax.sharding import PartitionSpec as P

BLOCK = 128
COARSE = 64
SWEEPS = 4


drag_rate = 0.5
evap_rate = 0.08
warming_speed = 0.3
latent_boiling_energy = 0.5
vapour_heat = 1.5
volume_inverse = 4.0


def with_halo(shard, sides, width):
    for axis, dim in sides:
        devices, length = (lax.axis_size(axis), shard.shape[dim])
        up = [(i, (i + 1) % devices) for i in range(devices - 1)]
        down = [(j, i) for i, j in up]
        last = lax.slice_in_dim(shard, length - width, length, axis=dim)
        leading = lax.slice_in_dim(shard, 0, width, axis=dim)
        before = lax.ppermute(last, axis, up)
        after = lax.ppermute(leading, axis, down)
        shard = jnp.concatenate([before, shard, after], axis=dim)
    return shard


def shifted(shard, axis, by):
    devices = lax.axis_size(axis)
    pairs = [(i, i + by) for i in range(devices) if 0 <= i + by < devices]
    return lax.ppermute(shard, axis, pairs)


def partner(shard, axis, bit):
    return lax.ppermute(shard, axis, [(i, i ^ 1 << bit) for i in range(lax.axis_size(axis))])


def advance(
    ambient_layer_fields, parcel_record, condensed_shares, surface_steam_factor, alive_mask
):
    gas_velocity = ambient_layer_fields[0:3]
    ambient_thermal_level = ambient_layer_fields[3]
    gas_vapour = ambient_layer_fields[4:]
    parcel_velocity = parcel_record[0:3]
    parcel_thermal_level = parcel_record[3]
    parcel_weight_amount = parcel_record[4]
    slip_velocity = gas_velocity - parcel_velocity
    slip_squared = jnp.sum(slip_velocity * slip_velocity, axis=0)
    drag_factor = (
        drag_rate
        * jnp.power(parcel_weight_amount, -2.0 / 3.0)
        * (1.0 + 0.15 * jnp.power(slip_squared + 1.0, 0.3435))
    )
    following_motion = (parcel_velocity + drag_factor * gas_velocity) / (1.0 + drag_factor)
    surface_steam_share = (
        condensed_shares
        * surface_steam_factor[:, None]
        * jnp.exp(2.0 * (parcel_thermal_level - 0.75))
    )
    species_rates = evap_rate * parcel_weight_amount * (surface_steam_share - gas_vapour)
    evaporated_weight = jnp.sum(species_rates, axis=0)
    thermal_exchange = (
        warming_speed
        * (ambient_thermal_level - parcel_thermal_level)
        * jnp.power(parcel_weight_amount, 1.0 / 3.0)
    )
    following_thermal_level = (
        parcel_thermal_level
        + (thermal_exchange - latent_boiling_energy * evaporated_weight) / parcel_weight_amount
    )
    following_weight = parcel_weight_amount - evaporated_weight
    momentum_terms = (
        parcel_weight_amount * (parcel_velocity - following_motion)
        + evaporated_weight * following_motion
    )
    energy_terms = vapour_heat * evaporated_weight - thermal_exchange
    source_terms = jnp.concatenate([momentum_terms, energy_terms[None], species_rates], axis=0)
    source_terms = source_terms * (alive_mask * volume_inverse)
    updated_parcel_record = jnp.concatenate(
        [following_motion, following_thermal_level[None], following_weight[None]], axis=0
    )
    parcel_next = jnp.where(alive_mask[None] > 0.5, updated_parcel_record, parcel_record)
    return (source_terms, parcel_next, evaporated_weight * alive_mask)


def neighbours(values_grid):
    edge = values_grid.shape[0]
    padded_x = jnp.pad(values_grid, ((1, 1), (0, 0)))
    summed = padded_x[2:] + padded_x[:-2]
    padded_y = jnp.pad(values_grid, ((0, 0), (edge, edge)))
    summed = summed + padded_y[:, 2 * edge :] + padded_y[:, : -2 * edge]
    padded_z = jnp.pad(values_grid, ((0, 0), (1, 1)))
    depth = jnp.arange(values_grid.shape[1], dtype=jnp.int32) % edge
    upper_mask = (depth < edge - 1).astype(values_grid.dtype)
    lower_mask = (depth > 0).astype(values_grid.dtype)
    return summed + padded_z[:, 2:] * upper_mask + padded_z[:, :-2] * lower_mask


def relax(coarse_source):
    solution = jnp.zeros_like(coarse_source)
    for sweep in range(SWEEPS):
        solution = (neighbours(solution) + coarse_source) / 6.0
    return solution


def body(gas_state, parcel_record, condensed_shares, surface_steam_factor, fine_cell, block_counts):
    fields = gas_state.shape[0]
    planes = gas_state.shape[1]
    cross_cells = gas_state.shape[2]
    slab_count = lax.axis_size("slab")
    cross_count = lax.axis_size("cross")
    slab_index = lax.axis_index("slab")
    padded_gas = with_halo(gas_state, (("slab", 1),), 1)
    gas_flat = padded_gas.reshape(fields, (planes + 2) * cross_cells)
    ambient_layer_fields = jnp.take(gas_flat, fine_cell, axis=1)
    slot_in_block = jnp.arange(BLOCK, dtype=jnp.int32)
    alive_mask = (slot_in_block[None, :] < block_counts[:, None]).reshape(-1).astype(jnp.float32)
    source_terms, parcel_next, evaporated_weight = advance(
        ambient_layer_fields, parcel_record, condensed_shares, surface_steam_factor, alive_mask
    )
    extended = (
        jnp.zeros((fields, (planes + 2) * cross_cells), jnp.float32)
        .at[:, fine_cell]
        .add(source_terms)
    )
    extended = extended.reshape(fields, planes + 2, cross_cells)
    from_above = shifted(extended[:, 0], "slab", -1)
    from_below = shifted(extended[:, planes + 1], "slab", 1)
    fine_source = extended[:, 1 : planes + 1]
    fine_source = fine_source.at[:, planes - 1].add(from_above)
    fine_source = fine_source.at[:, 0].add(from_below)
    squared = COARSE * COARSE
    fine_per_coarse = planes * slab_count // COARSE
    cross_per_coarse = cross_cells * cross_count // squared
    column_count = cross_cells // cross_per_coarse
    mass_cells = jnp.sum(fine_source[4:], axis=0) * (1.0 / volume_inverse)
    if fine_per_coarse <= planes:
        own_planes = planes // fine_per_coarse
        owned = mass_cells.reshape(own_planes, fine_per_coarse, column_count, cross_per_coarse)
        owned = jnp.sum(owned, axis=(1, 3)).reshape(-1)
    else:
        group = fine_per_coarse // planes
        owned = jnp.sum(mass_cells.reshape(planes, column_count, cross_per_coarse), axis=(0, 2))
        levels = group.bit_length() - 1
        for level in range(levels - 1, -1, -1):
            half = owned.shape[0] // 2
            upper_side = slab_index // 2**level % 2 == 1
            lower_part = owned[:half]
            upper_part = owned[half:]
            keep = jnp.where(upper_side, upper_part, lower_part)
            send = jnp.where(upper_side, lower_part, upper_part)
            owned = keep + partner(send, "slab", level)
    gathered = lax.all_gather(owned[None], ("slab", "cross"), axis=0, tiled=True)
    if fine_per_coarse <= planes:
        gathered = gathered.reshape(
            slab_count, cross_count, planes // fine_per_coarse, column_count
        )
        coarse_source = jnp.transpose(gathered, (0, 2, 1, 3)).reshape(COARSE, squared)
    else:
        group = fine_per_coarse // planes
        gathered = gathered.reshape(COARSE, group, cross_count, column_count // group)
        coarse_source = jnp.transpose(gathered, (0, 2, 1, 3)).reshape(COARSE, squared)
    correction = relax(coarse_source)
    return (parcel_next, fine_source, correction)


def solution(mesh):
    in_specs = (
        P(None, "slab", "cross"),
        P(None, ("slab", "cross")),
        P(None, ("slab", "cross")),
        P(),
        P(("slab", "cross")),
        P(("slab", "cross")),
    )
    out_specs = (P(None, ("slab", "cross")), P(None, "slab", "cross"), P())
    return jax.shard_map(body, mesh=mesh, in_specs=in_specs, out_specs=out_specs, check_vma=False)
```

profile of v0, /device:TPU:8, one launch (start us, length us, event | category | flops | bytes accessed | tf_op | source)
XLA Modules:
  0.0 170.4 jit_solution(5224186087210317424)
XLA Ops:
  7.2 0.0 copy-start
  7.2 0.0 all-gather.3.cloned.1.call-start
  7.2 2.0 %fusion.50 = (f32[16,1,2048]{2,1,0:T(1,128)S(1)}, f32[16,1,2048]{2,1,0:T(1,128)S(1)}) fusion(f32[16,8,2048]{2,1,0:T(8,128)} %param.10), kind=kLoop, calls=%fused_computation.91 | loop fusion | bytes 524288 | tf_op jit(solution)/shard_map/slice | solution.py:24
  9.2 3.4 %collective-permute-start = (f32[16,1,2048]{2,0,1:T(8,128)S(1)}, f32[16,1,2048]{2,0,1:T(8,128)S(1)}, u32[]{:S(2)}, u32[]{:S(2)}) collective-permute-start(f32[16,1,2048]{2,0,1:T(8,128)S(1)} %copy.117), channel_id=1, source_target_pairs={{0,4},{4,8},{8,12},{12,16},{16,20},{20,24},{24,28},{1,5},{5,9},{9,... | collective-permute-start | bytes 393224 | tf_op jit(solution)/shard_map/ppermute | solution.py:26
  12.7 3.3 %collective-permute-start.1 = (f32[16,1,2048]{2,0,1:T(8,128)S(1)}, f32[16,1,2048]{2,0,1:T(8,128)S(1)}, u32[]{:S(2)}, u32[]{:S(2)}) collective-permute-start(f32[16,1,2048]{2,0,1:T(8,128)S(1)} %copy.118), channel_id=1, source_target_pairs={{4,0},{8,4},{12,8},{16,12},{20,16},{24,20},{28,24},{5,1},{9,5},{13... | collective-permute-start | bytes 393224 | tf_op jit(solution)/shard_map/ppermute | solution.py:27
  16.1 0.7 compare_select_fusion
  16.8 0.7 compare_and_fusion
  17.5 0.7 select_bitcast_fusion.1
  18.2 0.0 collective-permute-done
  18.2 0.1 copy.105
  18.4 1.7 %collective-permute-done.1 = f32[16,1,2048]{2,0,1:T(8,128)S(1)} collective-permute-done((f32[16,1,2048]{2,0,1:T(8,128)S(1)}, f32[16,1,2048]{2,0,1:T(8,128)S(1)}, u32[]{:S(2)}, u32[]{:S(2)}) %collective-permute-start.1) | collective-permute-done | bytes 131104 | tf_op jit(solution)/shard_map/ppermute | solution.py:27
  20.1 0.1 copy.106
  20.2 0.0 copy-done
  20.2 0.4 pad_maximum_fusion
  20.6 5.4 %copy.107 = f32[16,10,2048]{0,2,1:T(8,128)} copy(f32[16,10,2048]{2,1,0:T(8,128)S(1)} %pad_maximum_fusion) | data formatting | bytes 2621440 | tf_op jit(solution)/shard_map/concatenate | solution.py:28
  26.0 0.0 copy-start.1
  26.0 14.8 %gather_fusion = f32[4096,16]{1,0:T(8,128)S(1)} fusion(f32[16,20480]{0,1:T(8,128)} %bitcast.39, s32[4096]{0:T(1024)S(1)} %get-tuple-element.61), kind=kCustom, calls=%fused_computation | custom fusion | bytes 540672 | tf_op jit(solution)/shard_map/jit(_take)/gather | solution.py:119
  40.8 0.0 copy-start.2
  40.8 0.0 copy-start.4
  40.8 0.6 copy.108
  41.4 0.0 copy-done.1
  41.5 0.1 multiply_reduce_fusion
  41.5 0.2 broadcast_add_fusion
  41.7 0.0 copy-done.2
  41.8 0.0 copy-done.4
  41.8 0.1 fusion.47
  41.9 0.2 multiply_subtract_fusion
  42.1 0.1 multiply_add_fusion
  42.2 0.1 fusion.33
  42.3 0.6 copy.109
  42.9 26.9 %scatter_custom_fusion = f32[16,20480]{0,1:T(8,128)} fusion(s32[4096]{0:T(1024)S(1)} %get-tuple-element.60, f32[4096,16]{1,0:T(8,128)S(1)} %copy.109, f32[]{:T(128)} %constant.122.clone.1), kind=kCustom, calls=%fused_computation.2 | custom fusion | flops 65536 | bytes 1310724 | tf_op jit(solution)/shard_map/scatter-add | solution.py:128
  69.8 2.1 %fusion.49 = (f32[16,1,2048]{0,2,1:T(8,128)S(1)}, f32[16,1,2048]{0,2,1:T(8,128)S(1)}, f32[16,1,2048]{0,2,1:T(8,128)S(1)}) fusion(f32[16,10,2048]{0,2,1:T(8,128)} %bitcast.33), kind=kLoop, calls=%fused_computation.90 | loop fusion | bytes 786432 | tf_op jit(solution)/shard_map/slice | solution.py:132
  71.9 1.0 copy.121
  72.8 3.7 %collective-permute-start.2 = (f32[16,2048]{1,0:T(8,128)}, f32[16,2048]{1,0:T(8,128)}, u32[]{:S(2)}, u32[]{:S(2)}) collective-permute-start(f32[16,2048]{1,0:T(8,128)} %bitcast.13), channel_id=1, source_target_pairs={{4,0},{8,4},{12,8},{16,12},{20,16},{24,20},{28,24},{5,1},{9,5},{13... | collective-permute-start | bytes 393224 | tf_op jit(solution)/shard_map/ppermute | solution.py:35
  76.5 7.3 %slice.196 = f32[16,8,2048]{0,2,1:T(8,128)} slice(f32[16,10,2048]{0,2,1:T(8,128)} %bitcast.34), slice={[0:16], [1:9], [0:2048]} | slice | bytes 2097152 | tf_op jit(solution)/shard_map/slice | solution.py:133
  83.9 5.1 %copy.119 = f32[16,8,2048]{2,0,1:T(8,128)S(1)} copy(f32[16,8,2048]{0,2,1:T(8,128)} %slice.196) | data formatting | bytes 2097152
  89.0 0.3 copy.120
  89.3 0.3 copy.122
  89.6 2.3 %collective-permute-start.3 = (f32[16,2048]{1,0:T(8,128)S(1)}, f32[16,2048]{1,0:T(8,128)S(1)}, u32[]{:S(2)}, u32[]{:S(2)}) collective-permute-start(f32[16,2048]{1,0:T(8,128)S(1)} %bitcast.44), channel_id=1, source_target_pairs={{0,4},{4,8},{8,12},{12,16},{16,20},{20,24},{24,28},{1,5},{5,9},{9,... | collective-permute-start | bytes 393224 | tf_op jit(solution)/shard_map/ppermute | solution.py:35
  91.9 0.0 collective-permute-done.2
  91.9 0.9 fusion.35
  92.8 4.5 %collective-permute-done.3 = f32[16,2048]{1,0:T(8,128)S(1)} collective-permute-done((f32[16,2048]{1,0:T(8,128)S(1)}, f32[16,2048]{1,0:T(8,128)S(1)}, u32[]{:S(2)}, u32[]{:S(2)}) %collective-permute-start.3) | collective-permute-done | bytes 131104 | tf_op jit(solution)/shard_map/ppermute | solution.py:35
  97.4 0.0 copy-start.3
  97.4 0.2 slice_reduce_fusion
  97.6 0.3 copy.114
  98.0 1.3 reduce_sum.42
  99.3 0.2 copy.115
  99.4 0.7 reshape.210
  100.1 0.0 all-gather.3.cloned.1.call-update
  100.1 0.0 copy-done.3
  100.2 0.1 fusion.42
  100.2 0.1 divide_add_fusion
  100.3 0.7 maximum_select_fusion
  101.0 1.6 copy.116
  102.6 50.9 %all-gather.3.cloned.1.call-done = f32[32,1,8192]{2,1,0:T(1,128)} async-done(((f32[1,1,8192]{2,1,0:T(1,128)}), f32[32,1,8192]{2,1,0:T(1,128)}) %all-gather.3.cloned.1.call-update) | async-done | bytes 1048592 | tf_op jit(solution)/shard_map/all_gather | solution.py:157
  153.5 3.8 %reduce.5 = f32[32,8192]{1,0:T(8,128)S(1)} reduce(f32[32,1,8192]{2,1,0:T(1,128)} %all-gather.3.cloned.1.call-done, f32[]{:T(128)} %constant.162), dimensions={1}, to_apply=%all-gather.reduce_sub_computation | reduce | bytes 2097156 | tf_op jit(solution)/shard_map/all_gather | solution.py:157
  157.3 0.6 copy.123
  157.9 0.1 broadcast_in_dim.29
  158.0 1.1 fusion.28
  159.1 1.1 fusion.8
  160.3 1.1 fusion.15
  161.4 2.1 %fusion.22 = f32[64,4096]{1,0:T(8,128)} fusion(f32[64,4096]{1,0:T(8,128)S(1)} %bitcast.38, f32[64,4096]{1,0:T(8,128)S(1)} %fusion.15, f32[4096]{0:T(1024)S(1)} %get-tuple-element.63, f32[4096]{0:T(1024)S(1)} %get-tuple-element.62), kind=kLoop, calls=%fused_computation.37 | loop fusion | flops 2359296 | bytes 3178496 | tf_op jit(solution)/shard_map/div | solution.py:106
  (7 shorter events, 0.2 us)
Async XLA Ops:
  7.2 13.1 %copy-start = (f32[16,8,2048]{2,1,0:T(8,128)S(1)}, f32[16,8,2048]{2,1,0:T(8,128)}, u32[]{:S(2)}) copy-start(f32[16,8,2048]{2,1,0:T(8,128)} %param.10) | copy-start | bytes 3145732
  7.2 146.3 %all-gather.3.cloned.1.call-start = ((), (), s32[]{:S(2)}) async-start(), calls=%async_computation | async-start | bytes 1081344 | tf_op jit(solution)/shard_map/all_gather | solution.py:157
  9.2 9.0 %collective-permute-start = (f32[16,1,2048]{2,0,1:T(8,128)S(1)}, f32[16,1,2048]{2,0,1:T(8,128)S(1)}, u32[]{:S(2)}, u32[]{:S(2)}) collective-permute-start(f32[16,1,2048]{2,0,1:T(8,128)S(1)} %copy.117), channel_id=1, source_target_pairs={{0,4},{4,8},{8,12},{12,16},{16,20},{20,24},{24,28},{1,5},{5,9},{9,... | collective-permute-start | bytes 393224 | tf_op jit(solution)/shard_map/ppermute | solution.py:26
  12.7 7.4 %collective-permute-start.1 = (f32[16,1,2048]{2,0,1:T(8,128)S(1)}, f32[16,1,2048]{2,0,1:T(8,128)S(1)}, u32[]{:S(2)}, u32[]{:S(2)}) collective-permute-start(f32[16,1,2048]{2,0,1:T(8,128)S(1)} %copy.118), channel_id=1, source_target_pairs={{4,0},{8,4},{12,8},{16,12},{20,16},{24,20},{28,24},{5,1},{9,5},{13... | collective-permute-start | bytes 393224 | tf_op jit(solution)/shard_map/ppermute | solution.py:27
  26.0 15.4 %copy-start.1 = (f32[5,4096]{1,0:T(8,128)S(1)}, f32[5,4096]{1,0:T(8,128)}, u32[]{:S(2)}) copy-start(f32[5,4096]{1,0:T(8,128)} %param.11) | copy-start | bytes 245764
  40.8 1.0 copy-start.2
  40.8 0.9 copy-start.4
  72.8 19.1 %collective-permute-start.2 = (f32[16,2048]{1,0:T(8,128)}, f32[16,2048]{1,0:T(8,128)}, u32[]{:S(2)}, u32[]{:S(2)}) collective-permute-start(f32[16,2048]{1,0:T(8,128)} %bitcast.13), channel_id=1, source_target_pairs={{4,0},{8,4},{12,8},{16,12},{20,16},{24,20},{28,24},{5,1},{9,5},{13... | collective-permute-start | bytes 393224 | tf_op jit(solution)/shard_map/ppermute | solution.py:35
  89.6 7.8 %collective-permute-start.3 = (f32[16,2048]{1,0:T(8,128)S(1)}, f32[16,2048]{1,0:T(8,128)S(1)}, u32[]{:S(2)}, u32[]{:S(2)}) collective-permute-start(f32[16,2048]{1,0:T(8,128)S(1)} %bitcast.44), channel_id=1, source_target_pairs={{0,4},{4,8},{8,12},{12,16},{16,20},{20,24},{24,28},{1,5},{5,9},{9,... | collective-permute-start | bytes 393224 | tf_op jit(solution)/shard_map/ppermute | solution.py:35
  97.4 2.8 %copy-start.3 = (s32[32]{0:T(128)S(1)}, s32[32]{0:T(128)}, u32[]{:S(2)}) copy-start(s32[32]{0:T(128)} %param.15) | copy-start | bytes 388
Sparse Core Ops, SparseCore 0:
  100.3 53.1 all-gather.2
where the time goes:
time: 173 us; the launch traced here: 170 us
  waiting for transfers between devices  57.1 us (33%)
  local copies, waits for them, and re-layouts  43.2 us (25%)
  other arithmetic  43 us (25%)
  between operations  14.3 us (8%)
  starting transfers between devices  12.8 us (7%)
    all_gather x1, waiting for transfers between devices, body(): lax.all_gather(owned[None], ('slab', 'cross'), axis=0, tiled=True)  50.9 us
    scatter-add x1, other arithmetic, body(): extended = jnp.zeros((fields, (planes + 2) * cross_cells), jnp.float32).a...  26.9 us
    gather x2, local copies, waits for them, and re-layouts, body(): ambient_layer_fields = jnp.take(gas_flat, fine_cell, axis=1)  15.3 us
    unnamed x19, local copies, waits for them, and re-layouts  9.69 us
    slice x1, local copies, waits for them, and re-layouts, body(): fine_source = extended[:, 1:planes + 1]  7.3 us
    ppermute x2, starting transfers between devices, shifted(): return lax.ppermute(shard, axis, pairs)  6.01 us
    div x4, other arithmetic, relax(): solution = (neighbours(solution) + coarse_source) / 6.0  5.57 us
    concatenate x1, local copies, waits for them, and re-layouts, with_halo(): shard = jnp.concatenate([before, shard, after], axis=dim)  5.39 us
  transfers between devices with their start and end apart: 5, of which 3 were waited for; matrix products, arithmetic and copies ran while one was open for 11% of the time, Pallas kernels for 0%

commit v1 on v0

v1 whole, which is shorter than its diff:
```python
import functools

import jax
import jax.numpy as jnp
from jax import lax
from jax.experimental import pallas as pl
from jax.experimental.pallas import tpu as pltpu
from jax.sharding import PartitionSpec as P

BLOCK = 128
COARSE = 64
SWEEPS = 4
LANES = 128
WIDE = 8
UNROLL = 4
AXES = ("slab", "cross")
F32 = jnp.float32
VMEM = pl.BlockSpec(memory_space=pltpu.VMEM)
SMEM = pl.BlockSpec(memory_space=pltpu.SMEM)

drag_rate = 0.5
evap_rate = 0.08
warming_speed = 0.3
latent_boiling_energy = 0.5
vapour_heat = 1.5
volume_inverse = 4.0


def rows_in(tile, species):
    return jnp.concatenate([tile[:, 4 : 4 + species], tile[:, 0:4]], axis=1)


def plane_sides():
    return lax.rem(lax.axis_index("slab"), 2) == 0


def edges_kernel(gas, first_pair, second_pair):
    fields, planes, cells = gas.shape
    even = plane_sides()
    for k in range(cells // LANES):
        x = jnp.swapaxes(gas[:, :, k * LANES : (k + 1) * LANES], 0, 1)
        low, high = (rows_in(x[p : p + 1], fields - 4)[0] for p in (0, planes - 1))
        first_pair[k] = jnp.where(even, high, low)
        second_pair[k] = jnp.where(even, low, high)


def tiles_kernel(gas, tiles):
    fields, planes, cells = gas.shape
    per_plane = cells // LANES
    for k in range(per_plane):
        x = jnp.swapaxes(gas[:, :, k * LANES : (k + 1) * LANES], 0, 1)
        x = rows_in(x, fields - 4)
        for p in range(planes):
            tiles[p * per_plane + k] = x[p]


def advance_block(g, record, shares, steam, count):
    species = shares.shape[0]
    lane = lax.broadcasted_iota(jnp.int32, (1, LANES), 1)
    row = lax.broadcasted_iota(jnp.int32, (8, LANES), 0)
    rest = species - 8
    zeros = jnp.zeros((8 - rest, LANES), F32)
    g0, g1 = g
    s0 = shares[0:8]
    s1 = jnp.concatenate([shares[8:species], zeros], axis=0)
    r = jnp.concatenate([zeros, record[0:4]], axis=0)
    thermal = record[3:4]
    mass = record[4:5]
    d = g1 - r
    moving = (row >= 4) & (row < 7)
    slip_squared = jnp.sum(jnp.where(moving, d * d, 0.0), axis=0, keepdims=True)
    log_mass = jnp.log(mass)
    drag = (
        drag_rate
        * jnp.exp(log_mass * (-2.0 / 3.0))
        * (1.0 + 0.15 * jnp.exp(0.3435 * jnp.log(slip_squared + 1.0)))
    )
    following = (r + drag * g1) / (1.0 + drag)
    vapour = jnp.exp(2.0 * (thermal - 0.75))
    scale = evap_rate * mass
    rate0 = scale * (s0 * steam[0:8] * vapour - g0)
    rate1 = scale * (s1 * steam[8:16] * vapour - g1)
    evap = jnp.sum(rate0 + jnp.where(row < rest, rate1, 0.0), axis=0, keepdims=True)
    heat = warming_speed * d[7:8] * jnp.exp(log_mass * (1.0 / 3.0))
    next_thermal = thermal + (heat - latent_boiling_energy * evap) / mass
    next_mass = mass - evap
    momentum = mass * (r - following) + evap * following
    energy = vapour_heat * evap - heat
    alive = lane < count
    weight = jnp.where(alive, volume_inverse, 0.0)
    terms0 = rate0 * weight
    terms1 = jnp.where(row < rest, rate1, jnp.where(row < 7, momentum, energy)) * weight
    updated = jnp.concatenate([following[4:7], next_thermal, next_mass], axis=0)
    return (terms0, terms1), jnp.where(alive, updated, record)


def three_parts(x):
    high = x.astype(jnp.bfloat16).astype(F32)
    x = x - high
    middle = x.astype(jnp.bfloat16).astype(F32)
    return high, middle, x - middle


def deposit(parts, tile_of, first, onehot, number, acc):
    stack = []
    for j in range(number):
        here = tile_of == first + j
        for t0, t1 in parts:
            both = jnp.concatenate([jnp.where(here, t0, 0.0), jnp.where(here, t1, 0.0)], axis=0)
            stack.append(both.astype(jnp.bfloat16))
    stack = jnp.concatenate(stack, axis=0)
    sums = lax.dot_general(
        stack, onehot, (((1,), (1,)), ((), ())), preferred_element_type=F32
    )
    rows = 16
    for j in range(number):
        base = j * len(parts) * rows
        total = sums[base : base + rows]
        for i in range(1, len(parts)):
            total = total + sums[base + i * rows : base + (i + 1) * rows]
        acc[first + j] = acc[first + j] + total


def parcels_kernel(
    cell_s, count_s, steam_s, cell_v, tiles, pair_a, pair_b, record, shares,
    next_record, acc, send_a, send_b, coarse, gas,
):
    per_plane = pair_a.shape[0]
    inner = tiles.shape[0]
    blocks = cell_v.shape[0]
    species = shares.shape[0]
    even = plane_sides()
    below = jnp.where(even, 1, 0)
    for k in range(per_plane):
        a, b = pair_a[k], pair_b[k]
        gas[k] = jnp.where(even, b, a)
        gas[per_plane + inner + k] = jnp.where(even, a, b)

    def fill(i, _):
        for u in range(8):
            gas[per_plane + i * 8 + u] = tiles[i * 8 + u]
        return 0

    lax.fori_loop(0, inner // 8, fill, 0)

    def clear(i, _):
        for u in range(8):
            acc[i * 8 + u] = jnp.zeros(acc.shape[1:], F32)
        return 0

    lax.fori_loop(0, acc.shape[0] // 8, clear, 0)

    species_row = lax.broadcasted_iota(jnp.int32, (16, 1), 0)
    steam = jnp.zeros((16, 1), F32)
    for j in range(species):
        steam = jnp.where(species_row == j, steam_s[j], steam)
    steam = jnp.broadcast_to(steam, (16, LANES))
    spot = lax.broadcasted_iota(jnp.int32, (LANES, LANES), 0)

    def prepare(b):
        cell = cell_v[pl.ds(b, 1), :]
        return cell // LANES, jnp.broadcast_to(lax.rem(cell, LANES), (8, LANES))

    def pick(tile, tile_of, offset, first, j, old):
        here = tile_of == first + j
        return tuple(
            jnp.where(here, jnp.take_along_axis(tile[h * 8 : h * 8 + 8], offset, axis=1), o)
            for h, o in enumerate(old)
        )

    def advance(b, g):
        at = pl.ds(pl.multiple_of(b * LANES, LANES), LANES)
        terms, new = advance_block(g, record[:, at], shares[:, at], steam, count_s[b])
        next_record[:, at] = new
        return tuple(zip(*(three_parts(t) for t in terms)))

    def hot(offset):
        return jnp.where(spot == offset[0:1], 1.0, 0.0).astype(jnp.bfloat16)

    zero = jnp.zeros((8, LANES), F32)

    def group(i, _):
        base = i * UNROLL
        spans = []
        for u in range(UNROLL):
            first = cell_s[(base + u) * LANES] // LANES
            last = cell_s[(base + u) * LANES + LANES - 1] // LANES
            spans.append((first, last))
        narrow = functools.reduce(
            jnp.logical_and, [last - first < WIDE for first, last in spans]
        )

        @pl.when(narrow)
        def _():
            staged = []
            for u in range(UNROLL):
                first = spans[u][0]
                tile_of, offset = prepare(base + u)
                g = (zero, zero)
                for j in range(WIDE):
                    g = pick(gas[first + j], tile_of, offset, first, j, g)
                staged.append((first, tile_of, offset, g))
            staged = [
                (first, tile_of, offset, advance(base + u, g))
                for u, (first, tile_of, offset, g) in enumerate(staged)
            ]
            for first, tile_of, offset, parts in staged:
                deposit(parts, tile_of, first, hot(offset), WIDE, acc)

        @pl.when(jnp.logical_not(narrow))
        def _():
            def one(u, _):
                b = base + u
                first = cell_s[b * LANES] // LANES
                last = cell_s[b * LANES + LANES - 1] // LANES
                tile_of, offset = prepare(b)

                def step(t, g):
                    return pick(gas[t], tile_of, offset, t, 0, g)

                g = lax.fori_loop(first, last + 1, step, (zero, zero))
                parts = advance(b, g)
                onehot = hot(offset)

                def put(t, _):
                    deposit(parts, tile_of, t, onehot, 1, acc)
                    return 0

                return lax.fori_loop(first, last + 1, put, 0)

            lax.fori_loop(0, UNROLL, one, 0)

        return 0

    lax.fori_loop(0, blocks // UNROLL, group, 0)

    for k in range(per_plane):
        low, high = acc[k], acc[per_plane + inner + k]
        send_a[k] = jnp.where(even, high, low)
        send_b[k] = jnp.where(even, low, high)

    planes = inner // per_plane
    lane = lax.broadcasted_iota(jnp.int32, (8, LANES), 1)
    take = lax.rem(lane * 2, LANES)
    row = lax.broadcasted_iota(jnp.int32, (1, 16, 1), 1)

    def mass_of(stack):
        return jnp.sum(jnp.where(row < species, stack, 0.0), axis=1) * (1.0 / volume_inverse)

    def halves(pick_tiles):
        out = []
        for k in range(per_plane):
            mass = mass_of(pick_tiles(k))
            both = mass + pltpu.roll(mass, LANES - 1, axis=1)
            out.append(jnp.take_along_axis(both, take, axis=1))
        return [
            jnp.where(lane < LANES // 2, out[2 * i], out[2 * i + 1])
            for i in range(per_plane // 2)
        ]

    own = halves(
        lambda k: jnp.stack([acc[(p + 1) * per_plane + k] for p in range(planes)])
    )
    for i, piece in enumerate(own):
        coarse[:, i * LANES : (i + 1) * LANES] = piece
    ends = halves(
        lambda k: jnp.stack([acc[k], acc[per_plane + inner + k]] + [jnp.zeros((16, LANES), F32)] * 6)
    )
    columns = per_plane // 2 * LANES
    quarter = per_plane // 8
    for h in range(2):
        for i, piece in enumerate(ends):
            r, c = 4 * h + i // quarter, i % quarter
            coarse[r : r + 1, columns + c * LANES : columns + (c + 1) * LANES] = piece[h : h + 1]


def merge_kernel(acc, pair_a, pair_b, out):
    fields, planes, cells = out.shape
    per_plane = cells // LANES
    even = plane_sides()
    for k in range(per_plane):
        a, b = pair_a[k], pair_b[k]
        from_above = jnp.where(even, a, b)
        from_below = jnp.where(even, b, a)
        rows = [acc[(p + 1) * per_plane + k] for p in range(planes)]
        rows[0] = rows[0] + from_below
        rows[planes - 1] = rows[planes - 1] + from_above
        x = jnp.swapaxes(jnp.stack(rows), 0, 1)
        x = jnp.concatenate([x[fields - 4 :], x[: fields - 4]], axis=0)
        out[:, :, k * LANES : (k + 1) * LANES] = x


def relax_kernel(masks, columns, *refs):
    *parts, out, source, one, two = refs
    planes = parts[0].shape[1]
    cross_count = lax.axis_size("cross")
    slab_count = lax.axis_size("slab")
    me = lax.axis_index("slab") * cross_count + lax.axis_index("cross")
    edge = COARSE
    slabs = edge // planes
    pieces = [(mask, part, i) for part, part_masks in zip(parts, masks) for i, mask in enumerate(part_masks)]

    def place(mask):
        owner = lax.bitwise_xor(me, mask)
        slab = owner // cross_count
        at = pl.multiple_of(lax.rem(owner, cross_count) * columns, LANES)
        return slab, at

    for mask, part, i in pieces:
        slab, at = place(mask)
        source[slab, :, pl.ds(at, columns)] = part[i, :, :columns]
    quarter = columns // 4
    for mask, part, i in pieces:
        slab, at = place(mask)
        for h, target, line in ((0, slab - 1, planes - 1), (1, slab + 1, 0)):
            @pl.when((target >= 0) & (target < slab_count))
            def _():
                for j in range(4):
                    here = pl.ds(pl.multiple_of(at + j * quarter, LANES), quarter)
                    r = 4 * h + j
                    source[target, line : line + 1, here] = (
                        source[target, line : line + 1, here] + part[i, r : r + 1, columns:]
                    )

    squared = edge * edge
    width = squared // LANES
    lane = lax.broadcasted_iota(jnp.int32, (8, LANES), 1)
    row = lax.broadcasted_iota(jnp.int32, (8, LANES), 0)
    inside = lax.rem(lane, edge)
    sixth = 1.0 / 6.0

    def at_lanes(v):
        return pl.ds(v * LANES, LANES)

    def sweep(src, dst):
        def run(s, _):
            up = jnp.minimum(s + 1, slabs - 1)
            dn = jnp.maximum(s - 1, 0)
            has_up = s < slabs - 1
            has_dn = s > 0
            values = [src[s, :, at_lanes(v)] for v in range(width)]
            turned = [pltpu.roll(x, edge, axis=1) for x in values]
            for v in range(width):
                x = values[v]
                above = src[up, 0:1, at_lanes(v)]
                under = src[dn, 7:8, at_lanes(v)]
                above = jnp.where(has_up, above, 0.0)
                under = jnp.where(has_dn, under, 0.0)
                total = jnp.where(row == 7, above, pltpu.roll(x, 7, axis=0))
                total = total + jnp.where(row == 0, under, pltpu.roll(x, 1, axis=0))
                left = turned[v - 1] if v > 0 else jnp.zeros_like(x)
                right = turned[v + 1] if v < width - 1 else jnp.zeros_like(x)
                total = total + turned[v] + jnp.where(lane < edge, left, right)
                total = total + jnp.where(inside < edge - 1, pltpu.roll(x, LANES - 1, axis=1), 0.0)
                total = total + jnp.where(inside > 0, pltpu.roll(x, 1, axis=1), 0.0)
                dst(s, v, (total + source[s, :, at_lanes(v)]) * sixth)
            return 0

        lax.fori_loop(0, slabs, run, 0)

    def into(ref):
        def put(s, v, x):
            ref[s, :, at_lanes(v)] = x
        return put

    def final(s, v, x):
        out[pl.ds(pl.multiple_of(s * 8, 8), 8), at_lanes(v)] = x

    def begin(s, _):
        one[s] = source[s] * sixth
        return 0

    lax.fori_loop(0, slabs, begin, 0)
    buffers = (one, two)
    for step in range(1, SWEEPS):
        src = buffers[(step - 1) % 2]
        sweep(src, final if step == SWEEPS - 1 else into(buffers[step % 2]))


def neighbour_pairs(slab_count, cross_count, start):
    pairs = []
    for s in range(start, slab_count - 1, 2):
        for c in range(cross_count):
            i, j = s * cross_count + c, (s + 1) * cross_count + c
            pairs += [(i, j), (j, i)]
    return pairs


def body(gas_state, parcel_record, condensed_shares, surface_steam_factor, fine_cell, block_counts):
    fields, planes, cells = gas_state.shape
    slots = parcel_record.shape[1]
    slab_count = lax.axis_size("slab")
    cross_count = lax.axis_size("cross")
    device_count = slab_count * cross_count
    squared = COARSE * COARSE
    fine_per_coarse = planes * slab_count // COARSE
    columns = cells * cross_count // squared
    columns = cells // columns
    per_plane = cells // LANES
    inner = planes * per_plane
    blocks = slots // BLOCK
    pairs_a = neighbour_pairs(slab_count, cross_count, 0)
    pairs_b = neighbour_pairs(slab_count, cross_count, 1)

    def swap(a, b):
        return lax.ppermute(a, AXES, pairs_a), lax.ppermute(b, AXES, pairs_b)

    plane = jax.ShapeDtypeStruct((per_plane, fields, LANES), F32)
    edge_a, edge_b = pl.pallas_call(
        edges_kernel, out_shape=(plane, plane), in_specs=[VMEM], out_specs=(VMEM, VMEM), name="edges"
    )(gas_state)
    got_a, got_b = swap(edge_a, edge_b)
    tiles = pl.pallas_call(
        tiles_kernel,
        out_shape=jax.ShapeDtypeStruct((inner, fields, LANES), F32),
        in_specs=[VMEM], out_specs=VMEM, name="tiles",
    )(gas_state)
    total_tiles = inner + 2 * per_plane + WIDE
    parcel_next, acc, send_a, send_b, coarse = pl.pallas_call(
        parcels_kernel,
        out_shape=(
            jax.ShapeDtypeStruct(parcel_record.shape, F32),
            jax.ShapeDtypeStruct((total_tiles, fields, LANES), F32),
            plane,
            plane,
            jax.ShapeDtypeStruct((8, columns + columns // 4), F32),
        ),
        in_specs=[SMEM, SMEM, SMEM] + [VMEM] * 6,
        out_specs=(VMEM,) * 5,
        scratch_shapes=[pltpu.VMEM((total_tiles, fields, LANES), F32)],
        name="parcels",
    )(
        fine_cell, block_counts, surface_steam_factor, fine_cell.reshape(blocks, LANES),
        tiles, got_a, got_b, parcel_record, condensed_shares,
    )
    back_a, back_b = swap(send_a, send_b)
    fine_source = pl.pallas_call(
        merge_kernel,
        out_shape=jax.ShapeDtypeStruct(gas_state.shape, F32),
        in_specs=[VMEM] * 3, out_specs=VMEM, name="merge",
    )(acc, back_a, back_b)

    own_planes = planes
    if fine_per_coarse != 1:
        coarse, own_planes = shared_planes(coarse, columns, planes, fine_per_coarse)
    parts, masks = gather_all(coarse, device_count)
    if fine_per_coarse == 1:
        scratch = pltpu.VMEM((COARSE // planes, planes, squared), F32)
        correction = pl.pallas_call(
            functools.partial(relax_kernel, masks, columns),
            out_shape=jax.ShapeDtypeStruct((COARSE, squared), F32),
            in_specs=[VMEM] * len(parts), out_specs=VMEM,
            scratch_shapes=[scratch] * 3, name="relax",
        )(*parts)
    else:
        correction = relax_plain(arrange(parts, masks, columns, own_planes, fine_per_coarse, planes))
    return (parcel_next, fine_source, correction)


def gather_all(x, device_count):
    bits = list(range(device_count.bit_length() - 1))[::-1]
    groups = []
    upper = bits[:-1]
    if len(upper) % 2:
        groups.append(upper[:1])
        upper = upper[1:]
    groups += [upper[i : i + 2] for i in range(0, len(upper), 2)]
    held, masks = x[None], [0]

    def send(mask):
        return lax.ppermute(held, AXES, [(i, i ^ mask) for i in range(device_count)])

    for group in groups:
        steps = [1 << group[0]]
        if len(group) == 2:
            steps += [1 << group[1], (1 << group[0]) + (1 << group[1])]
        arrived = [send(mask) for mask in steps]
        held = jnp.concatenate([held] + arrived, axis=0)
        masks = masks + [m ^ mask for mask in steps for m in masks]
    return (held, send(1)), (masks, [m ^ 1 for m in masks])


def shared_planes(coarse, columns, planes, fine_per_coarse):
    slab_count = lax.axis_size("slab")
    slab_index = lax.axis_index("slab")
    own = coarse[:, :columns]
    ends = coarse[:, columns:].reshape(2, columns)
    up = [(i, i + 1) for i in range(slab_count - 1)]
    down = [(j, i) for i, j in up]
    own = own.at[planes - 1].add(lax.ppermute(ends[0], "slab", down))
    own = own.at[0].add(lax.ppermute(ends[1], "slab", up))
    if fine_per_coarse <= planes:
        own = own.reshape(planes // fine_per_coarse, fine_per_coarse, columns).sum(axis=1)
        return own.reshape(-1, LANES), planes // fine_per_coarse
    own = own.sum(axis=0)
    group = fine_per_coarse // planes
    for level in range(group.bit_length() - 2, -1, -1):
        half = own.shape[0] // 2
        upper_side = slab_index // 2**level % 2 == 1
        keep = jnp.where(upper_side, own[half:], own[:half])
        send = jnp.where(upper_side, own[:half], own[half:])
        pairs = [(i, i ^ 1 << level) for i in range(slab_count)]
        own = keep + lax.ppermute(send, "slab", pairs)
    return own.reshape(-1, LANES), 1


def arrange(parts, masks, columns, own_planes, fine_per_coarse, planes):
    slab_count = lax.axis_size("slab")
    cross_count = lax.axis_size("cross")
    me = lax.axis_index("slab") * cross_count + lax.axis_index("cross")
    rows = jnp.concatenate(parts, axis=0)
    rows = rows.reshape(rows.shape[0], -1)
    distance = jnp.array([m for part in masks for m in part], jnp.int32)
    position = jnp.argsort(distance)[lax.bitwise_xor(me, jnp.arange(rows.shape[0]))]
    rows = rows[position]
    if fine_per_coarse <= planes:
        rows = rows.reshape(slab_count, cross_count, own_planes, columns)
    else:
        group = fine_per_coarse // planes
        rows = rows.reshape(COARSE, group, cross_count, columns // group)
    return jnp.transpose(rows, (0, 2, 1, 3)).reshape(COARSE, COARSE * COARSE)


def neighbours(grid):
    edge = grid.shape[0]
    x = jnp.pad(grid, ((1, 1), (0, 0)))
    y = jnp.pad(grid, ((0, 0), (edge, edge)))
    z = jnp.pad(grid, ((0, 0), (1, 1)))
    depth = jnp.arange(grid.shape[1], dtype=jnp.int32) % edge
    total = x[2:] + x[:-2] + y[:, 2 * edge :] + y[:, : -2 * edge]
    return total + jnp.where(depth < edge - 1, z[:, 2:], 0.0) + jnp.where(depth > 0, z[:, :-2], 0.0)


def relax_plain(coarse_source):
    correction = jnp.zeros_like(coarse_source)
    for _ in range(SWEEPS):
        correction = (neighbours(correction) + coarse_source) / 6.0
    return correction


def solution(mesh):
    in_specs = (
        P(None, "slab", "cross"),
        P(None, ("slab", "cross")),
        P(None, ("slab", "cross")),
        P(),
        P(("slab", "cross")),
        P(("slab", "cross")),
    )
    out_specs = (P(None, ("slab", "cross")), P(None, "slab", "cross"), P())
    return jax.shard_map(body, mesh=mesh, in_specs=in_specs, out_specs=out_specs, check_vma=False)
```

time: 173 us -> 58.8 us (0.34); the launches traced: 170 us -> 58.4 us
  other arithmetic: 43 us -> 0.79 us
  local copies, waits for them, and re-layouts: 43.2 us -> 3.06 us
  waiting for transfers between devices: 57.1 us -> 18.1 us
  Pallas kernels: 0 us -> 21.1 us
  between operations: 14.3 us -> 0.75 us
  starting transfers between devices: 12.8 us -> 14.6 us
    all_gather x1 -> x0, waiting for transfers between devices: 50.9 us -> none  [body(): lax.all_gather(owned[None], ('slab', 'cross'), axis=0, tiled=True)]
    scatter-add x3 -> x0, other arithmetic: 27.9 us -> none  [the longest x1 26.9 us: body(): extended = jnp.zeros((fields, (planes + 2) * cross_cells), jnp.float32).a...]
    pallas_call x0 -> x5, Pallas kernels: none -> 21.1 us  [the longest x1 7.69 us: body(): pl.pallas_call(functools.partial(relax_kernel, masks, columns), out_shape...]
    gather x2 -> x0, local copies, waits for them, and re-layouts: 15.3 us -> none  [body(): ambient_layer_fields = jnp.take(gas_flat, fine_cell, axis=1)]
    ppermute x4 -> x11, waiting for transfers between devices: 6.23 us -> 18.1 us  [the longest x4 9.28 us: swap(): return (lax.ppermute(a, AXES, pairs_a), lax.ppermute(b, AXES, pairs_b))]
    slice x3 -> x0, local copies, waits for them, and re-layouts: 11.3 us -> none  [the longest x1 7.3 us: body(): fine_source = extended[:, 1:planes + 1]]
    unnamed x19 -> x22, local copies, waits for them, and re-layouts: 9.69 us -> 3.05 us
    div x4 -> x0, other arithmetic: 5.57 us -> none  [relax(): solution = (neighbours(solution) + coarse_source) / 6.0]
  transfers between devices with their start and end apart: 5 -> 11, of which waited for: 3 -> 6; matrix products, arithmetic and copies ran while one was open for 11% -> 2% of each run, Pallas kernels for 0% -> 9%
where the time goes in v1:
time: 58.8 us; the launch traced here: 58.4 us
  Pallas kernels  21.1 us (36%)
  waiting for transfers between devices  18.1 us (31%)
  starting transfers between devices  14.6 us (25%)
  local copies, waits for them, and re-layouts  3.06 us (5%)
  other arithmetic  0.79 us (1%)
  between operations  0.75 us (1%)
    ppermute x4, waiting for transfers between devices, swap(): return (lax.ppermute(a, AXES, pairs_a), lax.ppermute(b, AXES, pairs_b))  9.28 us
    ppermute x7, waiting for transfers between devices, send(): lax.ppermute(held, AXES, [(i, i ^ mask) for i in range(device_count)])  8.82 us
    ppermute x7, starting transfers between devices, send(): lax.ppermute(held, AXES, [(i, i ^ mask) for i in range(device_count)])  7.74 us
    pallas_call x1, Pallas kernels, body(): pl.pallas_call(functools.partial(relax_kernel, masks, columns), out_shape...  7.69 us
    ppermute x4, starting transfers between devices, swap(): return (lax.ppermute(a, AXES, pairs_a), lax.ppermute(b, AXES, pairs_b))  6.83 us
    pallas_call x1, Pallas kernels, body(): pl.pallas_call(parcels_kernel, out_shape=(jax.ShapeDtypeStruct(parcel_rec...  6.28 us
    unnamed x22, local copies, waits for them, and re-layouts  3.05 us
    pallas_call x1, Pallas kernels, body(): pl.pallas_call(merge_kernel, out_shape=jax.ShapeDtypeStruct(gas_state.sha...  2.61 us
  transfers between devices with their start and end apart: 11, of which 6 were waited for; matrix products, arithmetic and copies ran while one was open for 2% of the time, Pallas kernels for 9%

profile of v1, /device:TPU:8, one launch (start us, length us, event | category | flops | bytes accessed | tf_op | source)
XLA Modules:
  0.0 58.4 jit_solution(2387277207191945280)
XLA Ops:
  0.6 2.1 %edges.1 = (f32[16,16,128]{2,1,0:T(8,128)}, f32[16,16,128]{2,1,0:T(8,128)}) custom-call(f32[16,8,2048]{2,1,0:T(8,128)} %gas.3), custom_call_target="tpu_custom_call" | custom-call | tf_op jit(solution)/shard_map/edges/pallas_call | solution.py:409
  2.7 1.5 %collective-permute-start = (f32[16,16,128]{2,1,0:T(8,128)}, f32[16,16,128]{2,1,0:T(8,128)S(1)}, u32[]{:S(2)}, u32[]{:S(2)}) collective-permute-start(f32[16,16,128]{2,1,0:T(8,128)} %get-tuple-element.10), channel_id=1, source_target_pairs={{0,4},{4,0},{1,5},{5,1},{2,6},{6,2},{3,7},{7,3},{8,12},{12,8},{9,1... | collective-permute-start | bytes 393224 | tf_op jit(solution)/shard_map/ppermute | solution.py:406
  4.2 1.9 %collective-permute-start.1 = (f32[16,16,128]{2,1,0:T(8,128)}, f32[16,16,128]{2,1,0:T(8,128)S(1)}, u32[]{:S(2)}, u32[]{:S(2)}) collective-permute-start(f32[16,16,128]{2,1,0:T(8,128)} %get-tuple-element.11), channel_id=1, source_target_pairs={{4,8},{8,4},{5,9},{9,5},{6,10},{10,6},{7,11},{11,7},{12,16},{16,12... | collective-permute-start | bytes 393224 | tf_op jit(solution)/shard_map/ppermute | solution.py:406
  6.1 2.5 %tiles.1 = f32[128,16,128]{2,1,0:T(8,128)} custom-call(f32[16,8,2048]{2,1,0:T(8,128)} %gas.3), custom_call_target="tpu_custom_call" | custom-call | tf_op jit(solution)/shard_map/tiles/pallas_call | solution.py:413
  8.6 0.0 collective-permute-done.pair_a
  8.6 0.0 copy-start.2
  8.6 3.6 %collective-permute-done.1.pair_b = f32[16,16,128]{2,1,0:T(8,128)S(1)} collective-permute-done((f32[16,16,128]{2,1,0:T(8,128)}, f32[16,16,128]{2,1,0:T(8,128)S(1)}, u32[]{:S(2)}, u32[]{:S(2)}) %collective-permute-start.1) | collective-permute-done | bytes 131104 | tf_op jit(solution)/shard_map/ppermute | solution.py:406
  12.1 0.0 copy-start.3
  12.2 0.0 copy-done.2
  12.2 0.7 %copy-done.3 = f32[16,16,128]{2,1,0:T(8,128)} copy-done((f32[16,16,128]{2,1,0:T(8,128)}, f32[16,16,128]{2,1,0:T(8,128)S(1)}, u32[]{:S(2)}) %copy-start.3) | copy-done | bytes 131096
  12.8 6.3 %parcels.1 = (f32[5,4096]{1,0:T(8,128)}, f32[168,16,128]{2,1,0:T(8,128)}, f32[16,16,128]{2,1,0:T(8,128)}, f32[16,16,128]{2,1,0:T(8,128)}, f32[8,1280]{1,0:T(8,128)}) custom-call(s32[4096]{0:T(1024)} %cell_s.1, s32[32]{0:T(128)} %count_s.1, f32[12]{0:T(128)} %steam_s.1, s32[32,128]{1,0:T(8,128)} %bitcast.7, f32[128,16,128]{2,1,0:T(8,128)} %tiles.1, ...), custom_call_target="tpu_custom_call" | custom-call | tf_op jit(solution)/shard_map/parcels/pallas_call | solution.py:419
  19.1 0.0 copy-start.7
  19.1 0.0 copy-start.6
  19.1 1.6 %collective-permute-start.6 = (f32[1,8,1280]{2,1,0:T(8,128)}, f32[1,8,1280]{2,1,0:T(8,128)S(1)}, u32[]{:S(2)}, u32[]{:S(2)}) collective-permute-start(f32[1,8,1280]{2,1,0:T(8,128)} %bitcast.3), channel_id=1, source_target_pairs={{0,24},{1,25},{2,26},{3,27},{4,28},{5,29},{6,30},{7,31},{8,16},{9,... | collective-permute-start | bytes 122888 | tf_op jit(solution)/shard_map/ppermute | solution.py:471
  20.7 2.5 %collective-permute-start.5 = (f32[1,8,1280]{2,1,0:T(8,128)}, f32[1,8,1280]{2,1,0:T(8,128)S(1)}, u32[]{:S(2)}, u32[]{:S(2)}) collective-permute-start(f32[1,8,1280]{2,1,0:T(8,128)} %bitcast.4), channel_id=1, source_target_pairs={{0,8},{1,9},{2,10},{3,11},{4,12},{5,13},{6,14},{7,15},{8,0},{9,1},... | collective-permute-start | bytes 122888 | tf_op jit(solution)/shard_map/ppermute | solution.py:471
  23.2 0.0 collective-permute-start.4
  23.2 0.8 %constant_dynamic-update-slice_fusion.6 = f32[16,8,1280]{2,1,0:T(8,128)S(1)} fusion(f32[8,1280]{1,0:T(8,128)} %get-tuple-element.16), kind=kLoop, calls=%fused_computation.7 | loop fusion | bytes 81920
  24.1 0.0 collective-permute-done.6
  24.1 1.8 %collective-permute-done.5 = f32[1,8,1280]{2,1,0:T(8,128)S(1)} collective-permute-done((f32[1,8,1280]{2,1,0:T(8,128)}, f32[1,8,1280]{2,1,0:T(8,128)S(1)}, u32[]{:S(2)}, u32[]{:S(2)}) %collective-permute-start.5) | collective-permute-done | bytes 40992 | tf_op jit(solution)/shard_map/ppermute | solution.py:471
  25.8 2.5 %collective-permute-done.4 = f32[1,8,1280]{2,1,0:T(8,128)S(1)} collective-permute-done((f32[1,8,1280]{2,1,0:T(8,128)}, f32[1,8,1280]{2,1,0:T(8,128)S(1)}, u32[]{:S(2)}, u32[]{:S(2)}) %collective-permute-start.4) | collective-permute-done | bytes 40992 | tf_op jit(solution)/shard_map/ppermute | solution.py:471
  28.3 0.8 %pad_maximum_fusion = f32[4,8,1280]{2,1,0:T(8,128)S(1)} fusion(f32[1,8,1280]{2,1,0:T(8,128)S(1)} %collective-permute-done.6, f32[1,8,1280]{2,1,0:T(8,128)S(1)} %collective-permute-done.5, f32[1,8,1280]{2,1,0:T(8,128)S(1)} %collective-permute-done.4, f32[1,8,1280]{2,1,0:T(8,128)} %bitcast.6), kind=kLoop, calls=%fused_computation | loop fusion | flops 122880 | bytes 327680 | tf_op jit(solution)/shard_map/concatenate | solution.py:478
  29.1 0.1 collective-permute-start.9
  29.2 1.6 %collective-permute-start.8 = (f32[4,8,1280]{2,1,0:T(8,128)S(1)}, f32[4,8,1280]{2,1,0:T(8,128)S(1)}, u32[]{:S(2)}, u32[]{:S(2)}) collective-permute-start(f32[4,8,1280]{2,1,0:T(8,128)S(1)} %pad_maximum_fusion), channel_id=1, source_target_pairs={{0,2},{1,3},{2,0},{3,1},{4,6},{5,7},{6,4},{7,5},{8,10},{9,11},{10,... | collective-permute-start | bytes 491528 | tf_op jit(solution)/shard_map/ppermute | solution.py:471
  30.8 1.9 %collective-permute-start.7 = (f32[4,8,1280]{2,1,0:T(8,128)S(1)}, f32[4,8,1280]{2,1,0:T(8,128)S(1)}, u32[]{:S(2)}, u32[]{:S(2)}) collective-permute-start(f32[4,8,1280]{2,1,0:T(8,128)S(1)} %pad_maximum_fusion), channel_id=1, source_target_pairs={{0,4},{1,5},{2,6},{3,7},{4,0},{5,1},{6,2},{7,3},{8,12},{9,13},{10,... | collective-permute-start | bytes 491528 | tf_op jit(solution)/shard_map/ppermute | solution.py:471
  32.7 4.6 %collective-permute-done.7 = f32[4,8,1280]{2,1,0:T(8,128)S(1)} collective-permute-done((f32[4,8,1280]{2,1,0:T(8,128)S(1)}, f32[4,8,1280]{2,1,0:T(8,128)S(1)}, u32[]{:S(2)}, u32[]{:S(2)}) %collective-permute-start.7) | collective-permute-done | bytes 163872 | tf_op jit(solution)/shard_map/ppermute | solution.py:471
  37.3 0.0 collective-permute-done.8
  37.3 0.0 collective-permute-done.9
  37.3 0.0 copy-start
  37.3 0.1 collective-permute-start.10
  37.4 0.0 copy-done.7
  37.4 0.8 %collective-permute-start.2 = (f32[16,16,128]{2,1,0:T(8,128)S(1)}, f32[16,16,128]{2,1,0:T(8,128)S(1)}, u32[]{:S(2)}, u32[]{:S(2)}) collective-permute-start(f32[16,16,128]{2,1,0:T(8,128)S(1)} %copy-done.7), channel_id=1, source_target_pairs={{0,4},{4,0},{1,5},{5,1},{2,6},{6,2},{3,7},{7,3},{8,12},{12,8},{9,1... | collective-permute-start | bytes 393224 | tf_op jit(solution)/shard_map/ppermute | solution.py:406
  38.2 0.0 copy-done.6
  38.2 2.6 %collective-permute-start.3 = (f32[16,16,128]{2,1,0:T(8,128)S(1)}, f32[16,16,128]{2,1,0:T(8,128)S(1)}, u32[]{:S(2)}, u32[]{:S(2)}) collective-permute-start(f32[16,16,128]{2,1,0:T(8,128)S(1)} %copy-done.6), channel_id=1, source_target_pairs={{4,8},{8,4},{5,9},{9,5},{6,10},{10,6},{7,11},{11,7},{12,16},{16,12... | collective-permute-start | bytes 393224 | tf_op jit(solution)/shard_map/ppermute | solution.py:406
  40.9 2.5 %collective-permute-done.2.pair_a = f32[16,16,128]{2,1,0:T(8,128)S(1)} collective-permute-done((f32[16,16,128]{2,1,0:T(8,128)S(1)}, f32[16,16,128]{2,1,0:T(8,128)S(1)}, u32[]{:S(2)}, u32[]{:S(2)}) %collective-permute-start.2) | collective-permute-done | bytes 131104 | tf_op jit(solution)/shard_map/ppermute | solution.py:406
  43.3 0.0 copy-start.4
  43.3 3.2 %collective-permute-done.3.pair_b = f32[16,16,128]{2,1,0:T(8,128)S(1)} collective-permute-done((f32[16,16,128]{2,1,0:T(8,128)S(1)}, f32[16,16,128]{2,1,0:T(8,128)S(1)}, u32[]{:S(2)}, u32[]{:S(2)}) %collective-permute-start.3) | collective-permute-done | bytes 131104 | tf_op jit(solution)/shard_map/ppermute | solution.py:406
  46.6 0.0 copy-start.5
  46.6 0.0 copy-done.4
  46.6 0.6 %copy-done.5 = f32[16,16,128]{2,1,0:T(8,128)} copy-done((f32[16,16,128]{2,1,0:T(8,128)}, f32[16,16,128]{2,1,0:T(8,128)S(1)}, u32[]{:S(2)}) %copy-start.5) | copy-done | bytes 131096
  47.2 2.6 %merge.1 = f32[16,8,2048]{2,1,0:T(8,128)} custom-call(f32[168,16,128]{2,1,0:T(8,128)} %get-tuple-element.13.acc, f32[16,16,128]{2,1,0:T(8,128)} %copy-done.4, f32[16,16,128]{2,1,0:T(8,128)} %copy-done.5), custom_call_target="tpu_custom_call" | custom-call | tf_op jit(solution)/shard_map/merge/pallas_call | solution.py:437
  49.8 0.0 collective-permute-done.10.refs_1_
  49.8 0.0 copy-done
  49.8 0.0 copy-start.1
  49.8 0.8 %copy-done.1 = f32[16,8,1280]{2,1,0:T(8,128)} copy-done((f32[16,8,1280]{2,1,0:T(8,128)}, f32[16,8,1280]{2,1,0:T(8,128)S(1)}, u32[]{:S(2)}) %copy-start.1) | copy-done | bytes 655384
  50.7 7.7 %relax.1 = f32[64,4096]{1,0:T(8,128)} custom-call(f32[16,8,1280]{2,1,0:T(8,128)} %copy-done, f32[16,8,1280]{2,1,0:T(8,128)} %copy-done.1), custom_call_target="tpu_custom_call" | custom-call | tf_op jit(solution)/shard_map/relax/pallas_call | solution.py:449
  (6 shorter events, 0.1 us)
Async XLA Ops:
  2.7 5.9 %collective-permute-start = (f32[16,16,128]{2,1,0:T(8,128)}, f32[16,16,128]{2,1,0:T(8,128)S(1)}, u32[]{:S(2)}, u32[]{:S(2)}) collective-permute-start(f32[16,16,128]{2,1,0:T(8,128)} %get-tuple-element.10), channel_id=1, source_target_pairs={{0,4},{4,0},{1,5},{5,1},{2,6},{6,2},{3,7},{7,3},{8,12},{12,8},{9,1... | collective-permute-start | bytes 393224 | tf_op jit(solution)/shard_map/ppermute | solution.py:406
  4.2 8.0 %collective-permute-start.1 = (f32[16,16,128]{2,1,0:T(8,128)}, f32[16,16,128]{2,1,0:T(8,128)S(1)}, u32[]{:S(2)}, u32[]{:S(2)}) collective-permute-start(f32[16,16,128]{2,1,0:T(8,128)} %get-tuple-element.11), channel_id=1, source_target_pairs={{4,8},{8,4},{5,9},{9,5},{6,10},{10,6},{7,11},{11,7},{12,16},{16,12... | collective-permute-start | bytes 393224 | tf_op jit(solution)/shard_map/ppermute | solution.py:406
  8.6 3.6 %copy-start.2 = (f32[16,16,128]{2,1,0:T(8,128)}, f32[16,16,128]{2,1,0:T(8,128)S(1)}, u32[]{:S(2)}) copy-start(f32[16,16,128]{2,1,0:T(8,128)S(1)} %collective-permute-done.pair_a) | copy-start | bytes 393220
  12.1 0.7 %copy-start.3 = (f32[16,16,128]{2,1,0:T(8,128)}, f32[16,16,128]{2,1,0:T(8,128)S(1)}, u32[]{:S(2)}) copy-start(f32[16,16,128]{2,1,0:T(8,128)S(1)} %collective-permute-done.1.pair_b) | copy-start | bytes 393220
  19.1 18.3 %copy-start.7 = (f32[16,16,128]{2,1,0:T(8,128)S(1)}, f32[16,16,128]{2,1,0:T(8,128)}, u32[]{:S(2)}) copy-start(f32[16,16,128]{2,1,0:T(8,128)} %get-tuple-element.14) | copy-start | bytes 393220
  19.1 19.2 %copy-start.6 = (f32[16,16,128]{2,1,0:T(8,128)S(1)}, f32[16,16,128]{2,1,0:T(8,128)}, u32[]{:S(2)}) copy-start(f32[16,16,128]{2,1,0:T(8,128)} %get-tuple-element.15) | copy-start | bytes 393220
  19.1 5.0 %collective-permute-start.6 = (f32[1,8,1280]{2,1,0:T(8,128)}, f32[1,8,1280]{2,1,0:T(8,128)S(1)}, u32[]{:S(2)}, u32[]{:S(2)}) collective-permute-start(f32[1,8,1280]{2,1,0:T(8,128)} %bitcast.3), channel_id=1, source_target_pairs={{0,24},{1,25},{2,26},{3,27},{4,28},{5,29},{6,30},{7,31},{8,16},{9,... | collective-permute-start | bytes 122888 | tf_op jit(solution)/shard_map/ppermute | solution.py:471
  20.7 5.1 %collective-permute-start.5 = (f32[1,8,1280]{2,1,0:T(8,128)}, f32[1,8,1280]{2,1,0:T(8,128)S(1)}, u32[]{:S(2)}, u32[]{:S(2)}) collective-permute-start(f32[1,8,1280]{2,1,0:T(8,128)} %bitcast.4), channel_id=1, source_target_pairs={{0,8},{1,9},{2,10},{3,11},{4,12},{5,13},{6,14},{7,15},{8,0},{9,1},... | collective-permute-start | bytes 122888 | tf_op jit(solution)/shard_map/ppermute | solution.py:471
  23.2 5.1 %collective-permute-start.4 = (f32[1,8,1280]{2,1,0:T(8,128)}, f32[1,8,1280]{2,1,0:T(8,128)S(1)}, u32[]{:S(2)}, u32[]{:S(2)}) collective-permute-start(f32[1,8,1280]{2,1,0:T(8,128)} %bitcast.5), channel_id=1, source_target_pairs={{0,16},{1,17},{2,18},{3,19},{4,20},{5,21},{6,22},{7,23},{8,24},{9,... | collective-permute-start | bytes 122888 | tf_op jit(solution)/shard_map/ppermute | solution.py:471
  29.1 8.2 %collective-permute-start.9 = (f32[4,8,1280]{2,1,0:T(8,128)S(1)}, f32[4,8,1280]{2,1,0:T(8,128)S(1)}, u32[]{:S(2)}, u32[]{:S(2)}) collective-permute-start(f32[4,8,1280]{2,1,0:T(8,128)S(1)} %pad_maximum_fusion), channel_id=1, source_target_pairs={{0,6},{1,7},{2,4},{3,5},{4,2},{5,3},{6,0},{7,1},{8,14},{9,15},{10,... | collective-permute-start | bytes 491528 | tf_op jit(solution)/shard_map/ppermute | solution.py:471
  29.2 8.1 %collective-permute-start.8 = (f32[4,8,1280]{2,1,0:T(8,128)S(1)}, f32[4,8,1280]{2,1,0:T(8,128)S(1)}, u32[]{:S(2)}, u32[]{:S(2)}) collective-permute-start(f32[4,8,1280]{2,1,0:T(8,128)S(1)} %pad_maximum_fusion), channel_id=1, source_target_pairs={{0,2},{1,3},{2,0},{3,1},{4,6},{5,7},{6,4},{7,5},{8,10},{9,11},{10,... | collective-permute-start | bytes 491528 | tf_op jit(solution)/shard_map/ppermute | solution.py:471
  30.8 6.5 %collective-permute-start.7 = (f32[4,8,1280]{2,1,0:T(8,128)S(1)}, f32[4,8,1280]{2,1,0:T(8,128)S(1)}, u32[]{:S(2)}, u32[]{:S(2)}) collective-permute-start(f32[4,8,1280]{2,1,0:T(8,128)S(1)} %pad_maximum_fusion), channel_id=1, source_target_pairs={{0,4},{1,5},{2,6},{3,7},{4,0},{5,1},{6,2},{7,3},{8,12},{9,13},{10,... | collective-permute-start | bytes 491528 | tf_op jit(solution)/shard_map/ppermute | solution.py:471
  37.3 12.5 %copy-start = (f32[16,8,1280]{2,1,0:T(8,128)}, f32[16,8,1280]{2,1,0:T(8,128)S(1)}, u32[]{:S(2)}) copy-start(f32[16,8,1280]{2,1,0:T(8,128)S(1)} %constant_dynamic-update-slice_fusion.refs_0_) | copy-start | bytes 1966084
  37.3 12.5 %collective-permute-start.10 = (f32[16,8,1280]{2,1,0:T(8,128)S(1)}, f32[16,8,1280]{2,1,0:T(8,128)S(1)}, u32[]{:S(2)}, u32[]{:S(2)}) collective-permute-start(f32[16,8,1280]{2,1,0:T(8,128)S(1)} %constant_dynamic-update-slice_fusion.refs_0_), channel_id=1, source_target_pairs={{0,1},{1,0},{2,3},{3,2},{4,5},{5,4},{6,7},{7,6},{8,9},{9,8},{10,11... | collective-permute-start | bytes 1966088 | tf_op jit(solution)/shard_map/ppermute | solution.py:471
  37.4 5.9 %collective-permute-start.2 = (f32[16,16,128]{2,1,0:T(8,128)S(1)}, f32[16,16,128]{2,1,0:T(8,128)S(1)}, u32[]{:S(2)}, u32[]{:S(2)}) collective-permute-start(f32[16,16,128]{2,1,0:T(8,128)S(1)} %copy-done.7), channel_id=1, source_target_pairs={{0,4},{4,0},{1,5},{5,1},{2,6},{6,2},{3,7},{7,3},{8,12},{12,8},{9,1... | collective-permute-start | bytes 393224 | tf_op jit(solution)/shard_map/ppermute | solution.py:406
  38.2 8.3 %collective-permute-start.3 = (f32[16,16,128]{2,1,0:T(8,128)S(1)}, f32[16,16,128]{2,1,0:T(8,128)S(1)}, u32[]{:S(2)}, u32[]{:S(2)}) collective-permute-start(f32[16,16,128]{2,1,0:T(8,128)S(1)} %copy-done.6), channel_id=1, source_target_pairs={{4,8},{8,4},{5,9},{9,5},{6,10},{10,6},{7,11},{11,7},{12,16},{16,12... | collective-permute-start | bytes 393224 | tf_op jit(solution)/shard_map/ppermute | solution.py:406
  43.3 3.2 %copy-start.4 = (f32[16,16,128]{2,1,0:T(8,128)}, f32[16,16,128]{2,1,0:T(8,128)S(1)}, u32[]{:S(2)}) copy-start(f32[16,16,128]{2,1,0:T(8,128)S(1)} %collective-permute-done.2.pair_a) | copy-start | bytes 393220
  46.6 0.7 %copy-start.5 = (f32[16,16,128]{2,1,0:T(8,128)}, f32[16,16,128]{2,1,0:T(8,128)S(1)}, u32[]{:S(2)}) copy-start(f32[16,16,128]{2,1,0:T(8,128)S(1)} %collective-permute-done.3.pair_b) | copy-start | bytes 393220
  49.8 0.8 %copy-start.1 = (f32[16,8,1280]{2,1,0:T(8,128)}, f32[16,8,1280]{2,1,0:T(8,128)S(1)}, u32[]{:S(2)}) copy-start(f32[16,8,1280]{2,1,0:T(8,128)S(1)} %collective-permute-done.10.refs_1_) | copy-start | bytes 1966084

commit v2 on v1

--- a/solution.py
+++ b/solution.py
@@ -17,6 +17,11 @@
 F32 = jnp.float32
 VMEM = pl.BlockSpec(memory_space=pltpu.VMEM)
 SMEM = pl.BlockSpec(memory_space=pltpu.SMEM)
+
+
+def room(mib):
+    return pltpu.CompilerParams(vmem_limit_bytes=mib * 2**20)
+
 
 drag_rate = 0.5
 evap_rate = 0.08
@@ -291,37 +296,13 @@
 
 
 def relax_kernel(masks, columns, *refs):
-    *parts, out, source, one, two = refs
+    *parts, out, source, ends, one, two = refs
     planes = parts[0].shape[1]
     cross_count = lax.axis_size("cross")
-    slab_count = lax.axis_size("slab")
     me = lax.axis_index("slab") * cross_count + lax.axis_index("cross")
     edge = COARSE
     slabs = edge // planes
-    pieces = [(mask, part, i) for part, part_masks in zip(parts, masks) for i, mask in enumerate(part_masks)]
-
-    def place(mask):
-        owner = lax.bitwise_xor(me, mask)
-        slab = owner // cross_count
-        at = pl.multiple_of(lax.rem(owner, cross_count) * columns, LANES)
-        return slab, at
-
-    for mask, part, i in pieces:
-        slab, at = place(mask)
-        source[slab, :, pl.ds(at, columns)] = part[i, :, :columns]
     quarter = columns // 4
-    for mask, part, i in pieces:
-        slab, at = place(mask)
-        for h, target, line in ((0, slab - 1, planes - 1), (1, slab + 1, 0)):
-            @pl.when((target >= 0) & (target < slab_count))
-            def _():
-                for j in range(4):
-                    here = pl.ds(pl.multiple_of(at + j * quarter, LANES), quarter)
-                    r = 4 * h + j
-                    source[target, line : line + 1, here] = (
-                        source[target, line : line + 1, here] + part[i, r : r + 1, columns:]
-                    )
-
     squared = edge * edge
     width = squared // LANES
     lane = lax.broadcasted_iota(jnp.int32, (8, LANES), 1)
@@ -329,48 +310,72 @@
     inside = lax.rem(lane, edge)
     sixth = 1.0 / 6.0
 
+    for i in (0, slabs + 1):
+        ends[i] = jnp.zeros(ends.shape[1:], F32)
+        one[i] = jnp.zeros(one.shape[1:], F32)
+        two[i] = jnp.zeros(two.shape[1:], F32)
+    for part, part_masks in zip(parts, masks):
+        for i, mask in enumerate(part_masks):
+            owner = lax.bitwise_xor(me, mask)
+            slab = owner // cross_count
+            cross = lax.rem(owner, cross_count)
+            at = pl.ds(pl.multiple_of(cross * columns, LANES), columns)
+            source[slab, :, at] = part[i, :, :columns]
+            at = pl.ds(pl.multiple_of(cross * quarter, LANES), quarter)
+            ends[slab + 1, :, at] = part[i, :, columns:]
+
     def at_lanes(v):
         return pl.ds(v * LANES, LANES)
 
-    def sweep(src, dst):
+    def begin(s, _):
+        for v in range(width):
+            j, l = v * LANES % columns // quarter, v * LANES % quarter
+            here = pl.ds(v * LANES // columns * quarter + l, LANES)
+            above = jnp.broadcast_to(ends[s + 2, j : j + 1, here], (8, LANES))
+            under = jnp.broadcast_to(ends[s, 4 + j : 5 + j, here], (8, LANES))
+            x = source[s, :, at_lanes(v)]
+            x = x + jnp.where(row == 7, above, jnp.where(row == 0, under, 0.0))
+            source[s, :, at_lanes(v)] = x
+            one[s + 1, :, at_lanes(v)] = x * sixth
+        return 0
+
+    lax.fori_loop(0, slabs, begin, 0)
+
+    def sweep(src, put):
         def run(s, _):
-            up = jnp.minimum(s + 1, slabs - 1)
-            dn = jnp.maximum(s - 1, 0)
-            has_up = s < slabs - 1
-            has_dn = s > 0
-            values = [src[s, :, at_lanes(v)] for v in range(width)]
-            turned = [pltpu.roll(x, edge, axis=1) for x in values]
+            nothing = jnp.zeros((8, LANES), F32)
+            x, turned = nothing, nothing
+            after = src[s + 1, :, at_lanes(0)]
+            turned_after = pltpu.roll(after, edge, axis=1)
             for v in range(width):
-                x = values[v]
-                above = src[up, 0:1, at_lanes(v)]
-                under = src[dn, 7:8, at_lanes(v)]
-                above = jnp.where(has_up, above, 0.0)
-                under = jnp.where(has_dn, under, 0.0)
-                total = jnp.where(row == 7, above, pltpu.roll(x, 7, axis=0))
+                turned_before = turned
+                x, turned = after, turned_after
+                if v < width - 1:
+                    after = src[s + 1, :, at_lanes(v + 1)]
+                    turned_after = pltpu.roll(after, edge, axis=1)
+                else:
+                    turned_after = nothing
+                above = jnp.broadcast_to(src[s + 2, 0:1, at_lanes(v)], (8, LANES))
+                under = jnp.broadcast_to(src[s, 7:8, at_lanes(v)], (8, LANES))
+                total = source[s, :, at_lanes(v)] + turned
+                total = total + jnp.where(lane < edge, turned_before, turned_after)
+                total = total + jnp.where(row == 7, above, pltpu.roll(x, 7, axis=0))
                 total = total + jnp.where(row == 0, under, pltpu.roll(x, 1, axis=0))
-                left = turned[v - 1] if v > 0 else jnp.zeros_like(x)
-                right = turned[v + 1] if v < width - 1 else jnp.zeros_like(x)
-                total = total + turned[v] + jnp.where(lane < edge, left, right)
                 total = total + jnp.where(inside < edge - 1, pltpu.roll(x, LANES - 1, axis=1), 0.0)
                 total = total + jnp.where(inside > 0, pltpu.roll(x, 1, axis=1), 0.0)
-                dst(s, v, (total + source[s, :, at_lanes(v)]) * sixth)
+                put(s, v, total * sixth)
             return 0
 
         lax.fori_loop(0, slabs, run, 0)
 
     def into(ref):
         def put(s, v, x):
-            ref[s, :, at_lanes(v)] = x
+            ref[s + 1, :, at_lanes(v)] = x
         return put
 
     def final(s, v, x):
         out[pl.ds(pl.multiple_of(s * 8, 8), 8), at_lanes(v)] = x
 
-    def begin(s, _):
-        one[s] = source[s] * sixth
-        return 0
-
-    lax.fori_loop(0, slabs, begin, 0)
     buffers = (one, two)
     for step in range(1, SWEEPS):
         src = buffers[(step - 1) % 2]
@@ -407,13 +412,13 @@
 
     plane = jax.ShapeDtypeStruct((per_plane, fields, LANES), F32)
     edge_a, edge_b = pl.pallas_call(
-        edges_kernel, out_shape=(plane, plane), in_specs=[VMEM], out_specs=(VMEM, VMEM), name="edges"
+        edges_kernel, out_shape=(plane, plane), in_specs=[VMEM], out_specs=(VMEM, VMEM), name="edges", compiler_params=room(8)
     )(gas_state)
     got_a, got_b = swap(edge_a, edge_b)
     tiles = pl.pallas_call(
         tiles_kernel,
         out_shape=jax.ShapeDtypeStruct((inner, fields, LANES), F32),
-        in_specs=[VMEM], out_specs=VMEM, name="tiles",
+        in_specs=[VMEM], out_specs=VMEM, name="tiles", compiler_params=room(8),
     )(gas_state)
     total_tiles = inner + 2 * per_plane + WIDE
     parcel_next, acc, send_a, send_b, coarse = pl.pallas_call(
@@ -428,7 +433,7 @@
         in_specs=[SMEM, SMEM, SMEM] + [VMEM] * 6,
         out_specs=(VMEM,) * 5,
         scratch_shapes=[pltpu.VMEM((total_tiles, fields, LANES), F32)],
-        name="parcels",
+        name="parcels", compiler_params=room(16),
     )(
         fine_cell, block_counts, surface_steam_factor, fine_cell.reshape(blocks, LANES),
         tiles, got_a, got_b, parcel_record, condensed_shares,
@@ -437,7 +442,7 @@
     fine_source = pl.pallas_call(
         merge_kernel,
         out_shape=jax.ShapeDtypeStruct(gas_state.shape, F32),
-        in_specs=[VMEM] * 3, out_specs=VMEM, name="merge",
+        in_specs=[VMEM] * 3, out_specs=VMEM, name="merge", compiler_params=room(12),
     )(acc, back_a, back_b)
 
     own_planes = planes
@@ -445,12 +450,19 @@
         coarse, own_planes = shared_planes(coarse, columns, planes, fine_per_coarse)
     parts, masks = gather_all(coarse, device_count)
     if fine_per_coarse == 1:
-        scratch = pltpu.VMEM((COARSE // planes, planes, squared), F32)
+        slabs = COARSE // planes
+        padded = pltpu.VMEM((slabs + 2, planes, squared), F32)
         correction = pl.pallas_call(
             functools.partial(relax_kernel, masks, columns),
             out_shape=jax.ShapeDtypeStruct((COARSE, squared), F32),
             in_specs=[VMEM] * len(parts), out_specs=VMEM,
-            scratch_shapes=[scratch] * 3, name="relax",
+            scratch_shapes=[
+                pltpu.VMEM((slabs, planes, squared), F32),
+                pltpu.VMEM((slabs + 2, 8, squared // 4), F32),
+                padded,
+                padded,
+            ],
+            name="relax", compiler_params=room(16),
         )(*parts)
     else:
         correction = relax_plain(arrange(parts, masks, columns, own_planes, fine_per_coarse, planes))

time: 58.8 us -> 49.9 us (0.85)
  Pallas kernels: 21.1 us -> 12.4 us
  waiting for transfers between devices: 18.1 us -> 20.7 us
  local copies, waits for them, and re-layouts: 3.06 us -> 1.29 us
  other arithmetic: 0.79 us -> 0.01 us
    pallas_call x1, Pallas kernels: 2.46 us -> 0.26 us  [body(): pl.pallas_call(tiles_kernel, out_shape=jax.ShapeDtypeStruct((inner, field...]
    pallas_call x1, Pallas kernels: 7.69 us -> 5.64 us  [body(): pl.pallas_call(functools.partial(relax_kernel, masks, columns), out_shape...]
    ppermute x4, waiting for transfers between devices: 9.28 us -> 11.3 us  [swap(): return (lax.ppermute(a, AXES, pairs_a), lax.ppermute(b, AXES, pairs_b))]
    pallas_call x1, Pallas kernels: 2.07 us -> 0.15 us  [body(): pl.pallas_call(edges_kernel, out_shape=(plane, plane), in_specs=[VMEM], o...]
    unnamed x22 -> x18, local copies, waits for them, and re-layouts: 3.05 us -> 1.28 us
    pallas_call x1, Pallas kernels: 2.61 us -> 1.19 us  [body(): pl.pallas_call(merge_kernel, out_shape=jax.ShapeDtypeStruct(gas_state.sha...]
    pallas_call x1, Pallas kernels: 6.28 us -> 5.16 us  [body(): pl.pallas_call(parcels_kernel, out_shape=(jax.ShapeDtypeStruct(parcel_rec...]
    concatenate x1, other arithmetic: 0.79 us -> 0.01 us  [gather_all(): held = jnp.concatenate([held] + arrived, axis=0)]
  transfers between devices with their start and end apart: 11 -> 11, of which waited for: 6 -> 7; matrix products, arithmetic and copies ran while one was open for 2% -> 0% of each run, Pallas kernels for 9% -> 3%
where the time goes in v2:
time: 49.9 us; the launch traced here: 49.8 us
  waiting for transfers between devices  20.7 us (41%)
  starting transfers between devices  14.6 us (29%)
  Pallas kernels  12.4 us (25%)
  local copies, waits for them, and re-layouts  1.29 us (3%)
  between operations  0.78 us (2%)
    ppermute x4, waiting for transfers between devices, swap(): return (lax.ppermute(a, AXES, pairs_a), lax.ppermute(b, AXES, pairs_b))  11.3 us
    ppermute x7, waiting for transfers between devices, send(): lax.ppermute(held, AXES, [(i, i ^ mask) for i in range(device_count)])  9.47 us
    ppermute x7, starting transfers between devices, send(): lax.ppermute(held, AXES, [(i, i ^ mask) for i in range(device_count)])  7.67 us
    ppermute x4, starting transfers between devices, swap(): return (lax.ppermute(a, AXES, pairs_a), lax.ppermute(b, AXES, pairs_b))  6.89 us
    pallas_call x1, Pallas kernels, body(): pl.pallas_call(functools.partial(relax_kernel, masks, columns), out_shape...  5.64 us
    pallas_call x1, Pallas kernels, body(): pl.pallas_call(parcels_kernel, out_shape=(jax.ShapeDtypeStruct(parcel_rec...  5.16 us
    unnamed x18, local copies, waits for them, and re-layouts  1.28 us
    pallas_call x1, Pallas kernels, body(): pl.pallas_call(merge_kernel, out_shape=jax.ShapeDtypeStruct(gas_state.sha...  1.19 us
  transfers between devices with their start and end apart: 11, of which 7 were waited for; matrix products, arithmetic and copies ran while one was open for 0% of the time, Pallas kernels for 3%

profile of v2, /device:TPU:8, one launch (start us, length us, event | category | flops | bytes accessed | tf_op | source)
XLA Modules:
  0.0 49.8 jit_solution(12840415655934533345)
XLA Ops:
  0.6 0.0 copy-start
  0.6 1.2 %copy-done = f32[16,8,2048]{2,1,0:T(8,128)S(1)} copy-done((f32[16,8,2048]{2,1,0:T(8,128)S(1)}, f32[16,8,2048]{2,1,0:T(8,128)}, u32[]{:S(2)}) %copy-start) | copy-done | bytes 1048600
  1.9 0.0 copy-start.1
  1.9 0.0 copy-start.2
  1.9 0.0 copy-start.3
  1.9 0.0 copy-start.4
  1.9 0.0 copy-start.5
  1.9 0.1 edges.1
  2.0 1.6 %collective-permute-start = (f32[16,16,128]{2,1,0:T(8,128)S(1)}, f32[16,16,128]{2,1,0:T(8,128)S(1)}, u32[]{:S(2)}, u32[]{:S(2)}) collective-permute-start(f32[16,16,128]{2,1,0:T(8,128)S(1)} %get-tuple-element.10), channel_id=1, source_target_pairs={{0,4},{4,0},{1,5},{5,1},{2,6},{6,2},{3,7},{7,3},{8,12},{12,8},{9,1... | collective-permute-start | bytes 393224 | tf_op jit(solution)/shard_map/ppermute | solution.py:411
  3.6 1.9 %collective-permute-start.1 = (f32[16,16,128]{2,1,0:T(8,128)S(1)}, f32[16,16,128]{2,1,0:T(8,128)S(1)}, u32[]{:S(2)}, u32[]{:S(2)}) collective-permute-start(f32[16,16,128]{2,1,0:T(8,128)S(1)} %get-tuple-element.11), channel_id=1, source_target_pairs={{4,8},{8,4},{5,9},{9,5},{6,10},{10,6},{7,11},{11,7},{12,16},{16,12... | collective-permute-start | bytes 393224 | tf_op jit(solution)/shard_map/ppermute | solution.py:411
  5.5 0.3 tiles.1
  5.8 1.6 %collective-permute-done.pair_a = f32[16,16,128]{2,1,0:T(8,128)S(1)} collective-permute-done((f32[16,16,128]{2,1,0:T(8,128)S(1)}, f32[16,16,128]{2,1,0:T(8,128)S(1)}, u32[]{:S(2)}, u32[]{:S(2)}) %collective-permute-start) | collective-permute-done | bytes 131104 | tf_op jit(solution)/shard_map/ppermute | solution.py:411
  7.3 4.0 %collective-permute-done.1.pair_b = f32[16,16,128]{2,1,0:T(8,128)S(1)} collective-permute-done((f32[16,16,128]{2,1,0:T(8,128)S(1)}, f32[16,16,128]{2,1,0:T(8,128)S(1)}, u32[]{:S(2)}, u32[]{:S(2)}) %collective-permute-start.1) | collective-permute-done | bytes 131104 | tf_op jit(solution)/shard_map/ppermute | solution.py:411
  11.3 0.0 copy-done.1
  11.3 0.0 copy-done.2
  11.3 0.0 copy-done.3
  11.3 0.0 copy-done.4
  11.4 0.0 copy-done.5
  11.4 5.2 %parcels.1 = (f32[5,4096]{1,0:T(8,128)}, f32[168,16,128]{2,1,0:T(8,128)S(1)}, f32[16,16,128]{2,1,0:T(8,128)S(1)}, f32[16,16,128]{2,1,0:T(8,128)S(1)}, f32[8,1280]{1,0:T(8,128)S(1)}) custom-call(s32[4096]{0:T(1024)S(1)} %copy-done.3, s32[32]{0:T(128)S(1)} %copy-done.4, f32[12]{0:T(128)S(1)} %copy-done.5, s32[32,128]{1,0:T(8,128)S(1)} %bitcast.7, ...), custom_call_target="tpu_custom_call" | custom-call | tf_op jit(solution)/shard_map/parcels/pallas_call | solution.py:424
  16.5 1.6 %collective-permute-start.6 = (f32[1,8,1280]{2,1,0:T(8,128)S(1)}, f32[1,8,1280]{2,1,0:T(8,128)S(1)}, u32[]{:S(2)}, u32[]{:S(2)}) collective-permute-start(f32[1,8,1280]{2,1,0:T(8,128)S(1)} %bitcast.3), channel_id=1, source_target_pairs={{0,24},{1,25},{2,26},{3,27},{4,28},{5,29},{6,30},{7,31},{8,16},{9,... | collective-permute-start | bytes 122888 | tf_op jit(solution)/shard_map/ppermute | solution.py:483
  18.1 2.5 %collective-permute-start.5 = (f32[1,8,1280]{2,1,0:T(8,128)S(1)}, f32[1,8,1280]{2,1,0:T(8,128)S(1)}, u32[]{:S(2)}, u32[]{:S(2)}) collective-permute-start(f32[1,8,1280]{2,1,0:T(8,128)S(1)} %bitcast.4), channel_id=1, source_target_pairs={{0,8},{1,9},{2,10},{3,11},{4,12},{5,13},{6,14},{7,15},{8,0},{9,1},... | collective-permute-start | bytes 122888 | tf_op jit(solution)/shard_map/ppermute | solution.py:483
  20.6 0.0 collective-permute-start.4
  20.6 0.0 collective-permute-done.6
  20.6 2.4 %collective-permute-done.5 = f32[1,8,1280]{2,1,0:T(8,128)S(1)} collective-permute-done((f32[1,8,1280]{2,1,0:T(8,128)S(1)}, f32[1,8,1280]{2,1,0:T(8,128)S(1)}, u32[]{:S(2)}, u32[]{:S(2)}) %collective-permute-start.5) | collective-permute-done | bytes 40992 | tf_op jit(solution)/shard_map/ppermute | solution.py:483
  23.0 2.5 %collective-permute-done.4 = f32[1,8,1280]{2,1,0:T(8,128)S(1)} collective-permute-done((f32[1,8,1280]{2,1,0:T(8,128)S(1)}, f32[1,8,1280]{2,1,0:T(8,128)S(1)}, u32[]{:S(2)}, u32[]{:S(2)}) %collective-permute-start.4) | collective-permute-done | bytes 40992 | tf_op jit(solution)/shard_map/ppermute | solution.py:483
  25.5 0.1 collective-permute-start.9
  25.6 1.6 %collective-permute-start.8 = (f32[4,8,1280]{2,1,0:T(8,128)S(1)}, f32[4,8,1280]{2,1,0:T(8,128)S(1)}, u32[]{:S(2)}, u32[]{:S(2)}) collective-permute-start(f32[4,8,1280]{2,1,0:T(8,128)S(1)} %pad_maximum_fusion), channel_id=1, source_target_pairs={{0,2},{1,3},{2,0},{3,1},{4,6},{5,7},{6,4},{7,5},{8,10},{9,11},{10,... | collective-permute-start | bytes 491528 | tf_op jit(solution)/shard_map/ppermute | solution.py:483
  27.2 1.9 %collective-permute-start.7 = (f32[4,8,1280]{2,1,0:T(8,128)S(1)}, f32[4,8,1280]{2,1,0:T(8,128)S(1)}, u32[]{:S(2)}, u32[]{:S(2)}) collective-permute-start(f32[4,8,1280]{2,1,0:T(8,128)S(1)} %pad_maximum_fusion), channel_id=1, source_target_pairs={{0,4},{1,5},{2,6},{3,7},{4,0},{5,1},{6,2},{7,3},{8,12},{9,13},{10,... | collective-permute-start | bytes 491528 | tf_op jit(solution)/shard_map/ppermute | solution.py:483
  29.1 4.6 %collective-permute-done.7 = f32[4,8,1280]{2,1,0:T(8,128)S(1)} collective-permute-done((f32[4,8,1280]{2,1,0:T(8,128)S(1)}, f32[4,8,1280]{2,1,0:T(8,128)S(1)}, u32[]{:S(2)}, u32[]{:S(2)}) %collective-permute-start.7) | collective-permute-done | bytes 163872 | tf_op jit(solution)/shard_map/ppermute | solution.py:483
  33.7 0.0 collective-permute-done.8
  33.7 0.0 collective-permute-done.9
  33.7 0.1 collective-permute-start.10
  33.8 0.8 %collective-permute-start.2 = (f32[16,16,128]{2,1,0:T(8,128)S(1)}, f32[16,16,128]{2,1,0:T(8,128)S(1)}, u32[]{:S(2)}, u32[]{:S(2)}) collective-permute-start(f32[16,16,128]{2,1,0:T(8,128)S(1)} %get-tuple-element.14), channel_id=1, source_target_pairs={{0,4},{4,0},{1,5},{5,1},{2,6},{6,2},{3,7},{7,3},{8,12},{12,8},{9,1... | collective-permute-start | bytes 393224 | tf_op jit(solution)/shard_map/ppermute | solution.py:411
  34.6 2.6 %collective-permute-start.3 = (f32[16,16,128]{2,1,0:T(8,128)S(1)}, f32[16,16,128]{2,1,0:T(8,128)S(1)}, u32[]{:S(2)}, u32[]{:S(2)}) collective-permute-start(f32[16,16,128]{2,1,0:T(8,128)S(1)} %get-tuple-element.15), channel_id=1, source_target_pairs={{4,8},{8,4},{5,9},{9,5},{6,10},{10,6},{7,11},{11,7},{12,16},{16,12... | collective-permute-start | bytes 393224 | tf_op jit(solution)/shard_map/ppermute | solution.py:411
  37.2 2.5 %collective-permute-done.2.pair_a = f32[16,16,128]{2,1,0:T(8,128)S(1)} collective-permute-done((f32[16,16,128]{2,1,0:T(8,128)S(1)}, f32[16,16,128]{2,1,0:T(8,128)S(1)}, u32[]{:S(2)}, u32[]{:S(2)}) %collective-permute-start.2) | collective-permute-done | bytes 131104 | tf_op jit(solution)/shard_map/ppermute | solution.py:411
  39.7 3.2 %collective-permute-done.3.pair_b = f32[16,16,128]{2,1,0:T(8,128)S(1)} collective-permute-done((f32[16,16,128]{2,1,0:T(8,128)S(1)}, f32[16,16,128]{2,1,0:T(8,128)S(1)}, u32[]{:S(2)}, u32[]{:S(2)}) %collective-permute-start.3) | collective-permute-done | bytes 131104 | tf_op jit(solution)/shard_map/ppermute | solution.py:411
  42.9 1.2 %merge.1 = f32[16,8,2048]{2,1,0:T(8,128)} custom-call(f32[168,16,128]{2,1,0:T(8,128)S(1)} %get-tuple-element.13.acc, f32[16,16,128]{2,1,0:T(8,128)S(1)} %collective-permute-done.2.pair_a, f32[16,16,128]{2,1,0:T(8,128)S(1)} %collective-permute-done.3.pair_b), custom_call_target="tpu_custom_call" | custom-call | tf_op jit(solution)/shard_map/merge/pallas_call | solution.py:442
  44.1 0.0 collective-permute-done.10.refs_1_
  44.1 5.6 %relax.1 = f32[64,4096]{1,0:T(8,128)} custom-call(f32[16,8,1280]{2,1,0:T(8,128)S(1)} %constant_dynamic-update-slice_fusion.refs_0_, f32[16,8,1280]{2,1,0:T(8,128)S(1)} %collective-permute-done.10.refs_1_), custom_call_target="tpu_custom_call" | custom-call | tf_op jit(solution)/shard_map/relax/pallas_call | solution.py:455
  (8 shorter events, 0.1 us)
Async XLA Ops:
  0.6 1.2 %copy-start = (f32[16,8,2048]{2,1,0:T(8,128)S(1)}, f32[16,8,2048]{2,1,0:T(8,128)}, u32[]{:S(2)}) copy-start(f32[16,8,2048]{2,1,0:T(8,128)} %gas.3) | copy-start | bytes 3145732
  1.9 9.5 %copy-start.1 = (f32[12,4096]{1,0:T(8,128)S(1)}, f32[12,4096]{1,0:T(8,128)}, u32[]{:S(2)}) copy-start(f32[12,4096]{1,0:T(8,128)} %shares.1) | copy-start | bytes 589828
  1.9 9.5 %copy-start.2 = (f32[5,4096]{1,0:T(8,128)S(1)}, f32[5,4096]{1,0:T(8,128)}, u32[]{:S(2)}) copy-start(f32[5,4096]{1,0:T(8,128)} %record.1) | copy-start | bytes 245764
  1.9 9.5 %copy-start.3 = (s32[4096]{0:T(1024)S(1)}, s32[4096]{0:T(1024)}, u32[]{:S(2)}) copy-start(s32[4096]{0:T(1024)} %cell_s.1) | copy-start | bytes 49156
  1.9 9.5 %copy-start.4 = (s32[32]{0:T(128)S(1)}, s32[32]{0:T(128)}, u32[]{:S(2)}) copy-start(s32[32]{0:T(128)} %count_s.1) | copy-start | bytes 388
  1.9 9.5 %copy-start.5 = (f32[12]{0:T(128)S(1)}, f32[12]{0:T(128)}, u32[]{:S(2)}) copy-start(f32[12]{0:T(128)} %steam_s.1) | copy-start | bytes 148
  2.0 5.3 %collective-permute-start = (f32[16,16,128]{2,1,0:T(8,128)S(1)}, f32[16,16,128]{2,1,0:T(8,128)S(1)}, u32[]{:S(2)}, u32[]{:S(2)}) collective-permute-start(f32[16,16,128]{2,1,0:T(8,128)S(1)} %get-tuple-element.10), channel_id=1, source_target_pairs={{0,4},{4,0},{1,5},{5,1},{2,6},{6,2},{3,7},{7,3},{8,12},{12,8},{9,1... | collective-permute-start | bytes 393224 | tf_op jit(solution)/shard_map/ppermute | solution.py:411
  3.6 7.7 %collective-permute-start.1 = (f32[16,16,128]{2,1,0:T(8,128)S(1)}, f32[16,16,128]{2,1,0:T(8,128)S(1)}, u32[]{:S(2)}, u32[]{:S(2)}) collective-permute-start(f32[16,16,128]{2,1,0:T(8,128)S(1)} %get-tuple-element.11), channel_id=1, source_target_pairs={{4,8},{8,4},{5,9},{9,5},{6,10},{10,6},{7,11},{11,7},{12,16},{16,12... | collective-permute-start | bytes 393224 | tf_op jit(solution)/shard_map/ppermute | solution.py:411
  16.5 4.1 %collective-permute-start.6 = (f32[1,8,1280]{2,1,0:T(8,128)S(1)}, f32[1,8,1280]{2,1,0:T(8,128)S(1)}, u32[]{:S(2)}, u32[]{:S(2)}) collective-permute-start(f32[1,8,1280]{2,1,0:T(8,128)S(1)} %bitcast.3), channel_id=1, source_target_pairs={{0,24},{1,25},{2,26},{3,27},{4,28},{5,29},{6,30},{7,31},{8,16},{9,... | collective-permute-start | bytes 122888 | tf_op jit(solution)/shard_map/ppermute | solution.py:483
  18.1 4.9 %collective-permute-start.5 = (f32[1,8,1280]{2,1,0:T(8,128)S(1)}, f32[1,8,1280]{2,1,0:T(8,128)S(1)}, u32[]{:S(2)}, u32[]{:S(2)}) collective-permute-start(f32[1,8,1280]{2,1,0:T(8,128)S(1)} %bitcast.4), channel_id=1, source_target_pairs={{0,8},{1,9},{2,10},{3,11},{4,12},{5,13},{6,14},{7,15},{8,0},{9,1},... | collective-permute-start | bytes 122888 | tf_op jit(solution)/shard_map/ppermute | solution.py:483
  20.6 4.9 %collective-permute-start.4 = (f32[1,8,1280]{2,1,0:T(8,128)S(1)}, f32[1,8,1280]{2,1,0:T(8,128)S(1)}, u32[]{:S(2)}, u32[]{:S(2)}) collective-permute-start(f32[1,8,1280]{2,1,0:T(8,128)S(1)} %bitcast.5), channel_id=1, source_target_pairs={{0,16},{1,17},{2,18},{3,19},{4,20},{5,21},{6,22},{7,23},{8,24},{9,... | collective-permute-start | bytes 122888 | tf_op jit(solution)/shard_map/ppermute | solution.py:483
  25.5 8.2 %collective-permute-start.9 = (f32[4,8,1280]{2,1,0:T(8,128)S(1)}, f32[4,8,1280]{2,1,0:T(8,128)S(1)}, u32[]{:S(2)}, u32[]{:S(2)}) collective-permute-start(f32[4,8,1280]{2,1,0:T(8,128)S(1)} %pad_maximum_fusion), channel_id=1, source_target_pairs={{0,6},{1,7},{2,4},{3,5},{4,2},{5,3},{6,0},{7,1},{8,14},{9,15},{10,... | collective-permute-start | bytes 491528 | tf_op jit(solution)/shard_map/ppermute | solution.py:483
  25.6 8.1 %collective-permute-start.8 = (f32[4,8,1280]{2,1,0:T(8,128)S(1)}, f32[4,8,1280]{2,1,0:T(8,128)S(1)}, u32[]{:S(2)}, u32[]{:S(2)}) collective-permute-start(f32[4,8,1280]{2,1,0:T(8,128)S(1)} %pad_maximum_fusion), channel_id=1, source_target_pairs={{0,2},{1,3},{2,0},{3,1},{4,6},{5,7},{6,4},{7,5},{8,10},{9,11},{10,... | collective-permute-start | bytes 491528 | tf_op jit(solution)/shard_map/ppermute | solution.py:483
  27.2 6.5 %collective-permute-start.7 = (f32[4,8,1280]{2,1,0:T(8,128)S(1)}, f32[4,8,1280]{2,1,0:T(8,128)S(1)}, u32[]{:S(2)}, u32[]{:S(2)}) collective-permute-start(f32[4,8,1280]{2,1,0:T(8,128)S(1)} %pad_maximum_fusion), channel_id=1, source_target_pairs={{0,4},{1,5},{2,6},{3,7},{4,0},{5,1},{6,2},{7,3},{8,12},{9,13},{10,... | collective-permute-start | bytes 491528 | tf_op jit(solution)/shard_map/ppermute | solution.py:483
  33.7 10.4 %collective-permute-start.10 = (f32[16,8,1280]{2,1,0:T(8,128)S(1)}, f32[16,8,1280]{2,1,0:T(8,128)S(1)}, u32[]{:S(2)}, u32[]{:S(2)}) collective-permute-start(f32[16,8,1280]{2,1,0:T(8,128)S(1)} %constant_dynamic-update-slice_fusion.refs_0_), channel_id=1, source_target_pairs={{0,1},{1,0},{2,3},{3,2},{4,5},{5,4},{6,7},{7,6},{8,9},{9,8},{10,11... | collective-permute-start | bytes 1966088 | tf_op jit(solution)/shard_map/ppermute | solution.py:483
  33.8 5.9 %collective-permute-start.2 = (f32[16,16,128]{2,1,0:T(8,128)S(1)}, f32[16,16,128]{2,1,0:T(8,128)S(1)}, u32[]{:S(2)}, u32[]{:S(2)}) collective-permute-start(f32[16,16,128]{2,1,0:T(8,128)S(1)} %get-tuple-element.14), channel_id=1, source_target_pairs={{0,4},{4,0},{1,5},{5,1},{2,6},{6,2},{3,7},{7,3},{8,12},{12,8},{9,1... | collective-permute-start | bytes 393224 | tf_op jit(solution)/shard_map/ppermute | solution.py:411
  34.6 8.3 %collective-permute-start.3 = (f32[16,16,128]{2,1,0:T(8,128)S(1)}, f32[16,16,128]{2,1,0:T(8,128)S(1)}, u32[]{:S(2)}, u32[]{:S(2)}) collective-permute-start(f32[16,16,128]{2,1,0:T(8,128)S(1)} %get-tuple-element.15), channel_id=1, source_target_pairs={{4,8},{8,4},{5,9},{9,5},{6,10},{10,6},{7,11},{11,7},{12,16},{16,12... | collective-permute-start | bytes 393224 | tf_op jit(solution)/shard_map/ppermute | solution.py:411

commit v3 on v2

--- a/solution.py
+++ b/solution.py
@@ -6,6 +6,7 @@
 from jax.experimental import pallas as pl
 from jax.experimental.pallas import tpu as pltpu
 from jax.sharding import PartitionSpec as P
+
 
 BLOCK = 128
 COARSE = 64
@@ -17,6 +18,7 @@
 F32 = jnp.float32
 VMEM = pl.BlockSpec(memory_space=pltpu.VMEM)
 SMEM = pl.BlockSpec(memory_space=pltpu.SMEM)
+HBM = pl.BlockSpec(memory_space=pltpu.HBM)
 
 
 def room(mib):
@@ -39,24 +41,31 @@
     return lax.rem(lax.axis_index("slab"), 2) == 0
 
 
-def edges_kernel(gas, first_pair, second_pair):
+def load_kernel(
+    gas_in, record_in, shares_in, rows_in_hbm, count_in, steam_in,
+    gas, record, shares, rows, count, steam, first_pair, second_pair, sems,
+):
+    copies = [
+        pltpu.make_async_copy(source, target, sems.at[i])
+        for i, (source, target) in enumerate(
+            [
+                (gas_in, gas), (record_in, record), (shares_in, shares),
+                (rows_in_hbm, rows), (count_in, count), (steam_in, steam),
+            ]
+        )
+    ]
+    for copy in copies:
+        copy.start()
     fields, planes, cells = gas.shape
     even = plane_sides()
+    copies[0].wait()
     for k in range(cells // LANES):
         x = jnp.swapaxes(gas[:, :, k * LANES : (k + 1) * LANES], 0, 1)
         low, high = (rows_in(x[p : p + 1], fields - 4)[0] for p in (0, planes - 1))
         first_pair[k] = jnp.where(even, high, low)
         second_pair[k] = jnp.where(even, low, high)
-
-
-def tiles_kernel(gas, tiles):
-    fields, planes, cells = gas.shape
-    per_plane = cells // LANES
-    for k in range(per_plane):
-        x = jnp.swapaxes(gas[:, :, k * LANES : (k + 1) * LANES], 0, 1)
-        x = rows_in(x, fields - 4)
-        for p in range(planes):
-            tiles[p * per_plane + k] = x[p]
+    for copy in copies[1:]:
+        copy.wait()
 
 
 def advance_block(g, record, shares, steam, count):
@@ -126,48 +135,23 @@
         acc[first + j] = acc[first + j] + total
 
 
-def parcels_kernel(
-    cell_s, count_s, steam_s, cell_v, tiles, pair_a, pair_b, record, shares,
-    next_record, acc, send_a, send_b, coarse, gas,
-):
-    per_plane = pair_a.shape[0]
-    inner = tiles.shape[0]
+def run_groups(wanted, scalar_s, steam_s, cell_v, record, shares, next_record, acc, gas):
     blocks = cell_v.shape[0]
     species = shares.shape[0]
-    even = plane_sides()
-    below = jnp.where(even, 1, 0)
-    for k in range(per_plane):
-        a, b = pair_a[k], pair_b[k]
-        gas[k] = jnp.where(even, b, a)
-        gas[per_plane + inner + k] = jnp.where(even, a, b)
-
-    def fill(i, _):
-        for u in range(8):
-            gas[per_plane + i * 8 + u] = tiles[i * 8 + u]
-        return 0
-
-    lax.fori_loop(0, inner // 8, fill, 0)
-
-    def clear(i, _):
-        for u in range(8):
-            acc[i * 8 + u] = jnp.zeros(acc.shape[1:], F32)
-        return 0
-
-    lax.fori_loop(0, acc.shape[0] // 8, clear, 0)
-
     species_row = lax.broadcasted_iota(jnp.int32, (16, 1), 0)
     steam = jnp.zeros((16, 1), F32)
     for j in range(species):
         steam = jnp.where(species_row == j, steam_s[j], steam)
     steam = jnp.broadcast_to(steam, (16, LANES))
     spot = lax.broadcasted_iota(jnp.int32, (LANES, LANES), 0)
+    zero = jnp.zeros((8, LANES), F32)
 
     def prepare(b):
         cell = cell_v[pl.ds(b, 1), :]
         return cell // LANES, jnp.broadcast_to(lax.rem(cell, LANES), (8, LANES))
 
-    def pick(tile, tile_of, offset, first, j, old):
-        here = tile_of == first + j
+    def pick(tile, tile_of, offset, number, old):
+        here = tile_of == number
         return tuple(
             jnp.where(here, jnp.take_along_axis(tile[h * 8 : h * 8 + 8], offset, axis=1), o)
             for h, o in enumerate(old)
@@ -175,27 +159,25 @@
 
     def advance(b, g):
         at = pl.ds(pl.multiple_of(b * LANES, LANES), LANES)
-        terms, new = advance_block(g, record[:, at], shares[:, at], steam, count_s[b])
+        terms, new = advance_block(g, record[:, at], shares[:, at], steam, scalar_s[2 * blocks + b])
         next_record[:, at] = new
         return tuple(zip(*(three_parts(t) for t in terms)))
 
     def hot(offset):
         return jnp.where(spot == offset[0:1], 1.0, 0.0).astype(jnp.bfloat16)
 
-    zero = jnp.zeros((8, LANES), F32)
+    def span(b):
+        return scalar_s[b], scalar_s[blocks + b]
 
     def group(i, _):
         base = i * UNROLL
-        spans = []
-        for u in range(UNROLL):
-            first = cell_s[(base + u) * LANES] // LANES
-            last = cell_s[(base + u) * LANES + LANES - 1] // LANES
-            spans.append((first, last))
+        spans = [span(base + u) for u in range(UNROLL)]
+        chosen = wanted(spans[0][0], spans[-1][1])
         narrow = functools.reduce(
             jnp.logical_and, [last - first < WIDE for first, last in spans]
         )
 
-        @pl.when(narrow)
+        @pl.when(chosen & narrow)
         def _():
             staged = []
             for u in range(UNROLL):
@@ -203,7 +185,7 @@
                 tile_of, offset = prepare(base + u)
                 g = (zero, zero)
                 for j in range(WIDE):
-                    g = pick(gas[first + j], tile_of, offset, first, j, g)
+                    g = pick(gas[first + j], tile_of, offset, first + j, g)
                 staged.append((first, tile_of, offset, g))
             staged = [
                 (first, tile_of, offset, advance(base + u, g))
@@ -212,16 +194,15 @@
             for first, tile_of, offset, parts in staged:
                 deposit(parts, tile_of, first, hot(offset), WIDE, acc)
 
-        @pl.when(jnp.logical_not(narrow))
+        @pl.when(chosen & jnp.logical_not(narrow))
         def _():
             def one(u, _):
                 b = base + u
-                first = cell_s[b * LANES] // LANES
-                last = cell_s[b * LANES + LANES - 1] // LANES
+                first, last = span(b)
                 tile_of, offset = prepare(b)
 
                 def step(t, g):
-                    return pick(gas[t], tile_of, offset, t, 0, g)
+                    return pick(gas[t], tile_of, offset, t, g)
 
                 g = lax.fori_loop(first, last + 1, step, (zero, zero))
                 parts = advance(b, g)
@@ -239,6 +220,61 @@
 
     lax.fori_loop(0, blocks // UNROLL, group, 0)
 
+
+def inside_planes(per_plane, inner):
+    return lambda first, last: (first >= per_plane) & (last < per_plane + inner)
+
+
+def interior_kernel(
+    scalar_s, steam_s, cell_v, gas_state, record, shares, next_record, acc, gas
+):
+    fields, planes, cells = gas_state.shape
+    per_plane = cells // LANES
+    inner = planes * per_plane
+
+    def clear(i, _):
+        for u in range(8):
+            acc[i * 8 + u] = jnp.zeros(acc.shape[1:], F32)
+        return 0
+
+    lax.fori_loop(0, acc.shape[0] // 8, clear, 0)
+    for k in range(per_plane):
+        x = jnp.swapaxes(gas_state[:, :, k * LANES : (k + 1) * LANES], 0, 1)
+        x = rows_in(x, fields - 4)
+        for p in range(planes):
+            gas[(p + 1) * per_plane + k] = x[p]
+    run_groups(
+        inside_planes(per_plane, inner),
+        scalar_s, steam_s, cell_v, record, shares, next_record, acc, gas,
+    )
+
+
+def border_kernel(
+    scalar_s, steam_s, cell_v, pair_a, pair_b, record, shares,
+    record_before, acc_before, gas_before, next_record, acc, send_a, send_b, coarse, gas,
+):
+    per_plane = pair_a.shape[0]
+    inner = acc.shape[0] - 2 * per_plane - WIDE
+    next_record[...] = record_before[...]
+
+    def carry(i, _):
+        for u in range(8):
+            acc[i * 8 + u] = acc_before[i * 8 + u]
+            gas[i * 8 + u] = gas_before[i * 8 + u]
+        return 0
+
+    lax.fori_loop(0, acc.shape[0] // 8, carry, 0)
+    species = shares.shape[0]
+    even = plane_sides()
+    for k in range(per_plane):
+        a, b = pair_a[k], pair_b[k]
+        gas[k] = jnp.where(even, b, a)
+        gas[per_plane + inner + k] = jnp.where(even, a, b)
+    within = inside_planes(per_plane, inner)
+    run_groups(
+        lambda first, last: jnp.logical_not(within(first, last)),
+        scalar_s, steam_s, cell_v, record, shares, next_record, acc, gas,
+    )
     for k in range(per_plane):
         low, high = acc[k], acc[per_plane + inner + k]
         send_a[k] = jnp.where(even, high, low)
@@ -296,7 +332,7 @@
 
 
 def relax_kernel(masks, columns, *refs):
-    *parts, out, source, ends, one, two = refs
+    *parts, out, source, ends, one, two, done, sems = refs
     planes = parts[0].shape[1]
     cross_count = lax.axis_size("cross")
     me = lax.axis_index("slab") * cross_count + lax.axis_index("cross")
@@ -364,6 +400,8 @@
                 total = total + jnp.where(inside < edge - 1, pltpu.roll(x, LANES - 1, axis=1), 0.0)
                 total = total + jnp.where(inside > 0, pltpu.roll(x, 1, axis=1), 0.0)
                 put(s, v, total * sixth)
+            if put is final:
+                leave(s).start()
             return 0
 
         lax.fori_loop(0, slabs, run, 0)
@@ -371,15 +409,22 @@
     def into(ref):
         def put(s, v, x):
             ref[s + 1, :, at_lanes(v)] = x
+
         return put
 
     def final(s, v, x):
-        out[pl.ds(pl.multiple_of(s * 8, 8), 8), at_lanes(v)] = x
+        done[s, :, at_lanes(v)] = x
+
+    def leave(s):
+        rows = pl.ds(pl.multiple_of(s * 8, 8), 8)
+        return pltpu.make_async_copy(done.at[s], out.at[rows], sems.at[s])
 
     buffers = (one, two)
     for step in range(1, SWEEPS):
         src = buffers[(step - 1) % 2]
         sweep(src, final if step == SWEEPS - 1 else into(buffers[step % 2]))
+    for s in range(slabs):
+        leave(s).wait()
 
 
 def neighbour_pairs(slab_count, cross_count, start):
@@ -411,33 +456,47 @@
         return lax.ppermute(a, AXES, pairs_a), lax.ppermute(b, AXES, pairs_b)
 
     plane = jax.ShapeDtypeStruct((per_plane, fields, LANES), F32)
-    edge_a, edge_b = pl.pallas_call(
-        edges_kernel, out_shape=(plane, plane), in_specs=[VMEM], out_specs=(VMEM, VMEM), name="edges", compiler_params=room(8)
-    )(gas_state)
+    cell_rows = fine_cell.reshape(blocks, LANES)
+    inputs = (
+        gas_state, parcel_record, condensed_shares, cell_rows, block_counts, surface_steam_factor,
+    )
+    *held, edge_a, edge_b = pl.pallas_call(
+        load_kernel,
+        out_shape=tuple(jax.ShapeDtypeStruct(x.shape, x.dtype) for x in inputs) + (plane, plane),
+        in_specs=[HBM] * 6, out_specs=(VMEM,) * 8,
+        scratch_shapes=[pltpu.SemaphoreType.DMA((6,))],
+        name="load", compiler_params=room(8),
+    )(*[pltpu.with_memory_space_constraint(x, pltpu.HBM) for x in inputs])
+    gas_state, parcel_record, condensed_shares, cell_rows, block_counts, steam = held
     got_a, got_b = swap(edge_a, edge_b)
-    tiles = pl.pallas_call(
-        tiles_kernel,
-        out_shape=jax.ShapeDtypeStruct((inner, fields, LANES), F32),
-        in_specs=[VMEM], out_specs=VMEM, name="tiles", compiler_params=room(8),
-    )(gas_state)
     total_tiles = inner + 2 * per_plane + WIDE
+    all_tiles = jax.ShapeDtypeStruct((total_tiles, fields, LANES), F32)
+    record = jax.ShapeDtypeStruct(parcel_record.shape, F32)
+    scalars = jnp.concatenate(
+        [cell_rows[:, 0] // LANES, cell_rows[:, LANES - 1] // LANES, block_counts]
+    )
+    scalars = (scalars, steam)
+    partial = pl.pallas_call(
+        interior_kernel,
+        out_shape=(record, all_tiles, all_tiles),
+        in_specs=[SMEM] * 2 + [VMEM] * 4,
+        out_specs=(VMEM,) * 3,
+        name="interior", compiler_params=room(16),
+    )(*scalars, cell_rows, gas_state, parcel_record, condensed_shares)
     parcel_next, acc, send_a, send_b, coarse = pl.pallas_call(
-        parcels_kernel,
+        border_kernel,
         out_shape=(
-            jax.ShapeDtypeStruct(parcel_record.shape, F32),
-            jax.ShapeDtypeStruct((total_tiles, fields, LANES), F32),
+            record,
+            all_tiles,
             plane,
             plane,
             jax.ShapeDtypeStruct((8, columns + columns // 4), F32),
         ),
-        in_specs=[SMEM, SMEM, SMEM] + [VMEM] * 6,
+        in_specs=[SMEM] * 2 + [VMEM] * 8,
         out_specs=(VMEM,) * 5,
-        scratch_shapes=[pltpu.VMEM((total_tiles, fields, LANES), F32)],
-        name="parcels", compiler_params=room(16),
-    )(
-        fine_cell, block_counts, surface_steam_factor, fine_cell.reshape(blocks, LANES),
-        tiles, got_a, got_b, parcel_record, condensed_shares,
-    )
+        scratch_shapes=[pltpu.VMEM(all_tiles.shape, F32)],
+        name="border", compiler_params=room(16),
+    )(*scalars, cell_rows, got_a, got_b, parcel_record, condensed_shares, *partial)
     back_a, back_b = swap(send_a, send_b)
     fine_source = pl.pallas_call(
         merge_kernel,
@@ -455,12 +514,15 @@
         correction = pl.pallas_call(
             functools.partial(relax_kernel, masks, columns),
             out_shape=jax.ShapeDtypeStruct((COARSE, squared), F32),
-            in_specs=[VMEM] * len(parts), out_specs=VMEM,
+            in_specs=[VMEM] * len(parts),
+            out_specs=pl.BlockSpec(memory_space=pl.ANY),
             scratch_shapes=[
                 pltpu.VMEM((slabs, planes, squared), F32),
                 pltpu.VMEM((slabs + 2, 8, squared // 4), F32),
                 padded,
                 padded,
+                pltpu.VMEM((slabs, planes, squared), F32),
+                pltpu.SemaphoreType.DMA((slabs,)),
             ],
             name="relax", compiler_params=room(16),
         )(*parts)
@@ -489,7 +551,8 @@
         arrived = [send(mask) for mask in steps]
         held = jnp.concatenate([held] + arrived, axis=0)
         masks = masks + [m ^ mask for mask in steps for m in masks]
-    return (held, send(1)), (masks, [m ^ 1 for m in masks])
+    other = send(1)
+    return (held, other), (masks, [m ^ 1 for m in masks])
 
 
 def shared_planes(coarse, columns, planes, fine_per_coarse):
@@ -560,4 +623,9 @@
         P(("slab", "cross")),
     )
     out_specs = (P(None, ("slab", "cross")), P(None, "slab", "cross"), P())
-    return jax.shard_map(body, mesh=mesh, in_specs=in_specs, out_specs=out_specs, check_vma=False)
+
+    def step(*args):
+        return body(*args)
+
+    step = jax.shard_map(step, mesh=mesh, in_specs=in_specs, out_specs=out_specs, check_vma=False)
+    return step

time: 49.9 us -> 46.9 us (0.940)
  waiting for transfers between devices: 20.7 us -> 17.3 us
  Pallas kernels: 12.4 us -> 13.8 us
  local copies, waits for them, and re-layouts: 1.29 us -> 0.23 us
    ppermute x4, waiting for transfers between devices: 11.3 us -> 7.81 us  [swap(): return (lax.ppermute(a, AXES, pairs_a), lax.ppermute(b, AXES, pairs_b))]
    pallas_call x3, Pallas kernels: 5.57 us -> 7.18 us  [the longest x1 3.34 us: body(): pl.pallas_call(interior_kernel, out_shape=(record, all_tiles, all_tiles),...]
    unnamed x18 -> x6, local copies, waits for them, and re-layouts: 1.28 us -> 0.04 us
  transfers between devices with their start and end apart: 11 -> 11, of which waited for: 7 -> 6; matrix products, arithmetic and copies ran while one was open for 0% -> 1% of each run, Pallas kernels for 3% -> 10%
where the time goes in v3:
time: 46.9 us; the launch traced here: 46.8 us
  waiting for transfers between devices  17.3 us (37%)
  starting transfers between devices  14.6 us (31%)
  Pallas kernels  13.8 us (29%)
  between operations  0.76 us (2%)
    ppermute x7, waiting for transfers between devices, send(): lax.ppermute(held, AXES, [(i, i ^ mask) for i in range(device_count)])  9.47 us
    ppermute x4, waiting for transfers between devices, swap(): return (lax.ppermute(a, AXES, pairs_a), lax.ppermute(b, AXES, pairs_b))  7.81 us
    ppermute x7, starting transfers between devices, send(): lax.ppermute(held, AXES, [(i, i ^ mask) for i in range(device_count)])  7.67 us
    ppermute x4, starting transfers between devices, swap(): return (lax.ppermute(a, AXES, pairs_a), lax.ppermute(b, AXES, pairs_b))  6.97 us
    pallas_call x1, Pallas kernels, body(): pl.pallas_call(functools.partial(relax_kernel, masks, columns), out_shape...  5.39 us
    pallas_call x1, Pallas kernels, body(): pl.pallas_call(interior_kernel, out_shape=(record, all_tiles, all_tiles),...  3.34 us
    pallas_call x1, Pallas kernels, body(): pl.pallas_call(border_kernel, out_shape=(record, all_tiles, plane, plane,...  2.41 us
    pallas_call x1, Pallas kernels, body(): pl.pallas_call(load_kernel, out_shape=tuple((jax.ShapeDtypeStruct(x.shape...  1.43 us
  transfers between devices with their start and end apart: 11, of which 6 were waited for; matrix products, arithmetic and copies ran while one was open for 1% of the time, Pallas kernels for 10%

profile of v3, /device:TPU:8, one launch (start us, length us, event | category | flops | bytes accessed | tf_op | source)
XLA Modules:
  0.0 46.8 jit_solution(11109397995421671847)
XLA Ops:
  0.6 1.4 %load.1 = (f32[16,8,2048]{2,1,0:T(8,128)S(1)}, f32[5,4096]{1,0:T(8,128)S(1)}, f32[12,4096]{1,0:T(8,128)S(1)}, s32[32,128]{1,0:T(8,128)S(1)}, s32[32]{0:T(128)S(1...) custom-call(f32[16,8,2048]{2,1,0:T(8,128)} %gas_in.1, f32[5,4096]{1,0:T(8,128)} %record_in.1, ...), custom_call_target="tpu_custom_call" | custom-call | tf_op jit(solution)/shard_map/load/pallas_call | solution.py:463
  2.1 1.6 %collective-permute-start = (f32[16,16,128]{2,1,0:T(8,128)S(1)}, f32[16,16,128]{2,1,0:T(8,128)S(1)}, u32[]{:S(2)}, u32[]{:S(2)}) collective-permute-start(f32[16,16,128]{2,1,0:T(8,128)S(1)} %get-tuple-element.22), channel_id=1, source_target_pairs={{0,4},{4,0},{1,5},{5,1},{2,6},{6,2},{3,7},{7,3},{8,12},{12,8},{9,1... | collective-permute-start | bytes 393224 | tf_op jit(solution)/shard_map/ppermute | solution.py:456
  3.6 1.9 %collective-permute-start.1 = (f32[16,16,128]{2,1,0:T(8,128)S(1)}, f32[16,16,128]{2,1,0:T(8,128)S(1)}, u32[]{:S(2)}, u32[]{:S(2)}) collective-permute-start(f32[16,16,128]{2,1,0:T(8,128)S(1)} %get-tuple-element.23), channel_id=1, source_target_pairs={{4,8},{8,4},{5,9},{9,5},{6,10},{10,6},{7,11},{11,7},{12,16},{16,12... | collective-permute-start | bytes 393224 | tf_op jit(solution)/shard_map/ppermute | solution.py:456
  5.5 0.2 slice_reduce_fusion.1
  5.7 0.1 pad_add_fusion.scalar_s
  5.8 3.3 %interior.1 = (f32[5,4096]{1,0:T(8,128)S(1)}, f32[168,16,128]{2,1,0:T(8,128)S(1)}, f32[168,16,128]{2,1,0:T(8,128)S(1)}) custom-call(s32[96]{0:T(128)S(1)} %pad_add_fusion.scalar_s, f32[12]{0:T(128)S(1)} %get-tuple-element.21.steam_s, s32[32,128]{1,0:T(8,128)S(1)} %get-tuple-element.19.cell_v, f32[16,8,2048]{2,1,0:T(8,128)S(1)} %get-tuple-element.26.gas_state, ...), custom_call_target="tpu_custom_call" | custom-call | tf_op jit(solution)/shard_map/interior/pallas_call | solution.py:479
  9.2 0.0 collective-permute-done.pair_a
  9.2 2.2 %collective-permute-done.1.pair_b = f32[16,16,128]{2,1,0:T(8,128)S(1)} collective-permute-done((f32[16,16,128]{2,1,0:T(8,128)S(1)}, f32[16,16,128]{2,1,0:T(8,128)S(1)}, u32[]{:S(2)}, u32[]{:S(2)}) %collective-permute-start.1) | collective-permute-done | bytes 131104 | tf_op jit(solution)/shard_map/ppermute | solution.py:456
  11.4 2.4 %border.1 = (f32[5,4096]{1,0:T(8,128)}, f32[168,16,128]{2,1,0:T(8,128)S(1)}, f32[16,16,128]{2,1,0:T(8,128)S(1)}, f32[16,16,128]{2,1,0:T(8,128)S(1)}, f32[8,1280]{1,0:T(8,128)S(1)}) custom-call(s32[96]{0:T(128)S(1)} %pad_add_fusion.scalar_s, f32[12]{0:T(128)S(1)} %get-tuple-element.21.steam_s, s32[32,128]{1,0:T(8,128)S(1)} %get-tuple-element.19.cell_v, ...), custom_call_target="tpu_custom_call" | custom-call | tf_op jit(solution)/shard_map/border/pallas_call | solution.py:486
  13.8 1.6 %collective-permute-start.6 = (f32[1,8,1280]{2,1,0:T(8,128)S(1)}, f32[1,8,1280]{2,1,0:T(8,128)S(1)}, u32[]{:S(2)}, u32[]{:S(2)}) collective-permute-start(f32[1,8,1280]{2,1,0:T(8,128)S(1)} %bitcast.3), channel_id=1, source_target_pairs={{0,24},{1,25},{2,26},{3,27},{4,28},{5,29},{6,30},{7,31},{8,16},{9,... | collective-permute-start | bytes 122888 | tf_op jit(solution)/shard_map/ppermute | solution.py:545
  15.4 2.5 %collective-permute-start.5 = (f32[1,8,1280]{2,1,0:T(8,128)S(1)}, f32[1,8,1280]{2,1,0:T(8,128)S(1)}, u32[]{:S(2)}, u32[]{:S(2)}) collective-permute-start(f32[1,8,1280]{2,1,0:T(8,128)S(1)} %bitcast.4), channel_id=1, source_target_pairs={{0,8},{1,9},{2,10},{3,11},{4,12},{5,13},{6,14},{7,15},{8,0},{9,1},... | collective-permute-start | bytes 122888 | tf_op jit(solution)/shard_map/ppermute | solution.py:545
  17.8 0.0 collective-permute-start.4
  17.8 0.0 collective-permute-done.6
  17.8 2.4 %collective-permute-done.5 = f32[1,8,1280]{2,1,0:T(8,128)S(1)} collective-permute-done((f32[1,8,1280]{2,1,0:T(8,128)S(1)}, f32[1,8,1280]{2,1,0:T(8,128)S(1)}, u32[]{:S(2)}, u32[]{:S(2)}) %collective-permute-start.5) | collective-permute-done | bytes 40992 | tf_op jit(solution)/shard_map/ppermute | solution.py:545
  20.2 2.5 %collective-permute-done.4 = f32[1,8,1280]{2,1,0:T(8,128)S(1)} collective-permute-done((f32[1,8,1280]{2,1,0:T(8,128)S(1)}, f32[1,8,1280]{2,1,0:T(8,128)S(1)}, u32[]{:S(2)}, u32[]{:S(2)}) %collective-permute-start.4) | collective-permute-done | bytes 40992 | tf_op jit(solution)/shard_map/ppermute | solution.py:545
  22.8 0.1 collective-permute-start.9
  22.8 1.6 %collective-permute-start.8 = (f32[4,8,1280]{2,1,0:T(8,128)S(1)}, f32[4,8,1280]{2,1,0:T(8,128)S(1)}, u32[]{:S(2)}, u32[]{:S(2)}) collective-permute-start(f32[4,8,1280]{2,1,0:T(8,128)S(1)} %pad_maximum_fusion), channel_id=1, source_target_pairs={{0,2},{1,3},{2,0},{3,1},{4,6},{5,7},{6,4},{7,5},{8,10},{9,11},{10,... | collective-permute-start | bytes 491528 | tf_op jit(solution)/shard_map/ppermute | solution.py:545
  24.4 1.9 %collective-permute-start.7 = (f32[4,8,1280]{2,1,0:T(8,128)S(1)}, f32[4,8,1280]{2,1,0:T(8,128)S(1)}, u32[]{:S(2)}, u32[]{:S(2)}) collective-permute-start(f32[4,8,1280]{2,1,0:T(8,128)S(1)} %pad_maximum_fusion), channel_id=1, source_target_pairs={{0,4},{1,5},{2,6},{3,7},{4,0},{5,1},{6,2},{7,3},{8,12},{9,13},{10,... | collective-permute-start | bytes 491528 | tf_op jit(solution)/shard_map/ppermute | solution.py:545
  26.3 4.6 %collective-permute-done.7 = f32[4,8,1280]{2,1,0:T(8,128)S(1)} collective-permute-done((f32[4,8,1280]{2,1,0:T(8,128)S(1)}, f32[4,8,1280]{2,1,0:T(8,128)S(1)}, u32[]{:S(2)}, u32[]{:S(2)}) %collective-permute-start.7) | collective-permute-done | bytes 163872 | tf_op jit(solution)/shard_map/ppermute | solution.py:545
  30.9 0.0 collective-permute-done.8
  30.9 0.0 collective-permute-done.9
  31.0 0.1 collective-permute-start.10
  31.1 0.8 %collective-permute-start.2 = (f32[16,16,128]{2,1,0:T(8,128)S(1)}, f32[16,16,128]{2,1,0:T(8,128)S(1)}, u32[]{:S(2)}, u32[]{:S(2)}) collective-permute-start(f32[16,16,128]{2,1,0:T(8,128)S(1)} %get-tuple-element.32), channel_id=1, source_target_pairs={{0,4},{4,0},{1,5},{5,1},{2,6},{6,2},{3,7},{7,3},{8,12},{12,8},{9,1... | collective-permute-start | bytes 393224 | tf_op jit(solution)/shard_map/ppermute | solution.py:456
  31.9 2.7 %collective-permute-start.3 = (f32[16,16,128]{2,1,0:T(8,128)S(1)}, f32[16,16,128]{2,1,0:T(8,128)S(1)}, u32[]{:S(2)}, u32[]{:S(2)}) collective-permute-start(f32[16,16,128]{2,1,0:T(8,128)S(1)} %get-tuple-element.33), channel_id=1, source_target_pairs={{4,8},{8,4},{5,9},{9,5},{6,10},{10,6},{7,11},{11,7},{12,16},{16,12... | collective-permute-start | bytes 393224 | tf_op jit(solution)/shard_map/ppermute | solution.py:456
  34.6 2.4 %collective-permute-done.2.pair_a = f32[16,16,128]{2,1,0:T(8,128)S(1)} collective-permute-done((f32[16,16,128]{2,1,0:T(8,128)S(1)}, f32[16,16,128]{2,1,0:T(8,128)S(1)}, u32[]{:S(2)}, u32[]{:S(2)}) %collective-permute-start.2) | collective-permute-done | bytes 131104 | tf_op jit(solution)/shard_map/ppermute | solution.py:456
  37.0 3.2 %collective-permute-done.3.pair_b = f32[16,16,128]{2,1,0:T(8,128)S(1)} collective-permute-done((f32[16,16,128]{2,1,0:T(8,128)S(1)}, f32[16,16,128]{2,1,0:T(8,128)S(1)}, u32[]{:S(2)}, u32[]{:S(2)}) %collective-permute-start.3) | collective-permute-done | bytes 131104 | tf_op jit(solution)/shard_map/ppermute | solution.py:456
  40.2 1.2 %merge.1 = f32[16,8,2048]{2,1,0:T(8,128)} custom-call(f32[168,16,128]{2,1,0:T(8,128)S(1)} %get-tuple-element.31.acc, f32[16,16,128]{2,1,0:T(8,128)S(1)} %collective-permute-done.2.pair_a, f32[16,16,128]{2,1,0:T(8,128)S(1)} %collective-permute-done.3.pair_b), custom_call_target="tpu_custom_call" | custom-call | tf_op jit(solution)/shard_map/merge/pallas_call | solution.py:501
  41.4 0.0 collective-permute-done.10.refs_1_
  41.4 5.4 %relax.1 = f32[64,4096]{1,0:T(8,128)} custom-call(f32[16,8,1280]{2,1,0:T(8,128)S(1)} %constant_dynamic-update-slice_fusion.refs_0_, f32[16,8,1280]{2,1,0:T(8,128)S(1)} %collective-permute-done.10.refs_1_), custom_call_target="tpu_custom_call" | custom-call | tf_op jit(solution)/shard_map/relax/pallas_call | solution.py:514
  (9 shorter events, 0.1 us)
Async XLA Ops:
  2.1 7.1 %collective-permute-start = (f32[16,16,128]{2,1,0:T(8,128)S(1)}, f32[16,16,128]{2,1,0:T(8,128)S(1)}, u32[]{:S(2)}, u32[]{:S(2)}) collective-permute-start(f32[16,16,128]{2,1,0:T(8,128)S(1)} %get-tuple-element.22), channel_id=1, source_target_pairs={{0,4},{4,0},{1,5},{5,1},{2,6},{6,2},{3,7},{7,3},{8,12},{12,8},{9,1... | collective-permute-start | bytes 393224 | tf_op jit(solution)/shard_map/ppermute | solution.py:456
  3.6 7.7 %collective-permute-start.1 = (f32[16,16,128]{2,1,0:T(8,128)S(1)}, f32[16,16,128]{2,1,0:T(8,128)S(1)}, u32[]{:S(2)}, u32[]{:S(2)}) collective-permute-start(f32[16,16,128]{2,1,0:T(8,128)S(1)} %get-tuple-element.23), channel_id=1, source_target_pairs={{4,8},{8,4},{5,9},{9,5},{6,10},{10,6},{7,11},{11,7},{12,16},{16,12... | collective-permute-start | bytes 393224 | tf_op jit(solution)/shard_map/ppermute | solution.py:456
  13.8 4.1 %collective-permute-start.6 = (f32[1,8,1280]{2,1,0:T(8,128)S(1)}, f32[1,8,1280]{2,1,0:T(8,128)S(1)}, u32[]{:S(2)}, u32[]{:S(2)}) collective-permute-start(f32[1,8,1280]{2,1,0:T(8,128)S(1)} %bitcast.3), channel_id=1, source_target_pairs={{0,24},{1,25},{2,26},{3,27},{4,28},{5,29},{6,30},{7,31},{8,16},{9,... | collective-permute-start | bytes 122888 | tf_op jit(solution)/shard_map/ppermute | solution.py:545
  15.4 4.9 %collective-permute-start.5 = (f32[1,8,1280]{2,1,0:T(8,128)S(1)}, f32[1,8,1280]{2,1,0:T(8,128)S(1)}, u32[]{:S(2)}, u32[]{:S(2)}) collective-permute-start(f32[1,8,1280]{2,1,0:T(8,128)S(1)} %bitcast.4), channel_id=1, source_target_pairs={{0,8},{1,9},{2,10},{3,11},{4,12},{5,13},{6,14},{7,15},{8,0},{9,1},... | collective-permute-start | bytes 122888 | tf_op jit(solution)/shard_map/ppermute | solution.py:545
  17.8 4.9 %collective-permute-start.4 = (f32[1,8,1280]{2,1,0:T(8,128)S(1)}, f32[1,8,1280]{2,1,0:T(8,128)S(1)}, u32[]{:S(2)}, u32[]{:S(2)}) collective-permute-start(f32[1,8,1280]{2,1,0:T(8,128)S(1)} %bitcast.5), channel_id=1, source_target_pairs={{0,16},{1,17},{2,18},{3,19},{4,20},{5,21},{6,22},{7,23},{8,24},{9,... | collective-permute-start | bytes 122888 | tf_op jit(solution)/shard_map/ppermute | solution.py:545
  22.8 8.2 %collective-permute-start.9 = (f32[4,8,1280]{2,1,0:T(8,128)S(1)}, f32[4,8,1280]{2,1,0:T(8,128)S(1)}, u32[]{:S(2)}, u32[]{:S(2)}) collective-permute-start(f32[4,8,1280]{2,1,0:T(8,128)S(1)} %pad_maximum_fusion), channel_id=1, source_target_pairs={{0,6},{1,7},{2,4},{3,5},{4,2},{5,3},{6,0},{7,1},{8,14},{9,15},{10,... | collective-permute-start | bytes 491528 | tf_op jit(solution)/shard_map/ppermute | solution.py:545
  22.8 8.1 %collective-permute-start.8 = (f32[4,8,1280]{2,1,0:T(8,128)S(1)}, f32[4,8,1280]{2,1,0:T(8,128)S(1)}, u32[]{:S(2)}, u32[]{:S(2)}) collective-permute-start(f32[4,8,1280]{2,1,0:T(8,128)S(1)} %pad_maximum_fusion), channel_id=1, source_target_pairs={{0,2},{1,3},{2,0},{3,1},{4,6},{5,7},{6,4},{7,5},{8,10},{9,11},{10,... | collective-permute-start | bytes 491528 | tf_op jit(solution)/shard_map/ppermute | solution.py:545
  24.4 6.5 %collective-permute-start.7 = (f32[4,8,1280]{2,1,0:T(8,128)S(1)}, f32[4,8,1280]{2,1,0:T(8,128)S(1)}, u32[]{:S(2)}, u32[]{:S(2)}) collective-permute-start(f32[4,8,1280]{2,1,0:T(8,128)S(1)} %pad_maximum_fusion), channel_id=1, source_target_pairs={{0,4},{1,5},{2,6},{3,7},{4,0},{5,1},{6,2},{7,3},{8,12},{9,13},{10,... | collective-permute-start | bytes 491528 | tf_op jit(solution)/shard_map/ppermute | solution.py:545
  31.0 10.4 %collective-permute-start.10 = (f32[16,8,1280]{2,1,0:T(8,128)S(1)}, f32[16,8,1280]{2,1,0:T(8,128)S(1)}, u32[]{:S(2)}, u32[]{:S(2)}) collective-permute-start(f32[16,8,1280]{2,1,0:T(8,128)S(1)} %constant_dynamic-update-slice_fusion.refs_0_), channel_id=1, source_target_pairs={{0,1},{1,0},{2,3},{3,2},{4,5},{5,4},{6,7},{7,6},{8,9},{9,8},{10,11... | collective-permute-start | bytes 1966088 | tf_op jit(solution)/shard_map/ppermute | solution.py:545
  31.1 5.9 %collective-permute-start.2 = (f32[16,16,128]{2,1,0:T(8,128)S(1)}, f32[16,16,128]{2,1,0:T(8,128)S(1)}, u32[]{:S(2)}, u32[]{:S(2)}) collective-permute-start(f32[16,16,128]{2,1,0:T(8,128)S(1)} %get-tuple-element.32), channel_id=1, source_target_pairs={{0,4},{4,0},{1,5},{5,1},{2,6},{6,2},{3,7},{7,3},{8,12},{12,8},{9,1... | collective-permute-start | bytes 393224 | tf_op jit(solution)/shard_map/ppermute | solution.py:456
  31.9 8.3 %collective-permute-start.3 = (f32[16,16,128]{2,1,0:T(8,128)S(1)}, f32[16,16,128]{2,1,0:T(8,128)S(1)}, u32[]{:S(2)}, u32[]{:S(2)}) collective-permute-start(f32[16,16,128]{2,1,0:T(8,128)S(1)} %get-tuple-element.33), channel_id=1, source_target_pairs={{4,8},{8,4},{5,9},{9,5},{6,10},{10,6},{7,11},{11,7},{12,16},{16,12... | collective-permute-start | bytes 393224 | tf_op jit(solution)/shard_map/ppermute | solution.py:456

commit v4 on v3

--- a/solution.py
+++ b/solution.py
@@ -14,6 +14,8 @@
 LANES = 128
 WIDE = 8
 UNROLL = 4
+PIECES = 2
+GROUP = 2
 AXES = ("slab", "cross")
 F32 = jnp.float32
 VMEM = pl.BlockSpec(memory_space=pltpu.VMEM)
@@ -45,26 +47,28 @@
     gas_in, record_in, shares_in, rows_in_hbm, count_in, steam_in,
     gas, record, shares, rows, count, steam, first_pair, second_pair, sems,
 ):
+    fields, planes, cells = gas.shape
+    step = fields // PIECES
+    moves = [(gas_in.at[pl.ds(i * step, step)], gas.at[pl.ds(i * step, step)]) for i in range(PIECES)]
+    moves += [
+        (record_in, record), (shares_in, shares),
+        (rows_in_hbm, rows), (count_in, count), (steam_in, steam),
+    ]
     copies = [
         pltpu.make_async_copy(source, target, sems.at[i])
-        for i, (source, target) in enumerate(
-            [
-                (gas_in, gas), (record_in, record), (shares_in, shares),
-                (rows_in_hbm, rows), (count_in, count), (steam_in, steam),
-            ]
-        )
+        for i, (source, target) in enumerate(moves)
     ]
     for copy in copies:
         copy.start()
-    fields, planes, cells = gas.shape
     even = plane_sides()
-    copies[0].wait()
+    for copy in copies[:PIECES]:
+        copy.wait()
     for k in range(cells // LANES):
         x = jnp.swapaxes(gas[:, :, k * LANES : (k + 1) * LANES], 0, 1)
         low, high = (rows_in(x[p : p + 1], fields - 4)[0] for p in (0, planes - 1))
         first_pair[k] = jnp.where(even, high, low)
         second_pair[k] = jnp.where(even, low, high)
-    for copy in copies[1:]:
+    for copy in copies[PIECES:]:
         copy.wait()
 
 
@@ -185,7 +189,7 @@
                 tile_of, offset = prepare(base + u)
                 g = (zero, zero)
                 for j in range(WIDE):
-                    g = pick(gas[first + j], tile_of, offset, first + j, g)
+                    g = pick(gas(first + j), tile_of, offset, first + j, g)
                 staged.append((first, tile_of, offset, g))
             staged = [
                 (first, tile_of, offset, advance(base + u, g))
@@ -202,7 +206,7 @@
                 tile_of, offset = prepare(b)
 
                 def step(t, g):
-                    return pick(gas[t], tile_of, offset, t, g)
+                    return pick(gas(t), tile_of, offset, t, g)
 
                 g = lax.fori_loop(first, last + 1, step, (zero, zero))
                 parts = advance(b, g)
@@ -245,31 +249,32 @@
             gas[(p + 1) * per_plane + k] = x[p]
     run_groups(
         inside_planes(per_plane, inner),
-        scalar_s, steam_s, cell_v, record, shares, next_record, acc, gas,
+        scalar_s, steam_s, cell_v, record, shares, next_record, acc, lambda t: gas[t],
     )
 
 
 def border_kernel(
     scalar_s, steam_s, cell_v, pair_a, pair_b, record, shares,
-    record_before, acc_before, gas_before, next_record, acc, send_a, send_b, coarse, gas,
+    record_before, acc_before, gas_before, next_record, acc, send_a, send_b, coarse, halo,
 ):
     per_plane = pair_a.shape[0]
     inner = acc.shape[0] - 2 * per_plane - WIDE
     next_record[...] = record_before[...]
-
-    def carry(i, _):
-        for u in range(8):
-            acc[i * 8 + u] = acc_before[i * 8 + u]
-            gas[i * 8 + u] = gas_before[i * 8 + u]
-        return 0
-
-    lax.fori_loop(0, acc.shape[0] // 8, carry, 0)
+    for i in range(0, acc.shape[0], 8):
+        acc[i : i + 8] = acc_before[i : i + 8]
     species = shares.shape[0]
     even = plane_sides()
     for k in range(per_plane):
         a, b = pair_a[k], pair_b[k]
-        gas[k] = jnp.where(even, b, a)
-        gas[per_plane + inner + k] = jnp.where(even, a, b)
+        halo[k] = jnp.where(even, b, a)
+        halo[per_plane + k] = jnp.where(even, a, b)
+
+    def gas(t):
+        low = t < per_plane
+        high = t >= per_plane + inner
+        place = jnp.where(high, jnp.minimum(t - inner, 2 * per_plane - 1), jnp.minimum(t, per_plane - 1))
+        return jnp.where(low | high, halo[place], gas_before[t])
+
     within = inside_planes(per_plane, inner)
     run_groups(
         lambda first, last: jnp.logical_not(within(first, last)),
@@ -315,7 +320,8 @@
             coarse[r : r + 1, columns + c * LANES : columns + (c + 1) * LANES] = piece[h : h + 1]
 
 
-def merge_kernel(acc, pair_a, pair_b, out):
+def merge_kernel(acc, pair_a, pair_b, record_in, out, record):
+    record[...] = record_in[...]
     fields, planes, cells = out.shape
     per_plane = cells // LANES
     even = plane_sides()
@@ -332,7 +338,7 @@
 
 
 def relax_kernel(masks, columns, *refs):
-    *parts, out, source, ends, one, two, done, sems = refs
+    *parts, out, source, ends, one, two, done, even_products, odd_products, sems = refs
     planes = parts[0].shape[1]
     cross_count = lax.axis_size("cross")
     me = lax.axis_index("slab") * cross_count + lax.axis_index("cross")
@@ -343,13 +349,18 @@
     width = squared // LANES
     lane = lax.broadcasted_iota(jnp.int32, (8, LANES), 1)
     row = lax.broadcasted_iota(jnp.int32, (8, LANES), 0)
-    inside = lax.rem(lane, edge)
     sixth = 1.0 / 6.0
+
+    pitch = width + 1
+
+    def at_plane(plane, v):
+        return pl.ds((plane + 1) * pitch + v, 8, stride=pitch)
 
     for i in (0, slabs + 1):
         ends[i] = jnp.zeros(ends.shape[1:], F32)
-        one[i] = jnp.zeros(one.shape[1:], F32)
-        two[i] = jnp.zeros(two.shape[1:], F32)
+    for ref in (one, two):
+        for start in (0, (edge + 1) * pitch):
+            ref[pl.ds(start, pitch), :] = jnp.zeros((pitch, LANES), F32)
     for part, part_masks in zip(parts, masks):
         for i, mask in enumerate(part_masks):
             owner = lax.bitwise_xor(me, mask)
@@ -372,43 +383,62 @@
             x = source[s, :, at_lanes(v)]
             x = x + jnp.where(row == 7, above, jnp.where(row == 0, under, 0.0))
             source[s, :, at_lanes(v)] = x
-            one[s + 1, :, at_lanes(v)] = x * sixth
+            one[at_plane(s * 8, v), :] = x * sixth
         return 0
 
     lax.fori_loop(0, slabs, begin, 0)
 
-    def sweep(src, put):
-        def run(s, _):
-            nothing = jnp.zeros((8, LANES), F32)
-            x, turned = nothing, nothing
-            after = src[s + 1, :, at_lanes(0)]
-            turned_after = pltpu.roll(after, edge, axis=1)
+    k = lax.broadcasted_iota(jnp.int32, (2 * LANES, 2 * LANES), 0) % LANES
+    l = lax.broadcasted_iota(jnp.int32, (2 * LANES, 2 * LANES), 1)
+    crossed = k == lax.rem(l + edge, LANES)
+    beside = (jnp.abs(k - l) == 1) & (k // edge == l // edge)
+    near = jnp.where(crossed | beside, 1.0, 0.0).astype(jnp.bfloat16)
+
+    def multiply(src, group, products):
+        x = jnp.concatenate(
+            [
+                src[at_plane(s * 8, v), :]
+                for s in range(group * GROUP, (group + 1) * GROUP)
+                for v in range(width)
+            ],
+            axis=0,
+        )
+        high = x.astype(jnp.bfloat16)
+        middle = (x - high.astype(F32)).astype(jnp.bfloat16)
+        products[...] = jnp.dot(
+            jnp.concatenate([high, middle], axis=1), near, preferred_element_type=F32
+        )
+
+    def combine(src, group, products, put):
+        for i in range(GROUP):
+            s = group * GROUP + i
+            base = i * width * 8
+
+            def turned(v):
+                if 0 <= v < width:
+                    return products[base + v * 8 : base + v * 8 + 8, LANES:]
+                return jnp.zeros((8, LANES), F32)
+
             for v in range(width):
-                turned_before = turned
-                x, turned = after, turned_after
-                if v < width - 1:
-                    after = src[s + 1, :, at_lanes(v + 1)]
-                    turned_after = pltpu.roll(after, edge, axis=1)
-                else:
-                    turned_after = nothing
-                above = jnp.broadcast_to(src[s + 2, 0:1, at_lanes(v)], (8, LANES))
-                under = jnp.broadcast_to(src[s, 7:8, at_lanes(v)], (8, LANES))
-                total = source[s, :, at_lanes(v)] + turned
-                total = total + jnp.where(lane < edge, turned_before, turned_after)
-                total = total + jnp.where(row == 7, above, pltpu.roll(x, 7, axis=0))
-                total = total + jnp.where(row == 0, under, pltpu.roll(x, 1, axis=0))
-                total = total + jnp.where(inside < edge - 1, pltpu.roll(x, LANES - 1, axis=1), 0.0)
-                total = total + jnp.where(inside > 0, pltpu.roll(x, 1, axis=1), 0.0)
+                total = source[s, :, at_lanes(v)] + products[base + v * 8 : base + v * 8 + 8, :LANES]
+                total = total + jnp.where(lane < edge, turned(v - 1), turned(v + 1))
+                total = total + src[at_plane(s * 8 + 1, v), :] + src[at_plane(s * 8 - 1, v), :]
                 put(s, v, total * sixth)
             if put is final:
                 leave(s).start()
-            return 0
-
-        lax.fori_loop(0, slabs, run, 0)
+
+    def sweep(src, put):
+        groups = slabs // GROUP
+        multiply(src, 0, even_products)
+        for g in range(groups):
+            now, later = (even_products, odd_products)[:: 1 if g % 2 == 0 else -1]
+            if g + 1 < groups:
+                multiply(src, g + 1, later)
+            combine(src, g, now, put)
 
     def into(ref):
         def put(s, v, x):
-            ref[s + 1, :, at_lanes(v)] = x
+            ref[at_plane(s * 8, v), :] = x
 
         return put
 
@@ -464,7 +494,7 @@
         load_kernel,
         out_shape=tuple(jax.ShapeDtypeStruct(x.shape, x.dtype) for x in inputs) + (plane, plane),
         in_specs=[HBM] * 6, out_specs=(VMEM,) * 8,
-        scratch_shapes=[pltpu.SemaphoreType.DMA((6,))],
+        scratch_shapes=[pltpu.SemaphoreType.DMA((PIECES + 5,))],
         name="load", compiler_params=room(8),
     )(*[pltpu.with_memory_space_constraint(x, pltpu.HBM) for x in inputs])
     gas_state, parcel_record, condensed_shares, cell_rows, block_counts, steam = held
@@ -483,7 +513,7 @@
         out_specs=(VMEM,) * 3,
         name="interior", compiler_params=room(16),
     )(*scalars, cell_rows, gas_state, parcel_record, condensed_shares)
-    parcel_next, acc, send_a, send_b, coarse = pl.pallas_call(
+    updated, acc, send_a, send_b, coarse = pl.pallas_call(
         border_kernel,
         out_shape=(
             record,
@@ -494,15 +524,15 @@
         ),
         in_specs=[SMEM] * 2 + [VMEM] * 8,
         out_specs=(VMEM,) * 5,
-        scratch_shapes=[pltpu.VMEM(all_tiles.shape, F32)],
+        scratch_shapes=[pltpu.VMEM((2 * per_plane, fields, LANES), F32)],
         name="border", compiler_params=room(16),
     )(*scalars, cell_rows, got_a, got_b, parcel_record, condensed_shares, *partial)
     back_a, back_b = swap(send_a, send_b)
-    fine_source = pl.pallas_call(
+    fine_source, parcel_next = pl.pallas_call(
         merge_kernel,
-        out_shape=jax.ShapeDtypeStruct(gas_state.shape, F32),
-        in_specs=[VMEM] * 3, out_specs=VMEM, name="merge", compiler_params=room(12),
-    )(acc, back_a, back_b)
+        out_shape=(jax.ShapeDtypeStruct(gas_state.shape, F32), record),
+        in_specs=[VMEM] * 4, out_specs=(VMEM, VMEM), name="merge", compiler_params=room(12),
+    )(acc, back_a, back_b, updated)
 
     own_planes = planes
     if fine_per_coarse != 1:
@@ -510,7 +540,8 @@
     parts, masks = gather_all(coarse, device_count)
     if fine_per_coarse == 1:
         slabs = COARSE // planes
-        padded = pltpu.VMEM((slabs + 2, planes, squared), F32)
+        products = pltpu.VMEM((GROUP * planes * squared // LANES, 2 * LANES), F32)
+        padded = pltpu.VMEM(((COARSE + 2) * (squared // LANES + 1), LANES), F32)
         correction = pl.pallas_call(
             functools.partial(relax_kernel, masks, columns),
             out_shape=jax.ShapeDtypeStruct((COARSE, squared), F32),
@@ -522,6 +553,8 @@
                 padded,
                 padded,
                 pltpu.VMEM((slabs, planes, squared), F32),
+                products,
+                products,
                 pltpu.SemaphoreType.DMA((slabs,)),
             ],
             name="relax", compiler_params=room(16),
@@ -548,7 +581,9 @@
         steps = [1 << group[0]]
         if len(group) == 2:
             steps += [1 << group[1], (1 << group[0]) + (1 << group[1])]
-        arrived = [send(mask) for mask in steps]
+        arrived = []
+        for mask in steps:
+            arrived.append(send(mask))
         held = jnp.concatenate([held] + arrived, axis=0)
         masks = masks + [m ^ mask for mask in steps for m in masks]
     other = send(1)

time: 46.9 us -> 43.9 us (0.936)
  Pallas kernels: 13.8 us -> 10.7 us
    pallas_call x1, Pallas kernels: 5.39 us -> 2.55 us  [body(): pl.pallas_call(functools.partial(relax_kernel, masks, columns), out_shape...]
where the time goes in v4:
time: 43.9 us; the launch traced here: 43.7 us
  waiting for transfers between devices  17.3 us (39%)
  starting transfers between devices  14.7 us (33%)
  Pallas kernels  10.7 us (24%)
  between operations  0.77 us (2%)
    ppermute x7, waiting for transfers between devices, send(): lax.ppermute(held, AXES, [(i, i ^ mask) for i in range(device_count)])  9.46 us
    ppermute x4, waiting for transfers between devices, swap(): return (lax.ppermute(a, AXES, pairs_a), lax.ppermute(b, AXES, pairs_b))  7.81 us
    ppermute x7, starting transfers between devices, send(): lax.ppermute(held, AXES, [(i, i ^ mask) for i in range(device_count)])  7.74 us
    ppermute x4, starting transfers between devices, swap(): return (lax.ppermute(a, AXES, pairs_a), lax.ppermute(b, AXES, pairs_b))  6.98 us
    pallas_call x1, Pallas kernels, body(): pl.pallas_call(interior_kernel, out_shape=(record, all_tiles, all_tiles),...  3.34 us
    pallas_call x1, Pallas kernels, body(): pl.pallas_call(functools.partial(relax_kernel, masks, columns), out_shape...  2.55 us
    pallas_call x1, Pallas kernels, body(): pl.pallas_call(border_kernel, out_shape=(record, all_tiles, plane, plane,...  2.14 us
    pallas_call x1, Pallas kernels, body(): pl.pallas_call(load_kernel, out_shape=tuple((jax.ShapeDtypeStruct(x.shape...  1.42 us
  transfers between devices with their start and end apart: 11, of which 6 were waited for; matrix products, arithmetic and copies ran while one was open for 1% of the time, Pallas kernels for 10%

profile of v4, /device:TPU:8, one launch (start us, length us, event | category | flops | bytes accessed | tf_op | source)
XLA Modules:
  0.0 43.7 jit_solution(16175539055720678468)
XLA Ops:
  0.6 1.4 %load.1 = (f32[16,8,2048]{2,1,0:T(8,128)S(1)}, f32[5,4096]{1,0:T(8,128)S(1)}, f32[12,4096]{1,0:T(8,128)S(1)}, s32[32,128]{1,0:T(8,128)S(1)}, s32[32]{0:T(128)S(1...) custom-call(f32[16,8,2048]{2,1,0:T(8,128)} %gas_in.1, f32[5,4096]{1,0:T(8,128)} %record_in.1, ...), custom_call_target="tpu_custom_call" | custom-call | tf_op jit(solution)/shard_map/load/pallas_call | solution.py:493
  2.1 1.6 %collective-permute-start = (f32[16,16,128]{2,1,0:T(8,128)S(1)}, f32[16,16,128]{2,1,0:T(8,128)S(1)}, u32[]{:S(2)}, u32[]{:S(2)}) collective-permute-start(f32[16,16,128]{2,1,0:T(8,128)S(1)} %get-tuple-element.24), channel_id=1, source_target_pairs={{0,4},{4,0},{1,5},{5,1},{2,6},{6,2},{3,7},{7,3},{8,12},{12,8},{9,1... | collective-permute-start | bytes 393224 | tf_op jit(solution)/shard_map/ppermute | solution.py:486
  3.6 1.9 %collective-permute-start.1 = (f32[16,16,128]{2,1,0:T(8,128)S(1)}, f32[16,16,128]{2,1,0:T(8,128)S(1)}, u32[]{:S(2)}, u32[]{:S(2)}) collective-permute-start(f32[16,16,128]{2,1,0:T(8,128)S(1)} %get-tuple-element.25), channel_id=1, source_target_pairs={{4,8},{8,4},{5,9},{9,5},{6,10},{10,6},{7,11},{11,7},{12,16},{16,12... | collective-permute-start | bytes 393224 | tf_op jit(solution)/shard_map/ppermute | solution.py:486
  5.5 0.2 slice_reduce_fusion.1
  5.7 0.1 pad_add_fusion.scalar_s
  5.8 3.3 %interior.1 = (f32[5,4096]{1,0:T(8,128)S(1)}, f32[168,16,128]{2,1,0:T(8,128)S(1)}, f32[168,16,128]{2,1,0:T(8,128)S(1)}) custom-call(s32[96]{0:T(128)S(1)} %pad_add_fusion.scalar_s, f32[12]{0:T(128)S(1)} %get-tuple-element.23.steam_s, s32[32,128]{1,0:T(8,128)S(1)} %get-tuple-element.21.cell_v, f32[16,8,2048]{2,1,0:T(8,128)S(1)} %get-tuple-element.28.gas_state, ...), custom_call_target="tpu_custom_call" | custom-call | tf_op jit(solution)/shard_map/interior/pallas_call | solution.py:509
  9.2 0.0 collective-permute-done.pair_a
  9.2 2.2 %collective-permute-done.1.pair_b = f32[16,16,128]{2,1,0:T(8,128)S(1)} collective-permute-done((f32[16,16,128]{2,1,0:T(8,128)S(1)}, f32[16,16,128]{2,1,0:T(8,128)S(1)}, u32[]{:S(2)}, u32[]{:S(2)}) %collective-permute-start.1) | collective-permute-done | bytes 131104 | tf_op jit(solution)/shard_map/ppermute | solution.py:486
  11.4 2.1 %border.1 = (f32[5,4096]{1,0:T(8,128)S(1)}, f32[168,16,128]{2,1,0:T(8,128)S(1)}, f32[16,16,128]{2,1,0:T(8,128)S(1)}, f32[16,16,128]{2,1,0:T(8,128)S(1)}, f32[8,1280]{1,0:T(8,128)S(1)}) custom-call(s32[96]{0:T(128)S(1)} %pad_add_fusion.scalar_s, f32[12]{0:T(128)S(1)} %get-tuple-element.23.steam_s, s32[32,128]{1,0:T(8,128)S(1)} %get-tuple-element.21.cell_v, ...), custom_call_target="tpu_custom_call" | custom-call | tf_op jit(solution)/shard_map/border/pallas_call | solution.py:516
  13.5 1.6 %collective-permute-start.6 = (f32[1,8,1280]{2,1,0:T(8,128)S(1)}, f32[1,8,1280]{2,1,0:T(8,128)S(1)}, u32[]{:S(2)}, u32[]{:S(2)}) collective-permute-start(f32[1,8,1280]{2,1,0:T(8,128)S(1)} %bitcast.3), channel_id=1, source_target_pairs={{0,24},{1,25},{2,26},{3,27},{4,28},{5,29},{6,30},{7,31},{8,16},{9,... | collective-permute-start | bytes 122888 | tf_op jit(solution)/shard_map/ppermute | solution.py:578
  15.2 2.5 %collective-permute-start.5 = (f32[1,8,1280]{2,1,0:T(8,128)S(1)}, f32[1,8,1280]{2,1,0:T(8,128)S(1)}, u32[]{:S(2)}, u32[]{:S(2)}) collective-permute-start(f32[1,8,1280]{2,1,0:T(8,128)S(1)} %bitcast.4), channel_id=1, source_target_pairs={{0,8},{1,9},{2,10},{3,11},{4,12},{5,13},{6,14},{7,15},{8,0},{9,1},... | collective-permute-start | bytes 122888 | tf_op jit(solution)/shard_map/ppermute | solution.py:578
  17.6 0.0 collective-permute-start.4
  17.6 0.0 collective-permute-done.6
  17.6 2.4 %collective-permute-done.5 = f32[1,8,1280]{2,1,0:T(8,128)S(1)} collective-permute-done((f32[1,8,1280]{2,1,0:T(8,128)S(1)}, f32[1,8,1280]{2,1,0:T(8,128)S(1)}, u32[]{:S(2)}, u32[]{:S(2)}) %collective-permute-start.5) | collective-permute-done | bytes 40992 | tf_op jit(solution)/shard_map/ppermute | solution.py:578
  20.0 2.5 %collective-permute-done.4 = f32[1,8,1280]{2,1,0:T(8,128)S(1)} collective-permute-done((f32[1,8,1280]{2,1,0:T(8,128)S(1)}, f32[1,8,1280]{2,1,0:T(8,128)S(1)}, u32[]{:S(2)}, u32[]{:S(2)}) %collective-permute-start.4) | collective-permute-done | bytes 40992 | tf_op jit(solution)/shard_map/ppermute | solution.py:578
  22.5 0.1 collective-permute-start.9
  22.6 1.6 %collective-permute-start.8 = (f32[4,8,1280]{2,1,0:T(8,128)S(1)}, f32[4,8,1280]{2,1,0:T(8,128)S(1)}, u32[]{:S(2)}, u32[]{:S(2)}) collective-permute-start(f32[4,8,1280]{2,1,0:T(8,128)S(1)} %pad_maximum_fusion), channel_id=1, source_target_pairs={{0,2},{1,3},{2,0},{3,1},{4,6},{5,7},{6,4},{7,5},{8,10},{9,11},{10,... | collective-permute-start | bytes 491528 | tf_op jit(solution)/shard_map/ppermute | solution.py:578
  24.2 1.9 %collective-permute-start.7 = (f32[4,8,1280]{2,1,0:T(8,128)S(1)}, f32[4,8,1280]{2,1,0:T(8,128)S(1)}, u32[]{:S(2)}, u32[]{:S(2)}) collective-permute-start(f32[4,8,1280]{2,1,0:T(8,128)S(1)} %pad_maximum_fusion), channel_id=1, source_target_pairs={{0,4},{1,5},{2,6},{3,7},{4,0},{5,1},{6,2},{7,3},{8,12},{9,13},{10,... | collective-permute-start | bytes 491528 | tf_op jit(solution)/shard_map/ppermute | solution.py:578
  26.1 4.6 %collective-permute-done.7 = f32[4,8,1280]{2,1,0:T(8,128)S(1)} collective-permute-done((f32[4,8,1280]{2,1,0:T(8,128)S(1)}, f32[4,8,1280]{2,1,0:T(8,128)S(1)}, u32[]{:S(2)}, u32[]{:S(2)}) %collective-permute-start.7) | collective-permute-done | bytes 163872 | tf_op jit(solution)/shard_map/ppermute | solution.py:578
  30.7 0.0 collective-permute-done.8
  30.7 0.0 collective-permute-done.9
  30.8 0.1 collective-permute-start.10
  30.8 0.8 %collective-permute-start.2 = (f32[16,16,128]{2,1,0:T(8,128)S(1)}, f32[16,16,128]{2,1,0:T(8,128)S(1)}, u32[]{:S(2)}, u32[]{:S(2)}) collective-permute-start(f32[16,16,128]{2,1,0:T(8,128)S(1)} %get-tuple-element.33), channel_id=1, source_target_pairs={{0,4},{4,0},{1,5},{5,1},{2,6},{6,2},{3,7},{7,3},{8,12},{12,8},{9,1... | collective-permute-start | bytes 393224 | tf_op jit(solution)/shard_map/ppermute | solution.py:486
  31.6 2.7 %collective-permute-start.3 = (f32[16,16,128]{2,1,0:T(8,128)S(1)}, f32[16,16,128]{2,1,0:T(8,128)S(1)}, u32[]{:S(2)}, u32[]{:S(2)}) collective-permute-start(f32[16,16,128]{2,1,0:T(8,128)S(1)} %get-tuple-element.34), channel_id=1, source_target_pairs={{4,8},{8,4},{5,9},{9,5},{6,10},{10,6},{7,11},{11,7},{12,16},{16,12... | collective-permute-start | bytes 393224 | tf_op jit(solution)/shard_map/ppermute | solution.py:486
  34.4 2.4 %collective-permute-done.2.pair_a = f32[16,16,128]{2,1,0:T(8,128)S(1)} collective-permute-done((f32[16,16,128]{2,1,0:T(8,128)S(1)}, f32[16,16,128]{2,1,0:T(8,128)S(1)}, u32[]{:S(2)}, u32[]{:S(2)}) %collective-permute-start.2) | collective-permute-done | bytes 131104 | tf_op jit(solution)/shard_map/ppermute | solution.py:486
  36.7 3.2 %collective-permute-done.3.pair_b = f32[16,16,128]{2,1,0:T(8,128)S(1)} collective-permute-done((f32[16,16,128]{2,1,0:T(8,128)S(1)}, f32[16,16,128]{2,1,0:T(8,128)S(1)}, u32[]{:S(2)}, u32[]{:S(2)}) %collective-permute-start.3) | collective-permute-done | bytes 131104 | tf_op jit(solution)/shard_map/ppermute | solution.py:486
  40.0 1.2 %merge.1 = (f32[16,8,2048]{2,1,0:T(8,128)}, f32[5,4096]{1,0:T(8,128)}) custom-call(f32[168,16,128]{2,1,0:T(8,128)S(1)} %get-tuple-element.32.acc, f32[16,16,128]{2,1,0:T(8,128)S(1)} %collective-permute-done.2.pair_a, f32[16,16,128]{2,1,0:T(8,128)S(1)} %collective-permute-done.3.pair_b, f32[5,4096]{1,0:T(8,128)S(1)} %get-tuple-element.35.record_in), custom_call_target="tpu_custom_call" | custom-call | tf_op jit(solution)/shard_map/merge/pallas_call | solution.py:531
  41.2 0.0 collective-permute-done.10.refs_1_
  41.2 2.6 %relax.1 = f32[64,4096]{1,0:T(8,128)} custom-call(f32[16,8,1280]{2,1,0:T(8,128)S(1)} %constant_dynamic-update-slice_fusion.refs_0_, f32[16,8,1280]{2,1,0:T(8,128)S(1)} %collective-permute-done.10.refs_1_), custom_call_target="tpu_custom_call" | custom-call | tf_op jit(solution)/shard_map/relax/pallas_call | solution.py:545
  (9 shorter events, 0.1 us)
Async XLA Ops:
  2.1 7.1 %collective-permute-start = (f32[16,16,128]{2,1,0:T(8,128)S(1)}, f32[16,16,128]{2,1,0:T(8,128)S(1)}, u32[]{:S(2)}, u32[]{:S(2)}) collective-permute-start(f32[16,16,128]{2,1,0:T(8,128)S(1)} %get-tuple-element.24), channel_id=1, source_target_pairs={{0,4},{4,0},{1,5},{5,1},{2,6},{6,2},{3,7},{7,3},{8,12},{12,8},{9,1... | collective-permute-start | bytes 393224 | tf_op jit(solution)/shard_map/ppermute | solution.py:486
  3.6 7.7 %collective-permute-start.1 = (f32[16,16,128]{2,1,0:T(8,128)S(1)}, f32[16,16,128]{2,1,0:T(8,128)S(1)}, u32[]{:S(2)}, u32[]{:S(2)}) collective-permute-start(f32[16,16,128]{2,1,0:T(8,128)S(1)} %get-tuple-element.25), channel_id=1, source_target_pairs={{4,8},{8,4},{5,9},{9,5},{6,10},{10,6},{7,11},{11,7},{12,16},{16,12... | collective-permute-start | bytes 393224 | tf_op jit(solution)/shard_map/ppermute | solution.py:486
  13.5 4.1 %collective-permute-start.6 = (f32[1,8,1280]{2,1,0:T(8,128)S(1)}, f32[1,8,1280]{2,1,0:T(8,128)S(1)}, u32[]{:S(2)}, u32[]{:S(2)}) collective-permute-start(f32[1,8,1280]{2,1,0:T(8,128)S(1)} %bitcast.3), channel_id=1, source_target_pairs={{0,24},{1,25},{2,26},{3,27},{4,28},{5,29},{6,30},{7,31},{8,16},{9,... | collective-permute-start | bytes 122888 | tf_op jit(solution)/shard_map/ppermute | solution.py:578
  15.2 4.9 %collective-permute-start.5 = (f32[1,8,1280]{2,1,0:T(8,128)S(1)}, f32[1,8,1280]{2,1,0:T(8,128)S(1)}, u32[]{:S(2)}, u32[]{:S(2)}) collective-permute-start(f32[1,8,1280]{2,1,0:T(8,128)S(1)} %bitcast.4), channel_id=1, source_target_pairs={{0,8},{1,9},{2,10},{3,11},{4,12},{5,13},{6,14},{7,15},{8,0},{9,1},... | collective-permute-start | bytes 122888 | tf_op jit(solution)/shard_map/ppermute | solution.py:578
  17.6 4.9 %collective-permute-start.4 = (f32[1,8,1280]{2,1,0:T(8,128)S(1)}, f32[1,8,1280]{2,1,0:T(8,128)S(1)}, u32[]{:S(2)}, u32[]{:S(2)}) collective-permute-start(f32[1,8,1280]{2,1,0:T(8,128)S(1)} %bitcast.5), channel_id=1, source_target_pairs={{0,16},{1,17},{2,18},{3,19},{4,20},{5,21},{6,22},{7,23},{8,24},{9,... | collective-permute-start | bytes 122888 | tf_op jit(solution)/shard_map/ppermute | solution.py:578
  22.5 8.2 %collective-permute-start.9 = (f32[4,8,1280]{2,1,0:T(8,128)S(1)}, f32[4,8,1280]{2,1,0:T(8,128)S(1)}, u32[]{:S(2)}, u32[]{:S(2)}) collective-permute-start(f32[4,8,1280]{2,1,0:T(8,128)S(1)} %pad_maximum_fusion), channel_id=1, source_target_pairs={{0,6},{1,7},{2,4},{3,5},{4,2},{5,3},{6,0},{7,1},{8,14},{9,15},{10,... | collective-permute-start | bytes 491528 | tf_op jit(solution)/shard_map/ppermute | solution.py:578
  22.6 8.1 %collective-permute-start.8 = (f32[4,8,1280]{2,1,0:T(8,128)S(1)}, f32[4,8,1280]{2,1,0:T(8,128)S(1)}, u32[]{:S(2)}, u32[]{:S(2)}) collective-permute-start(f32[4,8,1280]{2,1,0:T(8,128)S(1)} %pad_maximum_fusion), channel_id=1, source_target_pairs={{0,2},{1,3},{2,0},{3,1},{4,6},{5,7},{6,4},{7,5},{8,10},{9,11},{10,... | collective-permute-start | bytes 491528 | tf_op jit(solution)/shard_map/ppermute | solution.py:578
  24.2 6.5 %collective-permute-start.7 = (f32[4,8,1280]{2,1,0:T(8,128)S(1)}, f32[4,8,1280]{2,1,0:T(8,128)S(1)}, u32[]{:S(2)}, u32[]{:S(2)}) collective-permute-start(f32[4,8,1280]{2,1,0:T(8,128)S(1)} %pad_maximum_fusion), channel_id=1, source_target_pairs={{0,4},{1,5},{2,6},{3,7},{4,0},{5,1},{6,2},{7,3},{8,12},{9,13},{10,... | collective-permute-start | bytes 491528 | tf_op jit(solution)/shard_map/ppermute | solution.py:578
  30.8 10.4 %collective-permute-start.10 = (f32[16,8,1280]{2,1,0:T(8,128)S(1)}, f32[16,8,1280]{2,1,0:T(8,128)S(1)}, u32[]{:S(2)}, u32[]{:S(2)}) collective-permute-start(f32[16,8,1280]{2,1,0:T(8,128)S(1)} %constant_dynamic-update-slice_fusion.refs_0_), channel_id=1, source_target_pairs={{0,1},{1,0},{2,3},{3,2},{4,5},{5,4},{6,7},{7,6},{8,9},{9,8},{10,11... | collective-permute-start | bytes 1966088 | tf_op jit(solution)/shard_map/ppermute | solution.py:578
  30.8 5.9 %collective-permute-start.2 = (f32[16,16,128]{2,1,0:T(8,128)S(1)}, f32[16,16,128]{2,1,0:T(8,128)S(1)}, u32[]{:S(2)}, u32[]{:S(2)}) collective-permute-start(f32[16,16,128]{2,1,0:T(8,128)S(1)} %get-tuple-element.33), channel_id=1, source_target_pairs={{0,4},{4,0},{1,5},{5,1},{2,6},{6,2},{3,7},{7,3},{8,12},{12,8},{9,1... | collective-permute-start | bytes 393224 | tf_op jit(solution)/shard_map/ppermute | solution.py:486
  31.6 8.3 %collective-permute-start.3 = (f32[16,16,128]{2,1,0:T(8,128)S(1)}, f32[16,16,128]{2,1,0:T(8,128)S(1)}, u32[]{:S(2)}, u32[]{:S(2)}) collective-permute-start(f32[16,16,128]{2,1,0:T(8,128)S(1)} %get-tuple-element.34), channel_id=1, source_target_pairs={{4,8},{8,4},{5,9},{9,5},{6,10},{10,6},{7,11},{11,7},{12,16},{16,12... | collective-permute-start | bytes 393224 | tf_op jit(solution)/shard_map/ppermute | solution.py:486

commit v5 on v4

--- a/solution.py
+++ b/solution.py
@@ -572,22 +572,22 @@
         groups.append(upper[:1])
         upper = upper[1:]
     groups += [upper[i : i + 2] for i in range(0, len(upper), 2)]
-    held, masks = x[None], [0]
-
-    def send(mask):
-        return lax.ppermute(held, AXES, [(i, i ^ mask) for i in range(device_count)])
+    held, masks = [x[None]], [[0]]
+
+    def send(part, mask):
+        return lax.ppermute(part, AXES, [(i, i ^ mask) for i in range(device_count)])
 
     for group in groups:
         steps = [1 << group[0]]
         if len(group) == 2:
             steps += [1 << group[1], (1 << group[0]) + (1 << group[1])]
-        arrived = []
-        for mask in steps:
-            arrived.append(send(mask))
-        held = jnp.concatenate([held] + arrived, axis=0)
-        masks = masks + [m ^ mask for mask in steps for m in masks]
-    other = send(1)
-    return (held, other), (masks, [m ^ 1 for m in masks])
+        if len(held) > 1:
+            held = [jnp.concatenate(held, axis=0)]
+            masks = [[m for part in masks for m in part]]
+        held = held + [send(held[0], mask) for mask in steps]
+        masks = masks + [[m ^ mask for m in masks[0]] for mask in steps]
+    held = held + [send(part, 1) for part in held]
+    return tuple(held), tuple(masks + [[m ^ 1 for m in part] for part in masks])
 
 
 def shared_planes(coarse, columns, planes, fine_per_coarse):

time: 43.9 us -> 44.5 us (1.014)
  waiting for transfers between devices: 17.3 us -> 17.9 us
    ppermute x4, waiting for transfers between devices: 7.81 us -> 8.27 us  [swap(): return (lax.ppermute(a, AXES, pairs_a), lax.ppermute(b, AXES, pairs_b))]
    ppermute x7 -> x10, starting transfers between devices: 7.74 us -> 8.12 us  [send(): lax.ppermute(part, AXES, [(i, i ^ mask) for i in range(device_count)])]
    ppermute x7 -> x10, waiting for transfers between devices: 9.46 us -> 9.67 us  [send(): lax.ppermute(part, AXES, [(i, i ^ mask) for i in range(device_count)])]
  transfers between devices with their start and end apart: 11 -> 14, of which waited for: 6 -> 8; matrix products, arithmetic and copies ran while one was open for 1% -> 1% of each run, Pallas kernels for 10% -> 10%
where the time goes in v5:
time: 44.5 us; the launch traced here: 44.4 us
  waiting for transfers between devices  17.9 us (40%)
  starting transfers between devices  14.8 us (33%)
  Pallas kernels  10.6 us (24%)
  between operations  0.73 us (2%)
    ppermute x10, waiting for transfers between devices, send(): lax.ppermute(part, AXES, [(i, i ^ mask) for i in range(device_count)])  9.67 us
    ppermute x4, waiting for transfers between devices, swap(): return (lax.ppermute(a, AXES, pairs_a), lax.ppermute(b, AXES, pairs_b))  8.27 us
    ppermute x10, starting transfers between devices, send(): lax.ppermute(part, AXES, [(i, i ^ mask) for i in range(device_count)])  8.12 us
    ppermute x4, starting transfers between devices, swap(): return (lax.ppermute(a, AXES, pairs_a), lax.ppermute(b, AXES, pairs_b))  6.68 us
    pallas_call x1, Pallas kernels, body(): pl.pallas_call(interior_kernel, out_shape=(record, all_tiles, all_tiles),...  3.34 us
    pallas_call x1, Pallas kernels, body(): pl.pallas_call(functools.partial(relax_kernel, masks, columns), out_shape...  2.55 us
    pallas_call x1, Pallas kernels, body(): pl.pallas_call(border_kernel, out_shape=(record, all_tiles, plane, plane,...  2.14 us
    pallas_call x1, Pallas kernels, body(): pl.pallas_call(load_kernel, out_shape=tuple((jax.ShapeDtypeStruct(x.shape...  1.42 us
  transfers between devices with their start and end apart: 14, of which 8 were waited for; matrix products, arithmetic and copies ran while one was open for 1% of the time, Pallas kernels for 10%

profile of v5, /device:TPU:8, one launch (start us, length us, event | category | flops | bytes accessed | tf_op | source)
XLA Modules:
  0.0 44.4 jit_solution(11773023416738240400)
XLA Ops:
  0.6 1.4 %load.1 = (f32[16,8,2048]{2,1,0:T(8,128)S(1)}, f32[5,4096]{1,0:T(8,128)S(1)}, f32[12,4096]{1,0:T(8,128)S(1)}, s32[32,128]{1,0:T(8,128)S(1)}, s32[32]{0:T(128)S(1...) custom-call(f32[16,8,2048]{2,1,0:T(8,128)} %gas_in.1, f32[5,4096]{1,0:T(8,128)} %record_in.1, ...), custom_call_target="tpu_custom_call" | custom-call | tf_op jit(solution)/shard_map/load/pallas_call | solution.py:493
  2.1 1.6 %collective-permute-start = (f32[16,16,128]{2,1,0:T(8,128)S(1)}, f32[16,16,128]{2,1,0:T(8,128)S(1)}, u32[]{:S(2)}, u32[]{:S(2)}) collective-permute-start(f32[16,16,128]{2,1,0:T(8,128)S(1)} %get-tuple-element.24), channel_id=1, source_target_pairs={{0,4},{4,0},{1,5},{5,1},{2,6},{6,2},{3,7},{7,3},{8,12},{12,8},{9,1... | collective-permute-start | bytes 393224 | tf_op jit(solution)/shard_map/ppermute | solution.py:486
  3.6 1.9 %collective-permute-start.1 = (f32[16,16,128]{2,1,0:T(8,128)S(1)}, f32[16,16,128]{2,1,0:T(8,128)S(1)}, u32[]{:S(2)}, u32[]{:S(2)}) collective-permute-start(f32[16,16,128]{2,1,0:T(8,128)S(1)} %get-tuple-element.25), channel_id=1, source_target_pairs={{4,8},{8,4},{5,9},{9,5},{6,10},{10,6},{7,11},{11,7},{12,16},{16,12... | collective-permute-start | bytes 393224 | tf_op jit(solution)/shard_map/ppermute | solution.py:486
  5.5 0.2 slice_reduce_fusion.1
  5.7 0.1 pad_add_fusion.scalar_s
  5.8 3.3 %interior.1 = (f32[5,4096]{1,0:T(8,128)S(1)}, f32[168,16,128]{2,1,0:T(8,128)S(1)}, f32[168,16,128]{2,1,0:T(8,128)S(1)}) custom-call(s32[96]{0:T(128)S(1)} %pad_add_fusion.scalar_s, f32[12]{0:T(128)S(1)} %get-tuple-element.23.steam_s, s32[32,128]{1,0:T(8,128)S(1)} %get-tuple-element.21.cell_v, f32[16,8,2048]{2,1,0:T(8,128)S(1)} %get-tuple-element.28.gas_state, ...), custom_call_target="tpu_custom_call" | custom-call | tf_op jit(solution)/shard_map/interior/pallas_call | solution.py:509
  9.2 0.0 collective-permute-done.pair_a
  9.2 2.2 %collective-permute-done.1.pair_b = f32[16,16,128]{2,1,0:T(8,128)S(1)} collective-permute-done((f32[16,16,128]{2,1,0:T(8,128)S(1)}, f32[16,16,128]{2,1,0:T(8,128)S(1)}, u32[]{:S(2)}, u32[]{:S(2)}) %collective-permute-start.1) | collective-permute-done | bytes 131104 | tf_op jit(solution)/shard_map/ppermute | solution.py:486
  11.4 2.1 %border.1 = (f32[5,4096]{1,0:T(8,128)S(1)}, f32[168,16,128]{2,1,0:T(8,128)S(1)}, f32[16,16,128]{2,1,0:T(8,128)S(1)}, f32[16,16,128]{2,1,0:T(8,128)S(1)}, f32[8,1280]{1,0:T(8,128)S(1)}) custom-call(s32[96]{0:T(128)S(1)} %pad_add_fusion.scalar_s, f32[12]{0:T(128)S(1)} %get-tuple-element.23.steam_s, s32[32,128]{1,0:T(8,128)S(1)} %get-tuple-element.21.cell_v, ...), custom_call_target="tpu_custom_call" | custom-call | tf_op jit(solution)/shard_map/border/pallas_call | solution.py:516
  13.5 1.6 %collective-permute-start.6 = (f32[1,8,1280]{2,1,0:T(8,128)S(1)}, f32[1,8,1280]{2,1,0:T(8,128)S(1)}, u32[]{:S(2)}, u32[]{:S(2)}) collective-permute-start(f32[1,8,1280]{2,1,0:T(8,128)S(1)} %bitcast.2), channel_id=1, source_target_pairs={{0,24},{1,25},{2,26},{3,27},{4,28},{5,29},{6,30},{7,31},{8,16},{9,... | collective-permute-start | bytes 122888 | tf_op jit(solution)/shard_map/ppermute | solution.py:578
  15.2 2.5 %collective-permute-start.5 = (f32[1,8,1280]{2,1,0:T(8,128)S(1)}, f32[1,8,1280]{2,1,0:T(8,128)S(1)}, u32[]{:S(2)}, u32[]{:S(2)}) collective-permute-start(f32[1,8,1280]{2,1,0:T(8,128)S(1)} %bitcast.3), channel_id=1, source_target_pairs={{0,8},{1,9},{2,10},{3,11},{4,12},{5,13},{6,14},{7,15},{8,0},{9,1},... | collective-permute-start | bytes 122888 | tf_op jit(solution)/shard_map/ppermute | solution.py:578
  17.6 0.0 collective-permute-start.4
  17.6 0.0 collective-permute-done.6
  17.6 2.4 %collective-permute-done.5 = f32[1,8,1280]{2,1,0:T(8,128)S(1)} collective-permute-done((f32[1,8,1280]{2,1,0:T(8,128)S(1)}, f32[1,8,1280]{2,1,0:T(8,128)S(1)}, u32[]{:S(2)}, u32[]{:S(2)}) %collective-permute-start.5) | collective-permute-done | bytes 40992 | tf_op jit(solution)/shard_map/ppermute | solution.py:578
  20.0 2.5 %collective-permute-done.4 = f32[1,8,1280]{2,1,0:T(8,128)S(1)} collective-permute-done((f32[1,8,1280]{2,1,0:T(8,128)S(1)}, f32[1,8,1280]{2,1,0:T(8,128)S(1)}, u32[]{:S(2)}, u32[]{:S(2)}) %collective-permute-start.4) | collective-permute-done | bytes 40992 | tf_op jit(solution)/shard_map/ppermute | solution.py:578
  22.5 0.1 collective-permute-start.9
  22.6 1.6 %collective-permute-start.8 = (f32[4,8,1280]{2,1,0:T(8,128)S(1)}, f32[4,8,1280]{2,1,0:T(8,128)S(1)}, u32[]{:S(2)}, u32[]{:S(2)}) collective-permute-start(f32[4,8,1280]{2,1,0:T(8,128)S(1)} %pad_maximum_fusion.refs_0_), channel_id=1, source_target_pairs={{0,2},{1,3},{2,0},{3,1},{4,6},{5,7},{6,4},{7,5},{8,10},{9,11},{10,... | collective-permute-start | bytes 491528 | tf_op jit(solution)/shard_map/ppermute | solution.py:578
  24.2 1.9 %collective-permute-start.7 = (f32[4,8,1280]{2,1,0:T(8,128)S(1)}, f32[4,8,1280]{2,1,0:T(8,128)S(1)}, u32[]{:S(2)}, u32[]{:S(2)}) collective-permute-start(f32[4,8,1280]{2,1,0:T(8,128)S(1)} %pad_maximum_fusion.refs_0_), channel_id=1, source_target_pairs={{0,4},{1,5},{2,6},{3,7},{4,0},{5,1},{6,2},{7,3},{8,12},{9,13},{10,... | collective-permute-start | bytes 491528 | tf_op jit(solution)/shard_map/ppermute | solution.py:578
  26.1 0.1 collective-permute-start.2
  26.2 0.0 collective-permute-start.10
  26.2 3.5 %collective-permute-done.9.refs_3_ = f32[4,8,1280]{2,1,0:T(8,128)S(1)} collective-permute-done((f32[4,8,1280]{2,1,0:T(8,128)S(1)}, f32[4,8,1280]{2,1,0:T(8,128)S(1)}, u32[]{:S(2)}, u32[]{:S(2)}) %collective-permute-start.9) | collective-permute-done | bytes 163872 | tf_op jit(solution)/shard_map/ppermute | solution.py:578
  29.7 0.0 collective-permute-start.13
  29.7 0.1 collective-permute-done.8.refs_2_
  29.8 0.4 collective-permute-start.12
  30.2 1.2 %collective-permute-done.7.refs_1_ = f32[4,8,1280]{2,1,0:T(8,128)S(1)} collective-permute-done((f32[4,8,1280]{2,1,0:T(8,128)S(1)}, f32[4,8,1280]{2,1,0:T(8,128)S(1)}, u32[]{:S(2)}, u32[]{:S(2)}) %collective-permute-start.7) | collective-permute-done | bytes 163872 | tf_op jit(solution)/shard_map/ppermute | solution.py:578
  31.4 0.0 collective-permute-start.11
  31.5 1.4 %collective-permute-done.2.pair_a = f32[16,16,128]{2,1,0:T(8,128)S(1)} collective-permute-done((f32[16,16,128]{2,1,0:T(8,128)S(1)}, f32[16,16,128]{2,1,0:T(8,128)S(1)}, u32[]{:S(2)}, u32[]{:S(2)}) %collective-permute-start.2) | collective-permute-done | bytes 131104 | tf_op jit(solution)/shard_map/ppermute | solution.py:486
  32.9 3.1 %collective-permute-start.3 = (f32[16,16,128]{2,1,0:T(8,128)S(1)}, f32[16,16,128]{2,1,0:T(8,128)S(1)}, u32[]{:S(2)}, u32[]{:S(2)}) collective-permute-start(f32[16,16,128]{2,1,0:T(8,128)S(1)} %get-tuple-element.34), channel_id=1, source_target_pairs={{4,8},{8,4},{5,9},{9,5},{6,10},{10,6},{7,11},{11,7},{12,16},{16,12... | collective-permute-start | bytes 393224 | tf_op jit(solution)/shard_map/ppermute | solution.py:486
  35.9 4.7 %collective-permute-done.3.pair_b = f32[16,16,128]{2,1,0:T(8,128)S(1)} collective-permute-done((f32[16,16,128]{2,1,0:T(8,128)S(1)}, f32[16,16,128]{2,1,0:T(8,128)S(1)}, u32[]{:S(2)}, u32[]{:S(2)}) %collective-permute-start.3) | collective-permute-done | bytes 131104 | tf_op jit(solution)/shard_map/ppermute | solution.py:486
  40.6 1.2 %merge.1 = (f32[16,8,2048]{2,1,0:T(8,128)}, f32[5,4096]{1,0:T(8,128)}) custom-call(f32[168,16,128]{2,1,0:T(8,128)S(1)} %get-tuple-element.32.acc, f32[16,16,128]{2,1,0:T(8,128)S(1)} %collective-permute-done.2.pair_a, f32[16,16,128]{2,1,0:T(8,128)S(1)} %collective-permute-done.3.pair_b, f32[5,4096]{1,0:T(8,128)S(1)} %get-tuple-element.35.record_in), custom_call_target="tpu_custom_call" | custom-call | tf_op jit(solution)/shard_map/merge/pallas_call | solution.py:531
  41.8 0.0 collective-permute-done.10.refs_4_
  41.8 0.0 collective-permute-done.13.refs_7_
  41.8 0.0 collective-permute-done.12.refs_6_
  41.8 0.0 collective-permute-done.11.refs_5_
  41.8 2.5 %relax.1 = f32[64,4096]{1,0:T(8,128)} custom-call(f32[4,8,1280]{2,1,0:T(8,128)S(1)} %pad_maximum_fusion.refs_0_, f32[4,8,1280]{2,1,0:T(8,128)S(1)} %collective-permute-done.7.refs_1_, f32[4,8,1280]{2,1,0:T(8,128)S(1)} %collective-permute-done.8.refs_2_, f32[4,8,1280]{2,1,0:T(8,128)S(1)} %collective-permute-done.9.refs_3_, ...), custom_call_target="tpu_custom_call" | custom-call | tf_op jit(solution)/shard_map/relax/pallas_call | solution.py:545
  (2 shorter events, 0.0 us)
Async XLA Ops:
  2.1 7.1 %collective-permute-start = (f32[16,16,128]{2,1,0:T(8,128)S(1)}, f32[16,16,128]{2,1,0:T(8,128)S(1)}, u32[]{:S(2)}, u32[]{:S(2)}) collective-permute-start(f32[16,16,128]{2,1,0:T(8,128)S(1)} %get-tuple-element.24), channel_id=1, source_target_pairs={{0,4},{4,0},{1,5},{5,1},{2,6},{6,2},{3,7},{7,3},{8,12},{12,8},{9,1... | collective-permute-start | bytes 393224 | tf_op jit(solution)/shard_map/ppermute | solution.py:486
  3.6 7.7 %collective-permute-start.1 = (f32[16,16,128]{2,1,0:T(8,128)S(1)}, f32[16,16,128]{2,1,0:T(8,128)S(1)}, u32[]{:S(2)}, u32[]{:S(2)}) collective-permute-start(f32[16,16,128]{2,1,0:T(8,128)S(1)} %get-tuple-element.25), channel_id=1, source_target_pairs={{4,8},{8,4},{5,9},{9,5},{6,10},{10,6},{7,11},{11,7},{12,16},{16,12... | collective-permute-start | bytes 393224 | tf_op jit(solution)/shard_map/ppermute | solution.py:486
  13.5 4.1 %collective-permute-start.6 = (f32[1,8,1280]{2,1,0:T(8,128)S(1)}, f32[1,8,1280]{2,1,0:T(8,128)S(1)}, u32[]{:S(2)}, u32[]{:S(2)}) collective-permute-start(f32[1,8,1280]{2,1,0:T(8,128)S(1)} %bitcast.2), channel_id=1, source_target_pairs={{0,24},{1,25},{2,26},{3,27},{4,28},{5,29},{6,30},{7,31},{8,16},{9,... | collective-permute-start | bytes 122888 | tf_op jit(solution)/shard_map/ppermute | solution.py:578
  15.2 4.9 %collective-permute-start.5 = (f32[1,8,1280]{2,1,0:T(8,128)S(1)}, f32[1,8,1280]{2,1,0:T(8,128)S(1)}, u32[]{:S(2)}, u32[]{:S(2)}) collective-permute-start(f32[1,8,1280]{2,1,0:T(8,128)S(1)} %bitcast.3), channel_id=1, source_target_pairs={{0,8},{1,9},{2,10},{3,11},{4,12},{5,13},{6,14},{7,15},{8,0},{9,1},... | collective-permute-start | bytes 122888 | tf_op jit(solution)/shard_map/ppermute | solution.py:578
  17.6 4.9 %collective-permute-start.4 = (f32[1,8,1280]{2,1,0:T(8,128)S(1)}, f32[1,8,1280]{2,1,0:T(8,128)S(1)}, u32[]{:S(2)}, u32[]{:S(2)}) collective-permute-start(f32[1,8,1280]{2,1,0:T(8,128)S(1)} %bitcast.4), channel_id=1, source_target_pairs={{0,16},{1,17},{2,18},{3,19},{4,20},{5,21},{6,22},{7,23},{8,24},{9,... | collective-permute-start | bytes 122888 | tf_op jit(solution)/shard_map/ppermute | solution.py:578
  22.5 7.1 %collective-permute-start.9 = (f32[4,8,1280]{2,1,0:T(8,128)S(1)}, f32[4,8,1280]{2,1,0:T(8,128)S(1)}, u32[]{:S(2)}, u32[]{:S(2)}) collective-permute-start(f32[4,8,1280]{2,1,0:T(8,128)S(1)} %pad_maximum_fusion.refs_0_), channel_id=1, source_target_pairs={{0,6},{1,7},{2,4},{3,5},{4,2},{5,3},{6,0},{7,1},{8,14},{9,15},{10,... | collective-permute-start | bytes 491528 | tf_op jit(solution)/shard_map/ppermute | solution.py:578
  22.6 7.1 %collective-permute-start.8 = (f32[4,8,1280]{2,1,0:T(8,128)S(1)}, f32[4,8,1280]{2,1,0:T(8,128)S(1)}, u32[]{:S(2)}, u32[]{:S(2)}) collective-permute-start(f32[4,8,1280]{2,1,0:T(8,128)S(1)} %pad_maximum_fusion.refs_0_), channel_id=1, source_target_pairs={{0,2},{1,3},{2,0},{3,1},{4,6},{5,7},{6,4},{7,5},{8,10},{9,11},{10,... | collective-permute-start | bytes 491528 | tf_op jit(solution)/shard_map/ppermute | solution.py:578
  24.2 7.2 %collective-permute-start.7 = (f32[4,8,1280]{2,1,0:T(8,128)S(1)}, f32[4,8,1280]{2,1,0:T(8,128)S(1)}, u32[]{:S(2)}, u32[]{:S(2)}) collective-permute-start(f32[4,8,1280]{2,1,0:T(8,128)S(1)} %pad_maximum_fusion.refs_0_), channel_id=1, source_target_pairs={{0,4},{1,5},{2,6},{3,7},{4,0},{5,1},{6,2},{7,3},{8,12},{9,13},{10,... | collective-permute-start | bytes 491528 | tf_op jit(solution)/shard_map/ppermute | solution.py:578
  26.1 6.8 %collective-permute-start.2 = (f32[16,16,128]{2,1,0:T(8,128)S(1)}, f32[16,16,128]{2,1,0:T(8,128)S(1)}, u32[]{:S(2)}, u32[]{:S(2)}) collective-permute-start(f32[16,16,128]{2,1,0:T(8,128)S(1)} %get-tuple-element.33), channel_id=1, source_target_pairs={{0,4},{4,0},{1,5},{5,1},{2,6},{6,2},{3,7},{7,3},{8,12},{12,8},{9,1... | collective-permute-start | bytes 393224 | tf_op jit(solution)/shard_map/ppermute | solution.py:486
  26.2 15.6 %collective-permute-start.10 = (f32[4,8,1280]{2,1,0:T(8,128)S(1)}, f32[4,8,1280]{2,1,0:T(8,128)S(1)}, u32[]{:S(2)}, u32[]{:S(2)}) collective-permute-start(f32[4,8,1280]{2,1,0:T(8,128)S(1)} %pad_maximum_fusion.refs_0_), channel_id=1, source_target_pairs={{0,1},{1,0},{2,3},{3,2},{4,5},{5,4},{6,7},{7,6},{8,9},{9,8},{10,11... | collective-permute-start | bytes 491528 | tf_op jit(solution)/shard_map/ppermute | solution.py:578
  29.7 12.1 %collective-permute-start.13 = (f32[4,8,1280]{2,1,0:T(8,128)S(1)}, f32[4,8,1280]{2,1,0:T(8,128)S(1)}, u32[]{:S(2)}, u32[]{:S(2)}) collective-permute-start(f32[4,8,1280]{2,1,0:T(8,128)S(1)} %collective-permute-done.9.refs_3_), channel_id=1, source_target_pairs={{0,1},{1,0},{2,3},{3,2},{4,5},{5,4},{6,7},{7,6},{8,9},{9,8},{10,11... | collective-permute-start | bytes 491528 | tf_op jit(solution)/shard_map/ppermute | solution.py:578
  29.8 12.1 %collective-permute-start.12 = (f32[4,8,1280]{2,1,0:T(8,128)S(1)}, f32[4,8,1280]{2,1,0:T(8,128)S(1)}, u32[]{:S(2)}, u32[]{:S(2)}) collective-permute-start(f32[4,8,1280]{2,1,0:T(8,128)S(1)} %collective-permute-done.8.refs_2_), channel_id=1, source_target_pairs={{0,1},{1,0},{2,3},{3,2},{4,5},{5,4},{6,7},{7,6},{8,9},{9,8},{10,11... | collective-permute-start | bytes 491528 | tf_op jit(solution)/shard_map/ppermute | solution.py:578
  31.4 10.4 %collective-permute-start.11 = (f32[4,8,1280]{2,1,0:T(8,128)S(1)}, f32[4,8,1280]{2,1,0:T(8,128)S(1)}, u32[]{:S(2)}, u32[]{:S(2)}) collective-permute-start(f32[4,8,1280]{2,1,0:T(8,128)S(1)} %collective-permute-done.7.refs_1_), channel_id=1, source_target_pairs={{0,1},{1,0},{2,3},{3,2},{4,5},{5,4},{6,7},{7,6},{8,9},{9,8},{10,11... | collective-permute-start | bytes 491528 | tf_op jit(solution)/shard_map/ppermute | solution.py:578
  32.9 7.7 %collective-permute-start.3 = (f32[16,16,128]{2,1,0:T(8,128)S(1)}, f32[16,16,128]{2,1,0:T(8,128)S(1)}, u32[]{:S(2)}, u32[]{:S(2)}) collective-permute-start(f32[16,16,128]{2,1,0:T(8,128)S(1)} %get-tuple-element.34), channel_id=1, source_target_pairs={{4,8},{8,4},{5,9},{9,5},{6,10},{10,6},{7,11},{11,7},{12,16},{16,12... | collective-permute-start | bytes 393224 | tf_op jit(solution)/shard_map/ppermute | solution.py:486

commit v6 on v5

--- a/solution.py
+++ b/solution.py
@@ -19,7 +19,6 @@
 AXES = ("slab", "cross")
 F32 = jnp.float32
 VMEM = pl.BlockSpec(memory_space=pltpu.VMEM)
-SMEM = pl.BlockSpec(memory_space=pltpu.SMEM)
 HBM = pl.BlockSpec(memory_space=pltpu.HBM)
 
 
@@ -45,14 +44,14 @@
 
 def load_kernel(
     gas_in, record_in, shares_in, rows_in_hbm, count_in, steam_in,
-    gas, record, shares, rows, count, steam, first_pair, second_pair, sems,
+    gas, record, shares, rows, count, steam, first_pair, second_pair, steam_s, sems,
 ):
     fields, planes, cells = gas.shape
     step = fields // PIECES
     moves = [(gas_in.at[pl.ds(i * step, step)], gas.at[pl.ds(i * step, step)]) for i in range(PIECES)]
     moves += [
         (record_in, record), (shares_in, shares),
-        (rows_in_hbm, rows), (count_in, count), (steam_in, steam),
+        (rows_in_hbm, rows), (count_in, count), (steam_in, steam_s),
     ]
     copies = [
         pltpu.make_async_copy(source, target, sems.at[i])
@@ -70,6 +69,11 @@
         second_pair[k] = jnp.where(even, low, high)
     for copy in copies[PIECES:]:
         copy.wait()
+    species_row = lax.broadcasted_iota(jnp.int32, steam.shape, 0)
+    spread = jnp.zeros(steam.shape, F32)
+    for j in range(shares.shape[0]):
+        spread = jnp.where(species_row == j, steam_s[j], spread)
+    steam[...] = spread
 
 
 def advance_block(g, record, shares, steam, count):
@@ -139,20 +143,20 @@
         acc[first + j] = acc[first + j] + total
 
 
-def run_groups(wanted, scalar_s, steam_s, cell_v, record, shares, next_record, acc, gas):
+def tile_number(cell):
+    return lax.shift_right_logical(cell, LANES.bit_length() - 1)
+
+
+def run_groups(wanted, scalar_s, steam_v, cell_v, record, shares, next_record, acc, gas):
     blocks = cell_v.shape[0]
-    species = shares.shape[0]
-    species_row = lax.broadcasted_iota(jnp.int32, (16, 1), 0)
-    steam = jnp.zeros((16, 1), F32)
-    for j in range(species):
-        steam = jnp.where(species_row == j, steam_s[j], steam)
-    steam = jnp.broadcast_to(steam, (16, LANES))
+    steam = steam_v[...]
     spot = lax.broadcasted_iota(jnp.int32, (LANES, LANES), 0)
     zero = jnp.zeros((8, LANES), F32)
 
     def prepare(b):
         cell = cell_v[pl.ds(b, 1), :]
-        return cell // LANES, jnp.broadcast_to(lax.rem(cell, LANES), (8, LANES))
+        offset = lax.bitwise_and(cell, LANES - 1)
+        return tile_number(cell), jnp.broadcast_to(offset, (8, LANES))
 
     def pick(tile, tile_of, offset, number, old):
         here = tile_of == number
@@ -230,8 +234,10 @@
 
 
 def interior_kernel(
-    scalar_s, steam_s, cell_v, gas_state, record, shares, next_record, acc, gas
+    scalar_v, steam_v, cell_v, gas_state, record, shares, next_record, acc, gas, scalar_s, sem
 ):
+    fetch = pltpu.make_async_copy(scalar_v, scalar_s, sem)
+    fetch.start()
     fields, planes, cells = gas_state.shape
     per_plane = cells // LANES
     inner = planes * per_plane
@@ -247,16 +253,20 @@
         x = rows_in(x, fields - 4)
         for p in range(planes):
             gas[(p + 1) * per_plane + k] = x[p]
+    fetch.wait()
     run_groups(
         inside_planes(per_plane, inner),
-        scalar_s, steam_s, cell_v, record, shares, next_record, acc, lambda t: gas[t],
+        scalar_s, steam_v, cell_v, record, shares, next_record, acc, lambda t: gas[t],
     )
 
 
 def border_kernel(
-    scalar_s, steam_s, cell_v, pair_a, pair_b, record, shares,
-    record_before, acc_before, gas_before, next_record, acc, send_a, send_b, coarse, halo,
+    scalar_v, steam_v, cell_v, pair_a, pair_b, record, shares,
+    record_before, acc_before, gas_before, next_record, acc, send_a, send_b, coarse,
+    halo, scalar_s, sem,
 ):
+    fetch = pltpu.make_async_copy(scalar_v, scalar_s, sem)
+    fetch.start()
     per_plane = pair_a.shape[0]
     inner = acc.shape[0] - 2 * per_plane - WIDE
     next_record[...] = record_before[...]
@@ -272,13 +282,14 @@
     def gas(t):
         low = t < per_plane
         high = t >= per_plane + inner
-        place = jnp.where(high, jnp.minimum(t - inner, 2 * per_plane - 1), jnp.minimum(t, per_plane - 1))
+        place = jnp.where(high, t - inner, jnp.where(low, t, 0))
         return jnp.where(low | high, halo[place], gas_before[t])
 
     within = inside_planes(per_plane, inner)
+    fetch.wait()
     run_groups(
         lambda first, last: jnp.logical_not(within(first, last)),
-        scalar_s, steam_s, cell_v, record, shares, next_record, acc, gas,
+        scalar_s, steam_v, cell_v, record, shares, next_record, acc, gas,
     )
     for k in range(per_plane):
         low, high = acc[k], acc[per_plane + inner + k]
@@ -293,31 +304,32 @@
     def mass_of(stack):
         return jnp.sum(jnp.where(row < species, stack, 0.0), axis=1) * (1.0 / volume_inverse)
 
-    def halves(pick_tiles):
-        out = []
-        for k in range(per_plane):
-            mass = mass_of(pick_tiles(k))
-            both = mass + pltpu.roll(mass, LANES - 1, axis=1)
-            out.append(jnp.take_along_axis(both, take, axis=1))
-        return [
-            jnp.where(lane < LANES // 2, out[2 * i], out[2 * i + 1])
-            for i in range(per_plane // 2)
-        ]
-
-    own = halves(
-        lambda k: jnp.stack([acc[(p + 1) * per_plane + k] for p in range(planes)])
-    )
-    for i, piece in enumerate(own):
-        coarse[:, i * LANES : (i + 1) * LANES] = piece
-    ends = halves(
-        lambda k: jnp.stack([acc[k], acc[per_plane + inner + k]] + [jnp.zeros((16, LANES), F32)] * 6)
-    )
+    def paired(stack):
+        mass = mass_of(stack)
+        both = mass + pltpu.roll(mass, LANES - 1, axis=1)
+        return jnp.take_along_axis(both, take, axis=1)
+
+    def join(left, right):
+        return jnp.where(lane[: left.shape[0]] < LANES // 2, left, right)
+
+    own = [
+        paired(jnp.stack([acc[(p + 1) * per_plane + k] for p in range(planes)]))
+        for k in range(per_plane)
+    ]
+    for i in range(per_plane // 2):
+        coarse[:, i * LANES : (i + 1) * LANES] = join(own[2 * i], own[2 * i + 1])
     columns = per_plane // 2 * LANES
     quarter = per_plane // 8
-    for h in range(2):
-        for i, piece in enumerate(ends):
-            r, c = 4 * h + i // quarter, i % quarter
-            coarse[r : r + 1, columns + c * LANES : columns + (c + 1) * LANES] = piece[h : h + 1]
+    for g in range(per_plane // 4):
+        sides = (0, per_plane + inner)
+        tile = paired(jnp.stack([acc[side + 4 * g + j] for side in sides for j in range(4)]))
+        for h in range(2):
+            for j in range(2):
+                i, at = 2 * g + j, 4 * h + 2 * j
+                r, c = 4 * h + i // quarter, i % quarter
+                coarse[r : r + 1, columns + c * LANES : columns + (c + 1) * LANES] = join(
+                    tile[at : at + 1], tile[at + 1 : at + 2]
+                )
 
 
 def merge_kernel(acc, pair_a, pair_b, record_in, out, record):
@@ -341,7 +353,6 @@
     *parts, out, source, ends, one, two, done, even_products, odd_products, sems = refs
     planes = parts[0].shape[1]
     cross_count = lax.axis_size("cross")
-    me = lax.axis_index("slab") * cross_count + lax.axis_index("cross")
     edge = COARSE
     slabs = edge // planes
     quarter = columns // 4
@@ -363,9 +374,8 @@
             ref[pl.ds(start, pitch), :] = jnp.zeros((pitch, LANES), F32)
     for part, part_masks in zip(parts, masks):
         for i, mask in enumerate(part_masks):
-            owner = lax.bitwise_xor(me, mask)
-            slab = owner // cross_count
-            cross = lax.rem(owner, cross_count)
+            slab = lax.bitwise_xor(lax.axis_index("slab"), mask // cross_count)
+            cross = lax.bitwise_xor(lax.axis_index("cross"), mask % cross_count)
             at = pl.ds(pl.multiple_of(cross * columns, LANES), columns)
             source[slab, :, at] = part[i, :, :columns]
             at = pl.ds(pl.multiple_of(cross * quarter, LANES), quarter)
@@ -492,9 +502,10 @@
     )
     *held, edge_a, edge_b = pl.pallas_call(
         load_kernel,
-        out_shape=tuple(jax.ShapeDtypeStruct(x.shape, x.dtype) for x in inputs) + (plane, plane),
+        out_shape=tuple(jax.ShapeDtypeStruct(x.shape, x.dtype) for x in inputs[:-1])
+        + (jax.ShapeDtypeStruct((16, LANES), F32), plane, plane),
         in_specs=[HBM] * 6, out_specs=(VMEM,) * 8,
-        scratch_shapes=[pltpu.SemaphoreType.DMA((PIECES + 5,))],
+        scratch_shapes=[pltpu.SMEM(surface_steam_factor.shape, F32), pltpu.SemaphoreType.DMA((PIECES + 5,))],
         name="load", compiler_params=room(8),
     )(*[pltpu.with_memory_space_constraint(x, pltpu.HBM) for x in inputs])
     gas_state, parcel_record, condensed_shares, cell_rows, block_counts, steam = held
@@ -503,14 +514,15 @@
     all_tiles = jax.ShapeDtypeStruct((total_tiles, fields, LANES), F32)
     record = jax.ShapeDtypeStruct(parcel_record.shape, F32)
     scalars = jnp.concatenate(
-        [cell_rows[:, 0] // LANES, cell_rows[:, LANES - 1] // LANES, block_counts]
+        [tile_number(cell_rows[:, 0]), tile_number(cell_rows[:, LANES - 1]), block_counts]
     )
     scalars = (scalars, steam)
     partial = pl.pallas_call(
         interior_kernel,
         out_shape=(record, all_tiles, all_tiles),
-        in_specs=[SMEM] * 2 + [VMEM] * 4,
+        in_specs=[VMEM] * 6,
         out_specs=(VMEM,) * 3,
+        scratch_shapes=[pltpu.SMEM(scalars[0].shape, jnp.int32), pltpu.SemaphoreType.DMA],
         name="interior", compiler_params=room(16),
     )(*scalars, cell_rows, gas_state, parcel_record, condensed_shares)
     updated, acc, send_a, send_b, coarse = pl.pallas_call(
@@ -522,9 +534,13 @@
             plane,
             jax.ShapeDtypeStruct((8, columns + columns // 4), F32),
         ),
-        in_specs=[SMEM] * 2 + [VMEM] * 8,
+        in_specs=[VMEM] * 10,
         out_specs=(VMEM,) * 5,
-        scratch_shapes=[pltpu.VMEM((2 * per_plane, fields, LANES), F32)],
+        scratch_shapes=[
+            pltpu.VMEM((2 * per_plane + WIDE, fields, LANES), F32),
+            pltpu.SMEM(scalars[0].shape, jnp.int32),
+            pltpu.SemaphoreType.DMA,
+        ],
         name="border", compiler_params=room(16),
     )(*scalars, cell_rows, got_a, got_b, parcel_record, condensed_shares, *partial)
     back_a, back_b = swap(send_a, send_b)

time: 44.5 us -> 44.3 us (level)
  waiting for transfers between devices: 17.9 us -> 18.7 us
  Pallas kernels: 10.6 us -> 10 us
    ppermute x4, waiting for transfers between devices: 8.27 us -> 9.04 us  [swap(): return (lax.ppermute(a, AXES, pairs_a), lax.ppermute(b, AXES, pairs_b))]
  transfers between devices with their start and end apart: 14 -> 14, of which waited for: 8 -> 8; matrix products, arithmetic and copies ran while one was open for 1% -> 1% of each run, Pallas kernels for 10% -> 9%
where the time goes in v6:
time: 44.3 us; the launch traced here: 44.1 us
  waiting for transfers between devices  18.7 us (42%)
  starting transfers between devices  14.4 us (33%)
  Pallas kernels  10 us (23%)
  between operations  0.72 us (2%)
    ppermute x10, waiting for transfers between devices, send(): lax.ppermute(part, AXES, [(i, i ^ mask) for i in range(device_count)])  9.66 us
    ppermute x4, waiting for transfers between devices, swap(): return (lax.ppermute(a, AXES, pairs_a), lax.ppermute(b, AXES, pairs_b))  9.04 us
    ppermute x10, starting transfers between devices, send(): lax.ppermute(part, AXES, [(i, i ^ mask) for i in range(device_count)])  8.11 us
    ppermute x4, starting transfers between devices, swap(): return (lax.ppermute(a, AXES, pairs_a), lax.ppermute(b, AXES, pairs_b))  6.3 us
    pallas_call x1, Pallas kernels, body(): pl.pallas_call(interior_kernel, out_shape=(record, all_tiles, all_tiles),...  2.96 us
    pallas_call x1, Pallas kernels, body(): pl.pallas_call(functools.partial(relax_kernel, masks, columns), out_shape...  2.44 us
    pallas_call x1, Pallas kernels, body(): pl.pallas_call(border_kernel, out_shape=(record, all_tiles, plane, plane,...  1.96 us
    pallas_call x1, Pallas kernels, body(): pl.pallas_call(load_kernel, out_shape=tuple((jax.ShapeDtypeStruct(x.shape...  1.43 us
  transfers between devices with their start and end apart: 14, of which 8 were waited for; matrix products, arithmetic and copies ran while one was open for 1% of the time, Pallas kernels for 9%

profile of v6, /device:TPU:8, one launch (start us, length us, event | category | flops | bytes accessed | tf_op | source)
XLA Modules:
  0.0 44.1 jit_solution(13828321330741705072)
XLA Ops:
  0.6 1.4 %load.1 = (f32[16,8,2048]{2,1,0:T(8,128)S(1)}, f32[5,4096]{1,0:T(8,128)S(1)}, f32[12,4096]{1,0:T(8,128)S(1)}, s32[32,128]{1,0:T(8,128)S(1)}, s32[32]{0:T(128)S(1...) custom-call(f32[16,8,2048]{2,1,0:T(8,128)} %gas_in.1, f32[5,4096]{1,0:T(8,128)} %record_in.1, ...), custom_call_target="tpu_custom_call" | custom-call | tf_op jit(solution)/shard_map/load/pallas_call | solution.py:503
  2.1 1.6 %collective-permute-start = (f32[16,16,128]{2,1,0:T(8,128)S(1)}, f32[16,16,128]{2,1,0:T(8,128)S(1)}, u32[]{:S(2)}, u32[]{:S(2)}) collective-permute-start(f32[16,16,128]{2,1,0:T(8,128)S(1)} %get-tuple-element.24), channel_id=1, source_target_pairs={{0,4},{4,0},{1,5},{5,1},{2,6},{6,2},{3,7},{7,3},{8,12},{12,8},{9,1... | collective-permute-start | bytes 393224 | tf_op jit(solution)/shard_map/ppermute | solution.py:496
  3.6 1.9 %collective-permute-start.1 = (f32[16,16,128]{2,1,0:T(8,128)S(1)}, f32[16,16,128]{2,1,0:T(8,128)S(1)}, u32[]{:S(2)}, u32[]{:S(2)}) collective-permute-start(f32[16,16,128]{2,1,0:T(8,128)S(1)} %get-tuple-element.25), channel_id=1, source_target_pairs={{4,8},{8,4},{5,9},{9,5},{6,10},{10,6},{7,11},{11,7},{12,16},{16,12... | collective-permute-start | bytes 393224 | tf_op jit(solution)/shard_map/ppermute | solution.py:496
  5.5 0.2 shift-right-logical_reduce_fusion.1
  5.7 0.1 pad_add_fusion.scalar_v
  5.8 3.0 %interior.1 = (f32[5,4096]{1,0:T(8,128)S(1)}, f32[168,16,128]{2,1,0:T(8,128)S(1)}, f32[168,16,128]{2,1,0:T(8,128)S(1)}) custom-call(s32[96]{0:T(128)S(1)} %pad_add_fusion.scalar_v, f32[16,128]{1,0:T(8,128)S(1)} %get-tuple-element.23.steam_v, s32[32,128]{1,0:T(8,128)S(1)} %get-tuple-element.21.cell_v, f32[16,8,2048]{2,1,0:T(8,128)S(1)} %get-tuple-element.28.gas_state, ...), custom_call_target="tpu_custom_call" | custom-call | tf_op jit(solution)/shard_map/interior/pallas_call | solution.py:520
  8.8 0.0 collective-permute-done.pair_a
  8.8 2.6 %collective-permute-done.1.pair_b = f32[16,16,128]{2,1,0:T(8,128)S(1)} collective-permute-done((f32[16,16,128]{2,1,0:T(8,128)S(1)}, f32[16,16,128]{2,1,0:T(8,128)S(1)}, u32[]{:S(2)}, u32[]{:S(2)}) %collective-permute-start.1) | collective-permute-done | bytes 131104 | tf_op jit(solution)/shard_map/ppermute | solution.py:496
  11.4 2.0 %border.1 = (f32[5,4096]{1,0:T(8,128)S(1)}, f32[168,16,128]{2,1,0:T(8,128)S(1)}, f32[16,16,128]{2,1,0:T(8,128)S(1)}, f32[16,16,128]{2,1,0:T(8,128)S(1)}, f32[8,1280]{1,0:T(8,128)S(1)}) custom-call(s32[96]{0:T(128)S(1)} %pad_add_fusion.scalar_v, f32[16,128]{1,0:T(8,128)S(1)} %get-tuple-element.23.steam_v, s32[32,128]{1,0:T(8,128)S(1)} %get-tuple-element.21.cell_v, ...), custom_call_target="tpu_custom_call" | custom-call | tf_op jit(solution)/shard_map/border/pallas_call | solution.py:528
  13.3 1.6 %collective-permute-start.6 = (f32[1,8,1280]{2,1,0:T(8,128)S(1)}, f32[1,8,1280]{2,1,0:T(8,128)S(1)}, u32[]{:S(2)}, u32[]{:S(2)}) collective-permute-start(f32[1,8,1280]{2,1,0:T(8,128)S(1)} %bitcast.2), channel_id=1, source_target_pairs={{0,24},{1,25},{2,26},{3,27},{4,28},{5,29},{6,30},{7,31},{8,16},{9,... | collective-permute-start | bytes 122888 | tf_op jit(solution)/shard_map/ppermute | solution.py:594
  15.0 2.5 %collective-permute-start.5 = (f32[1,8,1280]{2,1,0:T(8,128)S(1)}, f32[1,8,1280]{2,1,0:T(8,128)S(1)}, u32[]{:S(2)}, u32[]{:S(2)}) collective-permute-start(f32[1,8,1280]{2,1,0:T(8,128)S(1)} %bitcast.3), channel_id=1, source_target_pairs={{0,8},{1,9},{2,10},{3,11},{4,12},{5,13},{6,14},{7,15},{8,0},{9,1},... | collective-permute-start | bytes 122888 | tf_op jit(solution)/shard_map/ppermute | solution.py:594
  17.5 0.0 collective-permute-start.4
  17.5 0.0 collective-permute-done.6
  17.5 2.4 %collective-permute-done.5 = f32[1,8,1280]{2,1,0:T(8,128)S(1)} collective-permute-done((f32[1,8,1280]{2,1,0:T(8,128)S(1)}, f32[1,8,1280]{2,1,0:T(8,128)S(1)}, u32[]{:S(2)}, u32[]{:S(2)}) %collective-permute-start.5) | collective-permute-done | bytes 40992 | tf_op jit(solution)/shard_map/ppermute | solution.py:594
  19.9 2.5 %collective-permute-done.4 = f32[1,8,1280]{2,1,0:T(8,128)S(1)} collective-permute-done((f32[1,8,1280]{2,1,0:T(8,128)S(1)}, f32[1,8,1280]{2,1,0:T(8,128)S(1)}, u32[]{:S(2)}, u32[]{:S(2)}) %collective-permute-start.4) | collective-permute-done | bytes 40992 | tf_op jit(solution)/shard_map/ppermute | solution.py:594
  22.4 0.1 collective-permute-start.9
  22.5 1.6 %collective-permute-start.8 = (f32[4,8,1280]{2,1,0:T(8,128)S(1)}, f32[4,8,1280]{2,1,0:T(8,128)S(1)}, u32[]{:S(2)}, u32[]{:S(2)}) collective-permute-start(f32[4,8,1280]{2,1,0:T(8,128)S(1)} %pad_maximum_fusion.refs_0_), channel_id=1, source_target_pairs={{0,2},{1,3},{2,0},{3,1},{4,6},{5,7},{6,4},{7,5},{8,10},{9,11},{10,... | collective-permute-start | bytes 491528 | tf_op jit(solution)/shard_map/ppermute | solution.py:594
  24.0 1.9 %collective-permute-start.7 = (f32[4,8,1280]{2,1,0:T(8,128)S(1)}, f32[4,8,1280]{2,1,0:T(8,128)S(1)}, u32[]{:S(2)}, u32[]{:S(2)}) collective-permute-start(f32[4,8,1280]{2,1,0:T(8,128)S(1)} %pad_maximum_fusion.refs_0_), channel_id=1, source_target_pairs={{0,4},{1,5},{2,6},{3,7},{4,0},{5,1},{6,2},{7,3},{8,12},{9,13},{10,... | collective-permute-start | bytes 491528 | tf_op jit(solution)/shard_map/ppermute | solution.py:594
  25.9 0.1 collective-permute-start.2
  26.1 0.0 collective-permute-start.10
  26.1 3.5 %collective-permute-done.9.refs_3_ = f32[4,8,1280]{2,1,0:T(8,128)S(1)} collective-permute-done((f32[4,8,1280]{2,1,0:T(8,128)S(1)}, f32[4,8,1280]{2,1,0:T(8,128)S(1)}, u32[]{:S(2)}, u32[]{:S(2)}) %collective-permute-start.9) | collective-permute-done | bytes 163872 | tf_op jit(solution)/shard_map/ppermute | solution.py:594
  29.5 0.0 collective-permute-start.13
  29.5 0.1 collective-permute-done.8.refs_2_
  29.6 0.4 %collective-permute-start.12 = (f32[4,8,1280]{2,1,0:T(8,128)S(1)}, f32[4,8,1280]{2,1,0:T(8,128)S(1)}, u32[]{:S(2)}, u32[]{:S(2)}) collective-permute-start(f32[4,8,1280]{2,1,0:T(8,128)S(1)} %collective-permute-done.8.refs_2_), channel_id=1, source_target_pairs={{0,1},{1,0},{2,3},{3,2},{4,5},{5,4},{6,7},{7,6},{8,9},{9,8},{10,11... | collective-permute-start | bytes 491528 | tf_op jit(solution)/shard_map/ppermute | solution.py:594
  30.0 1.2 %collective-permute-done.7.refs_1_ = f32[4,8,1280]{2,1,0:T(8,128)S(1)} collective-permute-done((f32[4,8,1280]{2,1,0:T(8,128)S(1)}, f32[4,8,1280]{2,1,0:T(8,128)S(1)}, u32[]{:S(2)}, u32[]{:S(2)}) %collective-permute-start.7) | collective-permute-done | bytes 163872 | tf_op jit(solution)/shard_map/ppermute | solution.py:594
  31.3 0.0 collective-permute-start.11
  31.3 1.4 %collective-permute-done.2.pair_a = f32[16,16,128]{2,1,0:T(8,128)S(1)} collective-permute-done((f32[16,16,128]{2,1,0:T(8,128)S(1)}, f32[16,16,128]{2,1,0:T(8,128)S(1)}, u32[]{:S(2)}, u32[]{:S(2)}) %collective-permute-start.2) | collective-permute-done | bytes 131104 | tf_op jit(solution)/shard_map/ppermute | solution.py:496
  32.7 2.7 %collective-permute-start.3 = (f32[16,16,128]{2,1,0:T(8,128)S(1)}, f32[16,16,128]{2,1,0:T(8,128)S(1)}, u32[]{:S(2)}, u32[]{:S(2)}) collective-permute-start(f32[16,16,128]{2,1,0:T(8,128)S(1)} %get-tuple-element.34), channel_id=1, source_target_pairs={{4,8},{8,4},{5,9},{9,5},{6,10},{10,6},{7,11},{11,7},{12,16},{16,12... | collective-permute-start | bytes 393224 | tf_op jit(solution)/shard_map/ppermute | solution.py:496
  35.4 5.0 %collective-permute-done.3.pair_b = f32[16,16,128]{2,1,0:T(8,128)S(1)} collective-permute-done((f32[16,16,128]{2,1,0:T(8,128)S(1)}, f32[16,16,128]{2,1,0:T(8,128)S(1)}, u32[]{:S(2)}, u32[]{:S(2)}) %collective-permute-start.3) | collective-permute-done | bytes 131104 | tf_op jit(solution)/shard_map/ppermute | solution.py:496
  40.4 1.2 %merge.1 = (f32[16,8,2048]{2,1,0:T(8,128)}, f32[5,4096]{1,0:T(8,128)}) custom-call(f32[168,16,128]{2,1,0:T(8,128)S(1)} %get-tuple-element.32.acc, f32[16,16,128]{2,1,0:T(8,128)S(1)} %collective-permute-done.2.pair_a, f32[16,16,128]{2,1,0:T(8,128)S(1)} %collective-permute-done.3.pair_b, f32[5,4096]{1,0:T(8,128)S(1)} %get-tuple-element.35.record_in), custom_call_target="tpu_custom_call" | custom-call | tf_op jit(solution)/shard_map/merge/pallas_call | solution.py:547
  41.6 0.0 collective-permute-done.10.refs_4_
  41.6 0.0 collective-permute-done.13.refs_7_
  41.7 0.0 collective-permute-done.12.refs_6_
  41.7 0.0 collective-permute-done.11.refs_5_
  41.7 2.4 %relax.1 = f32[64,4096]{1,0:T(8,128)} custom-call(f32[4,8,1280]{2,1,0:T(8,128)S(1)} %pad_maximum_fusion.refs_0_, f32[4,8,1280]{2,1,0:T(8,128)S(1)} %collective-permute-done.7.refs_1_, f32[4,8,1280]{2,1,0:T(8,128)S(1)} %collective-permute-done.8.refs_2_, f32[4,8,1280]{2,1,0:T(8,128)S(1)} %collective-permute-done.9.refs_3_, ...), custom_call_target="tpu_custom_call" | custom-call | tf_op jit(solution)/shard_map/relax/pallas_call | solution.py:561
  (1 shorter events, 0.0 us)
Async XLA Ops:
  2.1 6.7 %collective-permute-start = (f32[16,16,128]{2,1,0:T(8,128)S(1)}, f32[16,16,128]{2,1,0:T(8,128)S(1)}, u32[]{:S(2)}, u32[]{:S(2)}) collective-permute-start(f32[16,16,128]{2,1,0:T(8,128)S(1)} %get-tuple-element.24), channel_id=1, source_target_pairs={{0,4},{4,0},{1,5},{5,1},{2,6},{6,2},{3,7},{7,3},{8,12},{12,8},{9,1... | collective-permute-start | bytes 393224 | tf_op jit(solution)/shard_map/ppermute | solution.py:496
  3.6 7.7 %collective-permute-start.1 = (f32[16,16,128]{2,1,0:T(8,128)S(1)}, f32[16,16,128]{2,1,0:T(8,128)S(1)}, u32[]{:S(2)}, u32[]{:S(2)}) collective-permute-start(f32[16,16,128]{2,1,0:T(8,128)S(1)} %get-tuple-element.25), channel_id=1, source_target_pairs={{4,8},{8,4},{5,9},{9,5},{6,10},{10,6},{7,11},{11,7},{12,16},{16,12... | collective-permute-start | bytes 393224 | tf_op jit(solution)/shard_map/ppermute | solution.py:496
  13.3 4.1 %collective-permute-start.6 = (f32[1,8,1280]{2,1,0:T(8,128)S(1)}, f32[1,8,1280]{2,1,0:T(8,128)S(1)}, u32[]{:S(2)}, u32[]{:S(2)}) collective-permute-start(f32[1,8,1280]{2,1,0:T(8,128)S(1)} %bitcast.2), channel_id=1, source_target_pairs={{0,24},{1,25},{2,26},{3,27},{4,28},{5,29},{6,30},{7,31},{8,16},{9,... | collective-permute-start | bytes 122888 | tf_op jit(solution)/shard_map/ppermute | solution.py:594
  15.0 4.9 %collective-permute-start.5 = (f32[1,8,1280]{2,1,0:T(8,128)S(1)}, f32[1,8,1280]{2,1,0:T(8,128)S(1)}, u32[]{:S(2)}, u32[]{:S(2)}) collective-permute-start(f32[1,8,1280]{2,1,0:T(8,128)S(1)} %bitcast.3), channel_id=1, source_target_pairs={{0,8},{1,9},{2,10},{3,11},{4,12},{5,13},{6,14},{7,15},{8,0},{9,1},... | collective-permute-start | bytes 122888 | tf_op jit(solution)/shard_map/ppermute | solution.py:594
  17.5 4.9 %collective-permute-start.4 = (f32[1,8,1280]{2,1,0:T(8,128)S(1)}, f32[1,8,1280]{2,1,0:T(8,128)S(1)}, u32[]{:S(2)}, u32[]{:S(2)}) collective-permute-start(f32[1,8,1280]{2,1,0:T(8,128)S(1)} %bitcast.4), channel_id=1, source_target_pairs={{0,16},{1,17},{2,18},{3,19},{4,20},{5,21},{6,22},{7,23},{8,24},{9,... | collective-permute-start | bytes 122888 | tf_op jit(solution)/shard_map/ppermute | solution.py:594
  22.4 7.1 %collective-permute-start.9 = (f32[4,8,1280]{2,1,0:T(8,128)S(1)}, f32[4,8,1280]{2,1,0:T(8,128)S(1)}, u32[]{:S(2)}, u32[]{:S(2)}) collective-permute-start(f32[4,8,1280]{2,1,0:T(8,128)S(1)} %pad_maximum_fusion.refs_0_), channel_id=1, source_target_pairs={{0,6},{1,7},{2,4},{3,5},{4,2},{5,3},{6,0},{7,1},{8,14},{9,15},{10,... | collective-permute-start | bytes 491528 | tf_op jit(solution)/shard_map/ppermute | solution.py:594
  22.5 7.1 %collective-permute-start.8 = (f32[4,8,1280]{2,1,0:T(8,128)S(1)}, f32[4,8,1280]{2,1,0:T(8,128)S(1)}, u32[]{:S(2)}, u32[]{:S(2)}) collective-permute-start(f32[4,8,1280]{2,1,0:T(8,128)S(1)} %pad_maximum_fusion.refs_0_), channel_id=1, source_target_pairs={{0,2},{1,3},{2,0},{3,1},{4,6},{5,7},{6,4},{7,5},{8,10},{9,11},{10,... | collective-permute-start | bytes 491528 | tf_op jit(solution)/shard_map/ppermute | solution.py:594
  24.0 7.2 %collective-permute-start.7 = (f32[4,8,1280]{2,1,0:T(8,128)S(1)}, f32[4,8,1280]{2,1,0:T(8,128)S(1)}, u32[]{:S(2)}, u32[]{:S(2)}) collective-permute-start(f32[4,8,1280]{2,1,0:T(8,128)S(1)} %pad_maximum_fusion.refs_0_), channel_id=1, source_target_pairs={{0,4},{1,5},{2,6},{3,7},{4,0},{5,1},{6,2},{7,3},{8,12},{9,13},{10,... | collective-permute-start | bytes 491528 | tf_op jit(solution)/shard_map/ppermute | solution.py:594
  25.9 6.8 %collective-permute-start.2 = (f32[16,16,128]{2,1,0:T(8,128)S(1)}, f32[16,16,128]{2,1,0:T(8,128)S(1)}, u32[]{:S(2)}, u32[]{:S(2)}) collective-permute-start(f32[16,16,128]{2,1,0:T(8,128)S(1)} %get-tuple-element.33), channel_id=1, source_target_pairs={{0,4},{4,0},{1,5},{5,1},{2,6},{6,2},{3,7},{7,3},{8,12},{12,8},{9,1... | collective-permute-start | bytes 393224 | tf_op jit(solution)/shard_map/ppermute | solution.py:496
  26.1 15.6 %collective-permute-start.10 = (f32[4,8,1280]{2,1,0:T(8,128)S(1)}, f32[4,8,1280]{2,1,0:T(8,128)S(1)}, u32[]{:S(2)}, u32[]{:S(2)}) collective-permute-start(f32[4,8,1280]{2,1,0:T(8,128)S(1)} %pad_maximum_fusion.refs_0_), channel_id=1, source_target_pairs={{0,1},{1,0},{2,3},{3,2},{4,5},{5,4},{6,7},{7,6},{8,9},{9,8},{10,11... | collective-permute-start | bytes 491528 | tf_op jit(solution)/shard_map/ppermute | solution.py:594
  29.5 12.1 %collective-permute-start.13 = (f32[4,8,1280]{2,1,0:T(8,128)S(1)}, f32[4,8,1280]{2,1,0:T(8,128)S(1)}, u32[]{:S(2)}, u32[]{:S(2)}) collective-permute-start(f32[4,8,1280]{2,1,0:T(8,128)S(1)} %collective-permute-done.9.refs_3_), channel_id=1, source_target_pairs={{0,1},{1,0},{2,3},{3,2},{4,5},{5,4},{6,7},{7,6},{8,9},{9,8},{10,11... | collective-permute-start | bytes 491528 | tf_op jit(solution)/shard_map/ppermute | solution.py:594
  29.6 12.1 %collective-permute-start.12 = (f32[4,8,1280]{2,1,0:T(8,128)S(1)}, f32[4,8,1280]{2,1,0:T(8,128)S(1)}, u32[]{:S(2)}, u32[]{:S(2)}) collective-permute-start(f32[4,8,1280]{2,1,0:T(8,128)S(1)} %collective-permute-done.8.refs_2_), channel_id=1, source_target_pairs={{0,1},{1,0},{2,3},{3,2},{4,5},{5,4},{6,7},{7,6},{8,9},{9,8},{10,11... | collective-permute-start | bytes 491528 | tf_op jit(solution)/shard_map/ppermute | solution.py:594
  31.3 10.4 %collective-permute-start.11 = (f32[4,8,1280]{2,1,0:T(8,128)S(1)}, f32[4,8,1280]{2,1,0:T(8,128)S(1)}, u32[]{:S(2)}, u32[]{:S(2)}) collective-permute-start(f32[4,8,1280]{2,1,0:T(8,128)S(1)} %collective-permute-done.7.refs_1_), channel_id=1, source_target_pairs={{0,1},{1,0},{2,3},{3,2},{4,5},{5,4},{6,7},{7,6},{8,9},{9,8},{10,11... | collective-permute-start | bytes 491528 | tf_op jit(solution)/shard_map/ppermute | solution.py:594
  32.7 7.7 %collective-permute-start.3 = (f32[16,16,128]{2,1,0:T(8,128)S(1)}, f32[16,16,128]{2,1,0:T(8,128)S(1)}, u32[]{:S(2)}, u32[]{:S(2)}) collective-permute-start(f32[16,16,128]{2,1,0:T(8,128)S(1)} %get-tuple-element.34), channel_id=1, source_target_pairs={{4,8},{8,4},{5,9},{9,5},{6,10},{10,6},{7,11},{11,7},{12,16},{16,12... | collective-permute-start | bytes 393224 | tf_op jit(solution)/shard_map/ppermute | solution.py:496

commit v7 on v6

--- a/solution.py
+++ b/solution.py
@@ -116,11 +116,9 @@
     return (terms0, terms1), jnp.where(alive, updated, record)
 
 
-def three_parts(x):
+def two_parts(x):
     high = x.astype(jnp.bfloat16).astype(F32)
-    x = x - high
-    middle = x.astype(jnp.bfloat16).astype(F32)
-    return high, middle, x - middle
+    return high, x - high
 
 
 def deposit(parts, tile_of, first, onehot, number, acc):
@@ -169,7 +167,7 @@
         at = pl.ds(pl.multiple_of(b * LANES, LANES), LANES)
         terms, new = advance_block(g, record[:, at], shares[:, at], steam, scalar_s[2 * blocks + b])
         next_record[:, at] = new
-        return tuple(zip(*(three_parts(t) for t in terms)))
+        return tuple(zip(*(two_parts(t) for t in terms)))
 
     def hot(offset):
         return jnp.where(spot == offset[0:1], 1.0, 0.0).astype(jnp.bfloat16)

time: 44.3 us -> 44.2 us (level)
  no operation moved by 1% of the time
where the time goes in v7:
time: 44.2 us; the launch traced here: 44.1 us
  waiting for transfers between devices  18.8 us (43%)
  starting transfers between devices  14.4 us (33%)
  Pallas kernels  9.88 us (22%)
  between operations  0.72 us (2%)
    ppermute x10, waiting for transfers between devices, send(): lax.ppermute(part, AXES, [(i, i ^ mask) for i in range(device_count)])  9.67 us
    ppermute x4, waiting for transfers between devices, swap(): return (lax.ppermute(a, AXES, pairs_a), lax.ppermute(b, AXES, pairs_b))  9.11 us
    ppermute x10, starting transfers between devices, send(): lax.ppermute(part, AXES, [(i, i ^ mask) for i in range(device_count)])  8.11 us
    ppermute x4, starting transfers between devices, swap(): return (lax.ppermute(a, AXES, pairs_a), lax.ppermute(b, AXES, pairs_b))  6.3 us
    pallas_call x1, Pallas kernels, body(): pl.pallas_call(interior_kernel, out_shape=(record, all_tiles, all_tiles),...  2.89 us
    pallas_call x1, Pallas kernels, body(): pl.pallas_call(functools.partial(relax_kernel, masks, columns), out_shape...  2.44 us
    pallas_call x1, Pallas kernels, body(): pl.pallas_call(border_kernel, out_shape=(record, all_tiles, plane, plane,...  1.91 us
    pallas_call x1, Pallas kernels, body(): pl.pallas_call(load_kernel, out_shape=tuple((jax.ShapeDtypeStruct(x.shape...  1.43 us
  transfers between devices with their start and end apart: 14, of which 8 were waited for; matrix products, arithmetic and copies ran while one was open for 1% of the time, Pallas kernels for 9%

profile of v7, /device:TPU:8, one launch (start us, length us, event | category | flops | bytes accessed | tf_op | source)
XLA Modules:
  0.0 44.1 jit_solution(11675881365351173581)
XLA Ops:
  0.6 1.4 %load.1 = (f32[16,8,2048]{2,1,0:T(8,128)S(1)}, f32[5,4096]{1,0:T(8,128)S(1)}, f32[12,4096]{1,0:T(8,128)S(1)}, s32[32,128]{1,0:T(8,128)S(1)}, s32[32]{0:T(128)S(1...) custom-call(f32[16,8,2048]{2,1,0:T(8,128)} %gas_in.1, f32[5,4096]{1,0:T(8,128)} %record_in.1, ...), custom_call_target="tpu_custom_call" | custom-call | tf_op jit(solution)/shard_map/load/pallas_call | solution.py:501
  2.1 1.6 %collective-permute-start = (f32[16,16,128]{2,1,0:T(8,128)S(1)}, f32[16,16,128]{2,1,0:T(8,128)S(1)}, u32[]{:S(2)}, u32[]{:S(2)}) collective-permute-start(f32[16,16,128]{2,1,0:T(8,128)S(1)} %get-tuple-element.24), channel_id=1, source_target_pairs={{0,4},{4,0},{1,5},{5,1},{2,6},{6,2},{3,7},{7,3},{8,12},{12,8},{9,1... | collective-permute-start | bytes 393224 | tf_op jit(solution)/shard_map/ppermute | solution.py:494
  3.6 1.9 %collective-permute-start.1 = (f32[16,16,128]{2,1,0:T(8,128)S(1)}, f32[16,16,128]{2,1,0:T(8,128)S(1)}, u32[]{:S(2)}, u32[]{:S(2)}) collective-permute-start(f32[16,16,128]{2,1,0:T(8,128)S(1)} %get-tuple-element.25), channel_id=1, source_target_pairs={{4,8},{8,4},{5,9},{9,5},{6,10},{10,6},{7,11},{11,7},{12,16},{16,12... | collective-permute-start | bytes 393224 | tf_op jit(solution)/shard_map/ppermute | solution.py:494
  5.5 0.2 shift-right-logical_reduce_fusion.1
  5.7 0.1 pad_add_fusion.scalar_v
  5.8 2.9 %interior.1 = (f32[5,4096]{1,0:T(8,128)S(1)}, f32[168,16,128]{2,1,0:T(8,128)S(1)}, f32[168,16,128]{2,1,0:T(8,128)S(1)}) custom-call(s32[96]{0:T(128)S(1)} %pad_add_fusion.scalar_v, f32[16,128]{1,0:T(8,128)S(1)} %get-tuple-element.23.steam_v, s32[32,128]{1,0:T(8,128)S(1)} %get-tuple-element.21.cell_v, f32[16,8,2048]{2,1,0:T(8,128)S(1)} %get-tuple-element.28.gas_state, ...), custom_call_target="tpu_custom_call" | custom-call | tf_op jit(solution)/shard_map/interior/pallas_call | solution.py:518
  8.7 0.0 collective-permute-done.pair_a
  8.7 2.7 %collective-permute-done.1.pair_b = f32[16,16,128]{2,1,0:T(8,128)S(1)} collective-permute-done((f32[16,16,128]{2,1,0:T(8,128)S(1)}, f32[16,16,128]{2,1,0:T(8,128)S(1)}, u32[]{:S(2)}, u32[]{:S(2)}) %collective-permute-start.1) | collective-permute-done | bytes 131104 | tf_op jit(solution)/shard_map/ppermute | solution.py:494
  11.4 1.9 %border.1 = (f32[5,4096]{1,0:T(8,128)S(1)}, f32[168,16,128]{2,1,0:T(8,128)S(1)}, f32[16,16,128]{2,1,0:T(8,128)S(1)}, f32[16,16,128]{2,1,0:T(8,128)S(1)}, f32[8,1280]{1,0:T(8,128)S(1)}) custom-call(s32[96]{0:T(128)S(1)} %pad_add_fusion.scalar_v, f32[16,128]{1,0:T(8,128)S(1)} %get-tuple-element.23.steam_v, s32[32,128]{1,0:T(8,128)S(1)} %get-tuple-element.21.cell_v, ...), custom_call_target="tpu_custom_call" | custom-call | tf_op jit(solution)/shard_map/border/pallas_call | solution.py:526
  13.3 1.6 %collective-permute-start.6 = (f32[1,8,1280]{2,1,0:T(8,128)S(1)}, f32[1,8,1280]{2,1,0:T(8,128)S(1)}, u32[]{:S(2)}, u32[]{:S(2)}) collective-permute-start(f32[1,8,1280]{2,1,0:T(8,128)S(1)} %bitcast.2), channel_id=1, source_target_pairs={{0,24},{1,25},{2,26},{3,27},{4,28},{5,29},{6,30},{7,31},{8,16},{9,... | collective-permute-start | bytes 122888 | tf_op jit(solution)/shard_map/ppermute | solution.py:592
  14.9 2.5 %collective-permute-start.5 = (f32[1,8,1280]{2,1,0:T(8,128)S(1)}, f32[1,8,1280]{2,1,0:T(8,128)S(1)}, u32[]{:S(2)}, u32[]{:S(2)}) collective-permute-start(f32[1,8,1280]{2,1,0:T(8,128)S(1)} %bitcast.3), channel_id=1, source_target_pairs={{0,8},{1,9},{2,10},{3,11},{4,12},{5,13},{6,14},{7,15},{8,0},{9,1},... | collective-permute-start | bytes 122888 | tf_op jit(solution)/shard_map/ppermute | solution.py:592
  17.4 0.0 collective-permute-start.4
  17.4 0.0 collective-permute-done.6
  17.4 2.4 %collective-permute-done.5 = f32[1,8,1280]{2,1,0:T(8,128)S(1)} collective-permute-done((f32[1,8,1280]{2,1,0:T(8,128)S(1)}, f32[1,8,1280]{2,1,0:T(8,128)S(1)}, u32[]{:S(2)}, u32[]{:S(2)}) %collective-permute-start.5) | collective-permute-done | bytes 40992 | tf_op jit(solution)/shard_map/ppermute | solution.py:592
  19.8 2.5 %collective-permute-done.4 = f32[1,8,1280]{2,1,0:T(8,128)S(1)} collective-permute-done((f32[1,8,1280]{2,1,0:T(8,128)S(1)}, f32[1,8,1280]{2,1,0:T(8,128)S(1)}, u32[]{:S(2)}, u32[]{:S(2)}) %collective-permute-start.4) | collective-permute-done | bytes 40992 | tf_op jit(solution)/shard_map/ppermute | solution.py:592
  22.3 0.1 collective-permute-start.9
  22.4 1.6 %collective-permute-start.8 = (f32[4,8,1280]{2,1,0:T(8,128)S(1)}, f32[4,8,1280]{2,1,0:T(8,128)S(1)}, u32[]{:S(2)}, u32[]{:S(2)}) collective-permute-start(f32[4,8,1280]{2,1,0:T(8,128)S(1)} %pad_maximum_fusion.refs_0_), channel_id=1, source_target_pairs={{0,2},{1,3},{2,0},{3,1},{4,6},{5,7},{6,4},{7,5},{8,10},{9,11},{10,... | collective-permute-start | bytes 491528 | tf_op jit(solution)/shard_map/ppermute | solution.py:592
  24.0 1.9 %collective-permute-start.7 = (f32[4,8,1280]{2,1,0:T(8,128)S(1)}, f32[4,8,1280]{2,1,0:T(8,128)S(1)}, u32[]{:S(2)}, u32[]{:S(2)}) collective-permute-start(f32[4,8,1280]{2,1,0:T(8,128)S(1)} %pad_maximum_fusion.refs_0_), channel_id=1, source_target_pairs={{0,4},{1,5},{2,6},{3,7},{4,0},{5,1},{6,2},{7,3},{8,12},{9,13},{10,... | collective-permute-start | bytes 491528 | tf_op jit(solution)/shard_map/ppermute | solution.py:592
  25.9 0.1 collective-permute-start.2
  26.0 0.0 collective-permute-start.10
  26.0 3.5 %collective-permute-done.9.refs_3_ = f32[4,8,1280]{2,1,0:T(8,128)S(1)} collective-permute-done((f32[4,8,1280]{2,1,0:T(8,128)S(1)}, f32[4,8,1280]{2,1,0:T(8,128)S(1)}, u32[]{:S(2)}, u32[]{:S(2)}) %collective-permute-start.9) | collective-permute-done | bytes 163872 | tf_op jit(solution)/shard_map/ppermute | solution.py:592
  29.5 0.0 collective-permute-start.13
  29.5 0.1 collective-permute-done.8.refs_2_
  29.5 0.4 %collective-permute-start.12 = (f32[4,8,1280]{2,1,0:T(8,128)S(1)}, f32[4,8,1280]{2,1,0:T(8,128)S(1)}, u32[]{:S(2)}, u32[]{:S(2)}) collective-permute-start(f32[4,8,1280]{2,1,0:T(8,128)S(1)} %collective-permute-done.8.refs_2_), channel_id=1, source_target_pairs={{0,1},{1,0},{2,3},{3,2},{4,5},{5,4},{6,7},{7,6},{8,9},{9,8},{10,11... | collective-permute-start | bytes 491528 | tf_op jit(solution)/shard_map/ppermute | solution.py:592
  30.0 1.2 %collective-permute-done.7.refs_1_ = f32[4,8,1280]{2,1,0:T(8,128)S(1)} collective-permute-done((f32[4,8,1280]{2,1,0:T(8,128)S(1)}, f32[4,8,1280]{2,1,0:T(8,128)S(1)}, u32[]{:S(2)}, u32[]{:S(2)}) %collective-permute-start.7) | collective-permute-done | bytes 163872 | tf_op jit(solution)/shard_map/ppermute | solution.py:592
  31.2 0.0 collective-permute-start.11
  31.2 1.4 %collective-permute-done.2.pair_a = f32[16,16,128]{2,1,0:T(8,128)S(1)} collective-permute-done((f32[16,16,128]{2,1,0:T(8,128)S(1)}, f32[16,16,128]{2,1,0:T(8,128)S(1)}, u32[]{:S(2)}, u32[]{:S(2)}) %collective-permute-start.2) | collective-permute-done | bytes 131104 | tf_op jit(solution)/shard_map/ppermute | solution.py:494
  32.6 2.7 %collective-permute-start.3 = (f32[16,16,128]{2,1,0:T(8,128)S(1)}, f32[16,16,128]{2,1,0:T(8,128)S(1)}, u32[]{:S(2)}, u32[]{:S(2)}) collective-permute-start(f32[16,16,128]{2,1,0:T(8,128)S(1)} %get-tuple-element.34), channel_id=1, source_target_pairs={{4,8},{8,4},{5,9},{9,5},{6,10},{10,6},{7,11},{11,7},{12,16},{16,12... | collective-permute-start | bytes 393224 | tf_op jit(solution)/shard_map/ppermute | solution.py:494
  35.3 5.0 %collective-permute-done.3.pair_b = f32[16,16,128]{2,1,0:T(8,128)S(1)} collective-permute-done((f32[16,16,128]{2,1,0:T(8,128)S(1)}, f32[16,16,128]{2,1,0:T(8,128)S(1)}, u32[]{:S(2)}, u32[]{:S(2)}) %collective-permute-start.3) | collective-permute-done | bytes 131104 | tf_op jit(solution)/shard_map/ppermute | solution.py:494
  40.4 1.2 %merge.1 = (f32[16,8,2048]{2,1,0:T(8,128)}, f32[5,4096]{1,0:T(8,128)}) custom-call(f32[168,16,128]{2,1,0:T(8,128)S(1)} %get-tuple-element.32.acc, f32[16,16,128]{2,1,0:T(8,128)S(1)} %collective-permute-done.2.pair_a, f32[16,16,128]{2,1,0:T(8,128)S(1)} %collective-permute-done.3.pair_b, f32[5,4096]{1,0:T(8,128)S(1)} %get-tuple-element.35.record_in), custom_call_target="tpu_custom_call" | custom-call | tf_op jit(solution)/shard_map/merge/pallas_call | solution.py:545
  41.6 0.0 collective-permute-done.10.refs_4_
  41.6 0.0 collective-permute-done.13.refs_7_
  41.6 0.0 collective-permute-done.12.refs_6_
  41.6 0.0 collective-permute-done.11.refs_5_
  41.6 2.4 %relax.1 = f32[64,4096]{1,0:T(8,128)} custom-call(f32[4,8,1280]{2,1,0:T(8,128)S(1)} %pad_maximum_fusion.refs_0_, f32[4,8,1280]{2,1,0:T(8,128)S(1)} %collective-permute-done.7.refs_1_, f32[4,8,1280]{2,1,0:T(8,128)S(1)} %collective-permute-done.8.refs_2_, f32[4,8,1280]{2,1,0:T(8,128)S(1)} %collective-permute-done.9.refs_3_, ...), custom_call_target="tpu_custom_call" | custom-call | tf_op jit(solution)/shard_map/relax/pallas_call | solution.py:559
  (1 shorter events, 0.0 us)
Async XLA Ops:
  2.1 6.6 %collective-permute-start = (f32[16,16,128]{2,1,0:T(8,128)S(1)}, f32[16,16,128]{2,1,0:T(8,128)S(1)}, u32[]{:S(2)}, u32[]{:S(2)}) collective-permute-start(f32[16,16,128]{2,1,0:T(8,128)S(1)} %get-tuple-element.24), channel_id=1, source_target_pairs={{0,4},{4,0},{1,5},{5,1},{2,6},{6,2},{3,7},{7,3},{8,12},{12,8},{9,1... | collective-permute-start | bytes 393224 | tf_op jit(solution)/shard_map/ppermute | solution.py:494
  3.6 7.7 %collective-permute-start.1 = (f32[16,16,128]{2,1,0:T(8,128)S(1)}, f32[16,16,128]{2,1,0:T(8,128)S(1)}, u32[]{:S(2)}, u32[]{:S(2)}) collective-permute-start(f32[16,16,128]{2,1,0:T(8,128)S(1)} %get-tuple-element.25), channel_id=1, source_target_pairs={{4,8},{8,4},{5,9},{9,5},{6,10},{10,6},{7,11},{11,7},{12,16},{16,12... | collective-permute-start | bytes 393224 | tf_op jit(solution)/shard_map/ppermute | solution.py:494
  13.3 4.1 %collective-permute-start.6 = (f32[1,8,1280]{2,1,0:T(8,128)S(1)}, f32[1,8,1280]{2,1,0:T(8,128)S(1)}, u32[]{:S(2)}, u32[]{:S(2)}) collective-permute-start(f32[1,8,1280]{2,1,0:T(8,128)S(1)} %bitcast.2), channel_id=1, source_target_pairs={{0,24},{1,25},{2,26},{3,27},{4,28},{5,29},{6,30},{7,31},{8,16},{9,... | collective-permute-start | bytes 122888 | tf_op jit(solution)/shard_map/ppermute | solution.py:592
  14.9 4.9 %collective-permute-start.5 = (f32[1,8,1280]{2,1,0:T(8,128)S(1)}, f32[1,8,1280]{2,1,0:T(8,128)S(1)}, u32[]{:S(2)}, u32[]{:S(2)}) collective-permute-start(f32[1,8,1280]{2,1,0:T(8,128)S(1)} %bitcast.3), channel_id=1, source_target_pairs={{0,8},{1,9},{2,10},{3,11},{4,12},{5,13},{6,14},{7,15},{8,0},{9,1},... | collective-permute-start | bytes 122888 | tf_op jit(solution)/shard_map/ppermute | solution.py:592
  17.4 4.9 %collective-permute-start.4 = (f32[1,8,1280]{2,1,0:T(8,128)S(1)}, f32[1,8,1280]{2,1,0:T(8,128)S(1)}, u32[]{:S(2)}, u32[]{:S(2)}) collective-permute-start(f32[1,8,1280]{2,1,0:T(8,128)S(1)} %bitcast.4), channel_id=1, source_target_pairs={{0,16},{1,17},{2,18},{3,19},{4,20},{5,21},{6,22},{7,23},{8,24},{9,... | collective-permute-start | bytes 122888 | tf_op jit(solution)/shard_map/ppermute | solution.py:592
  22.3 7.1 %collective-permute-start.9 = (f32[4,8,1280]{2,1,0:T(8,128)S(1)}, f32[4,8,1280]{2,1,0:T(8,128)S(1)}, u32[]{:S(2)}, u32[]{:S(2)}) collective-permute-start(f32[4,8,1280]{2,1,0:T(8,128)S(1)} %pad_maximum_fusion.refs_0_), channel_id=1, source_target_pairs={{0,6},{1,7},{2,4},{3,5},{4,2},{5,3},{6,0},{7,1},{8,14},{9,15},{10,... | collective-permute-start | bytes 491528 | tf_op jit(solution)/shard_map/ppermute | solution.py:592
  22.4 7.1 %collective-permute-start.8 = (f32[4,8,1280]{2,1,0:T(8,128)S(1)}, f32[4,8,1280]{2,1,0:T(8,128)S(1)}, u32[]{:S(2)}, u32[]{:S(2)}) collective-permute-start(f32[4,8,1280]{2,1,0:T(8,128)S(1)} %pad_maximum_fusion.refs_0_), channel_id=1, source_target_pairs={{0,2},{1,3},{2,0},{3,1},{4,6},{5,7},{6,4},{7,5},{8,10},{9,11},{10,... | collective-permute-start | bytes 491528 | tf_op jit(solution)/shard_map/ppermute | solution.py:592
  24.0 7.2 %collective-permute-start.7 = (f32[4,8,1280]{2,1,0:T(8,128)S(1)}, f32[4,8,1280]{2,1,0:T(8,128)S(1)}, u32[]{:S(2)}, u32[]{:S(2)}) collective-permute-start(f32[4,8,1280]{2,1,0:T(8,128)S(1)} %pad_maximum_fusion.refs_0_), channel_id=1, source_target_pairs={{0,4},{1,5},{2,6},{3,7},{4,0},{5,1},{6,2},{7,3},{8,12},{9,13},{10,... | collective-permute-start | bytes 491528 | tf_op jit(solution)/shard_map/ppermute | solution.py:592
  25.9 6.8 %collective-permute-start.2 = (f32[16,16,128]{2,1,0:T(8,128)S(1)}, f32[16,16,128]{2,1,0:T(8,128)S(1)}, u32[]{:S(2)}, u32[]{:S(2)}) collective-permute-start(f32[16,16,128]{2,1,0:T(8,128)S(1)} %get-tuple-element.33), channel_id=1, source_target_pairs={{0,4},{4,0},{1,5},{5,1},{2,6},{6,2},{3,7},{7,3},{8,12},{12,8},{9,1... | collective-permute-start | bytes 393224 | tf_op jit(solution)/shard_map/ppermute | solution.py:494
  26.0 15.6 %collective-permute-start.10 = (f32[4,8,1280]{2,1,0:T(8,128)S(1)}, f32[4,8,1280]{2,1,0:T(8,128)S(1)}, u32[]{:S(2)}, u32[]{:S(2)}) collective-permute-start(f32[4,8,1280]{2,1,0:T(8,128)S(1)} %pad_maximum_fusion.refs_0_), channel_id=1, source_target_pairs={{0,1},{1,0},{2,3},{3,2},{4,5},{5,4},{6,7},{7,6},{8,9},{9,8},{10,11... | collective-permute-start | bytes 491528 | tf_op jit(solution)/shard_map/ppermute | solution.py:592
  29.5 12.1 %collective-permute-start.13 = (f32[4,8,1280]{2,1,0:T(8,128)S(1)}, f32[4,8,1280]{2,1,0:T(8,128)S(1)}, u32[]{:S(2)}, u32[]{:S(2)}) collective-permute-start(f32[4,8,1280]{2,1,0:T(8,128)S(1)} %collective-permute-done.9.refs_3_), channel_id=1, source_target_pairs={{0,1},{1,0},{2,3},{3,2},{4,5},{5,4},{6,7},{7,6},{8,9},{9,8},{10,11... | collective-permute-start | bytes 491528 | tf_op jit(solution)/shard_map/ppermute | solution.py:592
  29.5 12.1 %collective-permute-start.12 = (f32[4,8,1280]{2,1,0:T(8,128)S(1)}, f32[4,8,1280]{2,1,0:T(8,128)S(1)}, u32[]{:S(2)}, u32[]{:S(2)}) collective-permute-start(f32[4,8,1280]{2,1,0:T(8,128)S(1)} %collective-permute-done.8.refs_2_), channel_id=1, source_target_pairs={{0,1},{1,0},{2,3},{3,2},{4,5},{5,4},{6,7},{7,6},{8,9},{9,8},{10,11... | collective-permute-start | bytes 491528 | tf_op jit(solution)/shard_map/ppermute | solution.py:592
  31.2 10.4 %collective-permute-start.11 = (f32[4,8,1280]{2,1,0:T(8,128)S(1)}, f32[4,8,1280]{2,1,0:T(8,128)S(1)}, u32[]{:S(2)}, u32[]{:S(2)}) collective-permute-start(f32[4,8,1280]{2,1,0:T(8,128)S(1)} %collective-permute-done.7.refs_1_), channel_id=1, source_target_pairs={{0,1},{1,0},{2,3},{3,2},{4,5},{5,4},{6,7},{7,6},{8,9},{9,8},{10,11... | collective-permute-start | bytes 491528 | tf_op jit(solution)/shard_map/ppermute | solution.py:592
  32.6 7.7 %collective-permute-start.3 = (f32[16,16,128]{2,1,0:T(8,128)S(1)}, f32[16,16,128]{2,1,0:T(8,128)S(1)}, u32[]{:S(2)}, u32[]{:S(2)}) collective-permute-start(f32[16,16,128]{2,1,0:T(8,128)S(1)} %get-tuple-element.34), channel_id=1, source_target_pairs={{4,8},{8,4},{5,9},{9,5},{6,10},{10,6},{7,11},{11,7},{12,16},{16,12... | collective-permute-start | bytes 393224 | tf_op jit(solution)/shard_map/ppermute | solution.py:494
